TPU v7x, 32 devices: a whole 2x2x4 slice. The times are simulated.
32 devices in a mesh: dp: 8 (over y, x, core), shard: 4 (over z).
Axes of the slice: x: 2, y: 2, z: 4, core: 2. Of those that a mesh axis runs over, the one named last changes fastest.
Arguments:
- hidden_in: bfloat16 [16384, 960], P(('dp', 'shard')), may hold values from -6 to 6
- out_grad: bfloat16 [16384, 960], P(('dp', 'shard')), may hold values from -6 to 6
- seg_ids: int32 [8, 2048], P('dp'), may hold values from 0 to 11, as said below
- doc_start: int32 [16384], P(('dp', 'shard')), may hold values from 0 to 2047, as said below
- norm_gains: float32 [2, 960], replicated, may hold values from 0.5 to 1.5
- heads_weight: float32 [960, 1600], P('shard', 'dp'), may hold values from -0.1875 to 0.1875
- output_weight: float32 [960, 960], P('shard', 'dp'), may hold values from -1 to 1
- expand_weight: float32 [960, 5120], P('shard', 'dp'), may hold values from -0.1875 to 0.1875
- down_weight: float32 [2560, 960], P('shard', 'dp'), may hold values from -0.125 to 0.125
- gains_first: float32 [2, 960], replicated, may hold values from -80 to 80
- gains_second: float32 [2, 960], replicated, may hold values from 983.04 to 3932.16
- heads_first: float32 [960, 1600], P('shard', 'dp'), may hold values from -56 to 56
- heads_second: float32 [960, 1600], P('shard', 'dp'), may hold values from 819.2 to 3276.8
- output_first: float32 [960, 960], P('shard', 'dp'), may hold values from -12 to 12
- output_second: float32 [960, 960], P('shard', 'dp'), may hold values from 32.768 to 131.072
- expand_first: float32 [960, 5120], P('shard', 'dp'), may hold values from -40 to 40
- expand_second: float32 [960, 5120], P('shard', 'dp'), may hold values from 98.304 to 393.216
- down_first: float32 [2560, 960], P('shard', 'dp'), may hold values from -64 to 64
- down_second: float32 [2560, 960], P('shard', 'dp'), may hold values from 147.456 to 589.824
Outputs:
- hidden_out: bfloat16 [16384, 960], P(('dp', 'shard'))
- input_grad: float32 [16384, 960], P(('dp', 'shard'))
- gains_grad: float32 [2, 960], replicated
- heads_grad: float32 [960, 1600], P('shard', 'dp')
- output_grad: float32 [960, 960], P('shard', 'dp')
- expand_grad: float32 [960, 5120], P('shard', 'dp')
- down_grad: float32 [2560, 960], P('shard', 'dp')
- gains_new: float32 [2, 960], replicated
- heads_new: float32 [960, 1600], P('shard', 'dp')
- output_new: float32 [960, 960], P('shard', 'dp')
- expand_new: float32 [960, 5120], P('shard', 'dp')
- down_new: float32 [2560, 960], P('shard', 'dp')
- gains_first_new: float32 [2, 960], replicated
- gains_second_new: float32 [2, 960], replicated
- heads_first_new: float32 [960, 1600], P('shard', 'dp')
- heads_second_new: float32 [960, 1600], P('shard', 'dp')
- output_first_new: float32 [960, 960], P('shard', 'dp')
- output_second_new: float32 [960, 960], P('shard', 'dp')
- expand_first_new: float32 [960, 5120], P('shard', 'dp')
- expand_second_new: float32 [960, 5120], P('shard', 'dp')
- down_first_new: float32 [2560, 960], P('shard', 'dp')
- down_second_new: float32 [2560, 960], P('shard', 'dp')
Inputs may be any that keep to these rules, and one draw needn't show every extreme that they name: `seg_ids`: each row is one sequence; ids are 0 at its first token and rise by one at each document's first token. Every document has at most 2000 tokens, and every one but the first and last of its sequence at least 204. Some sequence holds a document of exactly 2000 tokens, and some sequence reaches the largest id. `doc_start`: agrees with seg_ids: for each token, the position within its sequence of the first token with the same id.
All inputs are finite; a program needn't handle non-finite values.
Results may differ from a plain program's by a relative error of at most 0.014.
Values may be sent and summed in bfloat16 or wider, within the bound.
A program may use at most 256 MiB of HBM per device.

v0:
```python
import jax
import jax.numpy as jnp
from jax import lax
from jax.sharding import PartitionSpec as P

QUERY_HEADS = 15
KEY_VALUE_HEADS = 5
HEAD_SIZE = 64
FF = 2560
ADAM_STEP = 10


norm_epsilon = 1e-05
beta_one = 0.9
beta_two = 0.95
adam_epsilon = 1e-08
matrix_rate = 0.03
output_rate = 0.15
gain_rate = 0.5
decay_rate = 0.1


def rotary_tables(relative):
    half_width = HEAD_SIZE // 2
    freq_table = jnp.power(10000.0, -jnp.arange(half_width).astype(jnp.float32) / half_width)
    angle_table = relative.astype(jnp.float32)[:, None] * freq_table[None, :]
    return (jnp.cos(angle_table), jnp.sin(angle_table))


def apply_rotary(values, cosine_table, sine_table):
    half_width = HEAD_SIZE // 2
    first_half = values[..., :half_width]
    second_half = values[..., half_width:]
    cos_part = cosine_table[:, None, :]
    sin_part = sine_table[:, None, :]
    return jnp.concatenate(
        [
            first_half * cos_part - second_half * sin_part,
            second_half * cos_part + first_half * sin_part,
        ],
        axis=-1,
    )


def reverse_rotary(values, cosine_table, sine_table):
    half_width = HEAD_SIZE // 2
    first_half = values[..., :half_width]
    second_half = values[..., half_width:]
    cos_part = cosine_table[:, None, :]
    sin_part = sine_table[:, None, :]
    return jnp.concatenate(
        [
            first_half * cos_part + second_half * sin_part,
            second_half * cos_part - first_half * sin_part,
        ],
        axis=-1,
    )


def rms_forward(values, gain):
    inverse = lax.rsqrt(jnp.mean(values * values, axis=-1, keepdims=True) + norm_epsilon)
    normed = values * inverse
    return (normed, inverse, (normed * gain).astype(jnp.bfloat16))


def rms_backward(upstream, normed, inverse, gain):
    scaled = upstream * gain
    gain_term = jnp.sum(upstream * normed, axis=0)
    back = inverse * (scaled - normed * jnp.mean(scaled * normed, axis=-1, keepdims=True))
    return (back, gain_term)


def times_transposed(left, right):
    return lax.dot_general(
        left, right, (((1,), (1,)), ((), ())), preferred_element_type=jnp.float32
    )


def transposed_times(left, right):
    return lax.dot_general(
        left, right, (((0,), (0,)), ((), ())), preferred_element_type=jnp.float32
    )


def adamw(weight, grad, first, second, rate, decay):
    first_new = beta_one * first + (1.0 - beta_one) * grad
    second_new = beta_two * second + (1.0 - beta_two) * grad * grad
    first_hat = first_new / (1.0 - beta_one**ADAM_STEP)
    second_hat = second_new / (1.0 - beta_two**ADAM_STEP)
    weight_new = weight - rate * (
        first_hat / (jnp.sqrt(second_hat) + adam_epsilon) + decay * weight
    )
    return (weight_new, first_new, second_new)


def attend_forward(queries, all_keys, allowed):
    group_width = QUERY_HEADS // KEY_VALUE_HEADS
    key_total_width = KEY_VALUE_HEADS * HEAD_SIZE
    outputs = []
    logsums = []
    for group_of_head in range(KEY_VALUE_HEADS):
        query_group = queries[:, group_of_head * group_width : (group_of_head + 1) * group_width, :]
        key_group = all_keys[:, group_of_head * HEAD_SIZE : (group_of_head + 1) * HEAD_SIZE]
        value_group = all_keys[
            :,
            key_total_width
            + group_of_head * HEAD_SIZE : key_total_width
            + (group_of_head + 1) * HEAD_SIZE,
        ]
        scores = jnp.einsum(
            "qhd,kd->hqk", query_group, key_group, preferred_element_type=jnp.float32
        ) * HEAD_SIZE ** (-0.5)
        exponent = jnp.where(allowed[None], jnp.exp(scores), 0.0)
        totals = jnp.sum(exponent, axis=-1)
        probs = (exponent / totals[..., None]).astype(jnp.bfloat16)
        outputs.append(
            jnp.einsum("hqk,kd->qhd", probs, value_group, preferred_element_type=jnp.float32)
        )
        logsums.append(jnp.log(totals))
    return (jnp.concatenate(outputs, axis=1), jnp.concatenate(logsums, axis=0))


def attend_backward(queries, all_keys, allowed, logsums, attended, attended_grad):
    group_width = QUERY_HEADS // KEY_VALUE_HEADS
    key_total_width = KEY_VALUE_HEADS * HEAD_SIZE
    row_delta = jnp.sum(attended_grad.astype(jnp.float32) * attended.astype(jnp.float32), axis=-1)
    query_grads = []
    key_grads = []
    value_grads = []
    for group_of_head in range(KEY_VALUE_HEADS):
        lower_head = group_of_head * group_width
        upper_head = lower_head + group_width
        query_group = queries[:, lower_head:upper_head, :]
        grad_group = attended_grad[:, lower_head:upper_head, :]
        key_group = all_keys[:, group_of_head * HEAD_SIZE : (group_of_head + 1) * HEAD_SIZE]
        value_group = all_keys[
            :,
            key_total_width
            + group_of_head * HEAD_SIZE : key_total_width
            + (group_of_head + 1) * HEAD_SIZE,
        ]
        scores = jnp.einsum(
            "qhd,kd->hqk", query_group, key_group, preferred_element_type=jnp.float32
        ) * HEAD_SIZE ** (-0.5)
        probs = jnp.where(
            allowed[None], jnp.exp(scores - logsums[lower_head:upper_head][..., None]), 0.0
        )
        probs_half = probs.astype(jnp.bfloat16)
        prob_grad = jnp.einsum(
            "qhd,kd->hqk", grad_group, value_group, preferred_element_type=jnp.float32
        )
        score_grad = (
            probs
            * (prob_grad - jnp.transpose(row_delta[:, lower_head:upper_head])[..., None])
            * HEAD_SIZE ** (-0.5)
        ).astype(jnp.bfloat16)
        query_grads.append(
            jnp.einsum("hqk,kd->qhd", score_grad, key_group, preferred_element_type=jnp.float32)
        )
        key_grads.append(
            jnp.einsum("hqk,qhd->kd", score_grad, query_group, preferred_element_type=jnp.float32)
        )
        value_grads.append(
            jnp.einsum("hqk,qhd->kd", probs_half, grad_group, preferred_element_type=jnp.float32)
        )
    return (jnp.concatenate(query_grads, axis=1), jnp.concatenate(key_grads + value_grads, axis=1))


def local(
    hidden_in,
    out_grad,
    seg_ids,
    doc_start,
    norm_gains,
    heads_weight,
    output_weight,
    expand_weight,
    down_weight,
    gains_first,
    gains_second,
    heads_first,
    heads_second,
    output_first,
    output_second,
    expand_first,
    expand_second,
    down_first,
    down_second,
):
    count_of_rows = hidden_in.shape[0]
    query_total_width = QUERY_HEADS * HEAD_SIZE
    key_total_width = KEY_VALUE_HEADS * HEAD_SIZE
    sectioned = (
        lax.all_gather(heads_weight.astype(jnp.bfloat16), "dp", axis=1, tiled=True),
        lax.all_gather(output_weight.astype(jnp.bfloat16), "dp", axis=1, tiled=True),
        lax.all_gather(expand_weight.astype(jnp.bfloat16), "dp", axis=1, tiled=True),
        lax.all_gather(down_weight.astype(jnp.bfloat16), "dp", axis=1, tiled=True),
    )
    heads_half, output_half, expand_half, down_half = (
        lax.all_gather(sectioned[0], "shard", axis=0, tiled=True),
        lax.all_gather(sectioned[1], "shard", axis=0, tiled=True),
        lax.all_gather(sectioned[2], "shard", axis=0, tiled=True),
        lax.all_gather(sectioned[3], "shard", axis=0, tiled=True),
    )
    first_row = lax.axis_index("shard") * count_of_rows
    positions = first_row + jnp.arange(count_of_rows, dtype=jnp.int32)
    cosine_table, sine_table = rotary_tables(positions - doc_start)
    seg_row = seg_ids[0]
    seg_query = lax.dynamic_slice_in_dim(seg_row, first_row, count_of_rows)
    key_places = jnp.arange(seg_row.shape[0], dtype=jnp.int32)
    allowed = (seg_query[:, None] == seg_row[None, :]) & (key_places[None, :] <= positions[:, None])
    gain_one = norm_gains[0]
    gain_two = norm_gains[1]
    inputs = hidden_in.astype(jnp.float32)
    normed_one, inverse_one, hidden_one = rms_forward(inputs, gain_one)
    projected_rows = jnp.dot(hidden_one, heads_half, preferred_element_type=jnp.float32)
    queries = apply_rotary(
        projected_rows[:, :query_total_width].reshape(count_of_rows, QUERY_HEADS, HEAD_SIZE),
        cosine_table,
        sine_table,
    ).astype(jnp.bfloat16)
    key_rotated = apply_rotary(
        projected_rows[:, query_total_width : query_total_width + key_total_width].reshape(
            count_of_rows, KEY_VALUE_HEADS, HEAD_SIZE
        ),
        cosine_table,
        sine_table,
    ).astype(jnp.bfloat16)
    values = projected_rows[:, query_total_width + key_total_width :].astype(jnp.bfloat16)
    packed = jnp.concatenate([key_rotated.reshape(count_of_rows, key_total_width), values], axis=1)
    all_keys = lax.all_gather(packed, "shard", axis=0, tiled=True)
    attended, logsums = attend_forward(queries, all_keys, allowed)
    attended_half = attended.astype(jnp.bfloat16)
    attended_flat = attended_half.reshape(count_of_rows, query_total_width)
    residual = inputs + jnp.dot(attended_flat, output_half, preferred_element_type=jnp.float32)
    normed_two, inverse_two, hidden_two = rms_forward(residual, gain_two)
    gate_up = jnp.dot(hidden_two, expand_half, preferred_element_type=jnp.float32)
    gate_part = gate_up[:, :FF]
    up_part = gate_up[:, FF:]
    sigmoid_gate = jax.nn.sigmoid(gate_part)
    silu_gate = gate_part * sigmoid_gate
    mixed_act = (silu_gate * up_part).astype(jnp.bfloat16)
    hidden_out = (
        residual + jnp.dot(mixed_act, down_half, preferred_element_type=jnp.float32)
    ).astype(jnp.bfloat16)
    upstream = out_grad.astype(jnp.float32)
    mixed_grad = times_transposed(out_grad, down_half)
    down_term = transposed_times(mixed_act, out_grad)
    gate_grad = mixed_grad * up_part * sigmoid_gate * (1.0 + gate_part * (1.0 - sigmoid_gate))
    up_grad = mixed_grad * silu_gate
    expand_delta = jnp.concatenate([gate_grad, up_grad], axis=1).astype(jnp.bfloat16)
    expand_term = transposed_times(hidden_two, expand_delta)
    hidden_two_grad = times_transposed(expand_delta, expand_half)
    residual_back, gain_two_term = rms_backward(hidden_two_grad, normed_two, inverse_two, gain_two)
    residual_grad = upstream + residual_back
    residual_delta = residual_grad.astype(jnp.bfloat16)
    output_term = transposed_times(attended_flat, residual_delta)
    attended_grad = (
        times_transposed(residual_delta, output_half)
        .astype(jnp.bfloat16)
        .reshape(count_of_rows, QUERY_HEADS, HEAD_SIZE)
    )
    query_grad, packed_terms = attend_backward(
        queries, all_keys, allowed, logsums, attended_half, attended_grad
    )
    packed_gradient = lax.psum_scatter(packed_terms, "shard", scatter_dimension=0, tiled=True)
    key_backward = reverse_rotary(
        packed_gradient[:, :key_total_width].reshape(count_of_rows, KEY_VALUE_HEADS, HEAD_SIZE),
        cosine_table,
        sine_table,
    ).reshape(count_of_rows, key_total_width)
    query_back = reverse_rotary(query_grad, cosine_table, sine_table).reshape(
        count_of_rows, query_total_width
    )
    heads_delta = jnp.concatenate(
        [query_back, key_backward, packed_gradient[:, key_total_width:]], axis=1
    ).astype(jnp.bfloat16)
    heads_term = transposed_times(hidden_one, heads_delta)
    hidden_one_grad = times_transposed(heads_delta, heads_half)
    input_back, gain_one_term = rms_backward(hidden_one_grad, normed_one, inverse_one, gain_one)
    input_grad = residual_grad + input_back
    gains_grad = lax.psum(jnp.stack([gain_one_term, gain_two_term], axis=0), ("dp", "shard"))
    reduced = (
        lax.psum_scatter(heads_term, "dp", scatter_dimension=1, tiled=True),
        lax.psum_scatter(output_term, "dp", scatter_dimension=1, tiled=True),
        lax.psum_scatter(expand_term, "dp", scatter_dimension=1, tiled=True),
        lax.psum_scatter(down_term, "dp", scatter_dimension=1, tiled=True),
    )
    heads_grad, output_grad, expand_grad, down_grad = (
        lax.psum_scatter(reduced[0], "shard", scatter_dimension=0, tiled=True),
        lax.psum_scatter(reduced[1], "shard", scatter_dimension=0, tiled=True),
        lax.psum_scatter(reduced[2], "shard", scatter_dimension=0, tiled=True),
        lax.psum_scatter(reduced[3], "shard", scatter_dimension=0, tiled=True),
    )
    gains_new, gains_first_new, gains_second_new = adamw(
        norm_gains, gains_grad, gains_first, gains_second, gain_rate, 0.0
    )
    heads_new, heads_first_new, heads_second_new = adamw(
        heads_weight, heads_grad, heads_first, heads_second, matrix_rate, decay_rate
    )
    output_new, output_first_new, output_second_new = adamw(
        output_weight, output_grad, output_first, output_second, output_rate, decay_rate
    )
    expand_new, expand_first_new, expand_second_new = adamw(
        expand_weight, expand_grad, expand_first, expand_second, matrix_rate, decay_rate
    )
    down_new, down_first_new, down_second_new = adamw(
        down_weight, down_grad, down_first, down_second, matrix_rate, decay_rate
    )
    return (
        hidden_out,
        input_grad,
        gains_grad,
        heads_grad,
        output_grad,
        expand_grad,
        down_grad,
        gains_new,
        heads_new,
        output_new,
        expand_new,
        down_new,
        gains_first_new,
        gains_second_new,
        heads_first_new,
        heads_second_new,
        output_first_new,
        output_second_new,
        expand_first_new,
        expand_second_new,
        down_first_new,
        down_second_new,
    )


def solution(mesh):
    return jax.shard_map(
        local,
        mesh=mesh,
        in_specs=(
            P(("dp", "shard"), None),
            P(("dp", "shard"), None),
            P("dp", None),
            P(("dp", "shard")),
            P(),
            P("shard", "dp"),
            P("shard", "dp"),
            P("shard", "dp"),
            P("shard", "dp"),
            P(),
            P(),
            P("shard", "dp"),
            P("shard", "dp"),
            P("shard", "dp"),
            P("shard", "dp"),
            P("shard", "dp"),
            P("shard", "dp"),
            P("shard", "dp"),
            P("shard", "dp"),
        ),
        out_specs=(
            P(("dp", "shard"), None),
            P(("dp", "shard"), None),
            P(),
            P("shard", "dp"),
            P("shard", "dp"),
            P("shard", "dp"),
            P("shard", "dp"),
            P(),
            P("shard", "dp"),
            P("shard", "dp"),
            P("shard", "dp"),
            P("shard", "dp"),
            P(),
            P(),
            P("shard", "dp"),
            P("shard", "dp"),
            P("shard", "dp"),
            P("shard", "dp"),
            P("shard", "dp"),
            P("shard", "dp"),
            P("shard", "dp"),
            P("shard", "dp"),
        ),
        check_vma=False,
    )
```

profile of v0, /device:TPU:0, one launch (start us, length us, event | category | flops | bytes accessed | tf_op | source)
XLA Modules:
  0.0 1189.5 jit_solution(16421250577596304187)
XLA Ops:
  8.3 12.0 %all_gather.27 = bf16[240,1600]{0,1:T(8,128)(2,1)S(1)} all-gather(bf16[240,200]{0,1:T(8,128)(2,1)S(1)} %convert_element_type.115), channel_id=1, replica_groups=mesh['dp'=8,'shard'=4] {'dp'}, dimensions={1}, use_global_device_ids=true | all-gather | bytes 864000 | tf_op jit(solution)/shard_map/all_gather | solution.py:194
  26.0 60.3 %all-gather.8.cloned.1.call-done = bf16[960,1600]{1,0:T(8,128)(2,1)} async-done(((bf16[240,1600]{1,0:T(8,128)(2,1)}), bf16[960,1600]{1,0:T(8,128)(2,1)}) %all-gather.8.cloned.1.call-update) | async-done | bytes 3072016 | tf_op jit(solution)/shard_map/all_gather | solution.py:200
  86.4 4.0 fusion.132
  93.9 12.5 %all_gather.30 = bf16[240,960]{0,1:T(8,128)(2,1)} all-gather(bf16[240,120]{0,1:T(8,128)(2,1)} %copy.89), channel_id=1, replica_groups=mesh['dp'=8,'shard'=4] {'dp'}, dimensions={1}, use_global_device_ids=true | all-gather | bytes 518400 | tf_op jit(solution)/shard_map/all_gather | solution.py:195
  108.5 9.7 all-gather.14.cloned.1.call-done
  120.1 24.8 %all-gather.18.cloned.1.call-done = bf16[640,960]{0,1:T(8,128)(2,1)} async-done(((bf16[640,120]{0,1:T(8,128)(2,1)}), bf16[640,960]{0,1:T(8,128)(2,1)}) %all-gather.18.cloned.1.call-update) | async-done | bytes 1228816 | tf_op jit(solution)/shard_map/all_gather | solution.py:197
  146.0 55.6 %all-gather.10.cloned.1.call-done = bf16[2048,640]{0,1:T(8,128)(2,1)} async-done(((bf16[512,640]{0,1:T(8,128)(2,1)}), bf16[2048,640]{0,1:T(8,128)(2,1)}) %all-gather.10.cloned.1.call-update) | async-done | bytes 2621456 | tf_op jit(solution)/shard_map/all_gather | solution.py:231
  204.5 6.9 fusion.137
  211.4 6.4 fusion.136
  217.9 6.4 fusion.135
  224.3 20.9 %fusion.34 = (f32[3,512]{1,0:T(4,128)S(1)}, f32[3,512]{1,0:T(4,128)S(1)}, f32[3,512]{1,0:T(4,128)S(1)}, f32[3,512]{1,0:T(4,128)S(1)}, f32[3,512]{1,0:T(4,128)S(1)}, /*index=5*/f32[2048,512,3]{1,0,2:T(8,128)}) fusion(pred[512,2048]{0,1:T(8,128)(4,1)S(1)} %copy-done.25, f32[2048,512,3]{1,0,2:T(8,128)} %fusion.136, f32[2048,512,3]{1,0,2:T(8,128)} %fusion.137, ...), kind=kOutput, calls=%fused_computation.54 | convolution fusion | flops 449831424 | bytes 64452608 | tf_op jit(solution)/shard_map/qhd,kd->hqk/dot_general | solution.py:110
  247.1 6.4 fusion.124
  253.5 7.8 fusion.122
  261.3 6.4 fusion.120
  267.8 3.5 fusion.118
  271.2 6.7 fusion.116
  281.0 138.3 %all-gather.16.cloned.1.call-done = bf16[960,5120]{1,0:T(8,128)(2,1)} async-done(((bf16[240,5120]{1,0:T(8,128)(2,1)}), bf16[960,5120]{1,0:T(8,128)(2,1)}) %all-gather.16.cloned.1.call-update) | async-done | bytes 9830416 | tf_op jit(solution)/shard_map/all_gather | solution.py:202
  419.3 12.2 %fusion.188 = f32[512,5120]{1,0:T(8,128)} fusion(bf16[960,5120]{1,0:T(8,128)(2,1)} %all-gather.16.cloned.1.call-done, f32[512,960]{0,1:T(8,128)S(1)} %get-tuple-element.68, f32[960]{0:T(1024)S(1)} %bitcast.381, f32[512]{0:T(512)S(1)} %add_rsqrt_fusion), kind=kOutput, calls=%fused_computation.266 | convolution fusion | flops 5034639360 | bytes 22288128 | tf_op jit(solution)/shard_map/dot_general | solution.py:237
  431.5 80.2 %all-gather.20.cloned.1.call-done = bf16[2560,960]{0,1:T(8,128)(2,1)} async-done(((bf16[640,960]{0,1:T(8,128)(2,1)}), bf16[2560,960]{0,1:T(8,128)(2,1)}) %all-gather.20.cloned.1.call-update) | async-done | bytes 4915216 | tf_op jit(solution)/shard_map/all_gather | solution.py:203
  511.8 11.5 multiply_convert_fusion.1
  523.3 9.8 multiply_reduce_fusion
  537.5 6.1 fusion.14
  546.5 7.4 fusion.11
  556.7 8.6 fusion.8
  568.3 6.1 fusion.5
  577.2 7.7 fusion.2
  588.0 6.9 fusion.71
  594.9 6.9 fusion.77
  601.8 7.0 fusion.83
  608.8 3.6 fusion.89
  612.5 3.6 fusion.95
  621.1 8.8 fusion.195
  629.9 4.3 fusion.114
  634.2 4.2 fusion.113
  646.7 61.8 %reduce-scatter.14.cloned.1.call-done = f32[512,640]{0,1:T(8,128)} async-done(((f32[2048,640]{0,1:T(8,128)}), f32[512,640]{0,1:T(8,128)}) %reduce-scatter.14.cloned.1.call-update) | async-done | bytes 1310736 | tf_op jit(solution)/shard_map/reduce_scatter | solution.py:266
  711.6 5.9 fusion.125
  717.6 12.7 %fusion.62 = f32[960,5120]{1,0:T(8,128)} fusion(bf16[512,2560]{1,0:T(8,128)(2,1)} %get-tuple-element.47, bf16[512,2560]{1,0:T(8,128)(2,1)} %get-tuple-element.46, f32[512,960]{0,1:T(8,128)} %copy-done.13, f32[960]{0:T(1024)S(1)} %bitcast.384, f32[512]{0:T(512)S(1)} %add_rsqrt_fusion), kind=kOutput, calls=%fused_computation.83 | convolution fusion | flops 5045125120 | bytes 26875648 | tf_op jit(solution)/shard_map/dot_general | solution.py:80
  730.4 32.0 %reduce-scatter.30.cloned.1.call-done = f32[120,960]{1,0:T(8,128)} async-done(((f32[960,960]{1,0:T(8,128)}), f32[120,960]{1,0:T(8,128)}) %reduce-scatter.30.cloned.1.call-update) | async-done | bytes 460816
  764.5 80.0 %reduce-scatter.24.cloned.1.call-done = f32[2560,120]{0,1:T(8,128)} async-done(((f32[2560,960]{0,1:T(8,128)}), f32[2560,120]{0,1:T(8,128)}) %reduce-scatter.24.cloned.1.call-update) | async-done | bytes 1228816 | tf_op jit(solution)/shard_map/reduce_scatter | solution.py:287
  844.5 66.4 %reduce-scatter.16.cloned.1.call-done = f32[960,200]{0,1:T(8,128)} async-done(((f32[960,1600]{0,1:T(8,128)}), f32[960,200]{0,1:T(8,128)}) %reduce-scatter.16.cloned.1.call-update) | async-done | bytes 768016 | tf_op jit(solution)/shard_map/reduce_scatter | solution.py:284
  913.7 130.5 %reduce-scatter.20.cloned.1.call-done = f32[960,640]{1,0:T(8,128)} async-done(((f32[960,5120]{1,0:T(8,128)}), f32[960,640]{1,0:T(8,128)}) %reduce-scatter.20.cloned.1.call-update) | async-done | bytes 2457616 | tf_op jit(solution)/shard_map/reduce_scatter | solution.py:286
  1044.3 7.5 add_convert_fusion
  1051.8 17.5 %reduce-scatter.18.cloned.1.call-done = f32[240,120]{1,0:T(8,128)} async-done(((f32[960,120]{1,0:T(8,128)}), f32[240,120]{1,0:T(8,128)}) %reduce-scatter.18.cloned.1.call-update) | async-done | bytes 115216 | tf_op jit(solution)/shard_map/reduce_scatter | solution.py:291
  1071.0 5.6 fusion.108
  1076.7 39.8 %psum.7 = f32[2,960]{1,0:T(2,128)S(1)} all-reduce(f32[2,960]{1,0:T(2,128)S(1)} %pad_maximum_fusion.11), channel_id=1, replica_groups=mesh['dp'=8,'shard'=4] {'dp','shard'}, use_global_device_ids=true, to_apply=%region_13.14 | all-reduce | flops 1920 | bytes 15360 | tf_op jit(solution)/shard_map/psum | solution.py:282
  1117.1 3.3 fusion.107
  1122.6 5.8 reduce-scatter.28.cloned.1.call-done
  1131.6 47.9 %reduce-scatter.22.cloned.1.call-done = f32[240,640]{1,0:T(8,128)} async-done(((f32[960,640]{1,0:T(8,128)}), f32[240,640]{1,0:T(8,128)}) %reduce-scatter.22.cloned.1.call-update) | async-done | bytes 614416 | tf_op jit(solution)/shard_map/reduce_scatter | solution.py:292
  (251 shorter events, 73.8 us)
Async XLA Ops:
  7.2 18.2 %copy-start.15 = (bf16[512,960]{0,1:T(8,128)(2,1)S(1)}, bf16[512,960]{0,1:T(8,128)(2,1)}, u32[]{:S(2)}) copy-start(bf16[512,960]{0,1:T(8,128)(2,1)} %param.19) | copy-start | bytes 2949124
  7.2 18.4 %copy-start.58 = (s32[512]{0:T(512)S(1)}, s32[512]{0:T(512)}, u32[]{:S(2)}) copy-start(s32[512]{0:T(512)} %param.22) | copy-start | bytes 6148
  7.2 18.4 %copy-start.38 = (f32[2,960]{1,0:T(2,128)S(1)}, f32[2,960]{1,0:T(2,128)}, u32[]{:S(2)}) copy-start(f32[2,960]{1,0:T(2,128)} %param.23) | copy-start | bytes 23044
  7.2 79.1 %all-gather.8.cloned.1.call-start = ((), (), s32[]{:S(2)}) async-start(), calls=%async_computation.9 | async-start | bytes 3993600 | tf_op jit(solution)/shard_map/all_gather | solution.py:200
  21.6 96.5 %all-gather.14.cloned.1.call-start = ((), (), s32[]{:S(2)}) async-start(), calls=%async_computation.12 | async-start | bytes 2764800 | tf_op jit(solution)/shard_map/all_gather | solution.py:196
  23.6 121.3 %all-gather.18.cloned.1.call-start = ((), (), s32[]{:S(2)}) async-start(), calls=%async_computation.14 | async-start | bytes 1382400 | tf_op jit(solution)/shard_map/all_gather | solution.py:197
  25.3 176.3 %all-gather.10.cloned.1.call-start = ((), (), s32[]{:S(2)}) async-start(), calls=%async_computation.10 | async-start | bytes 3276800 | tf_op jit(solution)/shard_map/all_gather | solution.py:231
  25.6 60.7 %copy-start.44 = (f32[512]{0:T(512)}, f32[512]{0:T(512)S(1)}, u32[]{:S(2)}) copy-start(f32[512]{0:T(512)S(1)} %add_rsqrt_fusion.1) | copy-start | bytes 6148
  25.7 60.7 %copy-start.41 = (f32[1,960]{1,0:T(1,128)}, f32[1,960]{1,0:T(1,128)S(1)}, u32[]{:S(2)}) copy-start(f32[1,960]{1,0:T(1,128)S(1)} %get-tuple-element.63) | copy-start | bytes 11524
  26.0 119.6 %copy-start.20 = (f32[512,32]{0,1:T(8,128)}, f32[512,32]{0,1:T(8,128)S(1)}, u32[]{:S(2)}) copy-start(f32[512,32]{0,1:T(8,128)S(1)} %get-tuple-element.64) | copy-start | bytes 196612
  26.0 119.6 %copy-start.22 = (f32[512,32]{0,1:T(8,128)}, f32[512,32]{0,1:T(8,128)S(1)}, u32[]{:S(2)}) copy-start(f32[512,32]{0,1:T(8,128)S(1)} %get-tuple-element.65) | copy-start | bytes 196612
  90.4 27.9 %copy-start.43 = (s32[1,2048]{1,0:T(1,128)S(1)}, s32[1,2048]{1,0:T(1,128)}, u32[]{:S(2)}) copy-start(s32[1,2048]{1,0:T(1,128)} %param.21) | copy-start | bytes 24580
  92.1 53.3 %copy-start.18 = (f32[512,1600]{0,1:T(8,128)S(1)}, f32[512,1600]{0,1:T(8,128)}, u32[]{:S(2)}) copy-start(f32[512,1600]{0,1:T(8,128)} %copy-done.17) | copy-start | bytes 9830404
  93.1 184.8 %all-gather.12.cloned.1.call-start = ((), (), s32[]{:S(2)}) async-start(), calls=%async_computation.11 | async-start | bytes 2457600 | tf_op jit(solution)/shard_map/all_gather | solution.py:201
  108.5 310.9 %all-gather.16.cloned.1.call-start = ((), (), s32[]{:S(2)}) async-start(), calls=%async_computation.13 | async-start | bytes 12288000 | tf_op jit(solution)/shard_map/all_gather | solution.py:202
  118.2 393.5 %all-gather.20.cloned.1.call-start = ((), (), s32[]{:S(2)}) async-start(), calls=%async_computation.15 | async-start | bytes 6144000 | tf_op jit(solution)/shard_map/all_gather | solution.py:203
  144.8 563.6 %reduce-scatter.14.cloned.1.call-start = ((), (), s32[]{:S(2)}) async-start(), calls=%async_computation.16 | async-start | bytes 6553600 | tf_op jit(solution)/shard_map/reduce_scatter | solution.py:266
  146.0 71.9 %copy-start = (bf16[512,15,32]{0,2,1:T(8,128)(2,1)}, bf16[512,15,32]{0,2,1:T(8,128)(2,1)S(1)}, u32[]{:S(2)}) copy-start(bf16[512,15,32]{0,2,1:T(8,128)(2,1)S(1)} %get-tuple-element.51) | copy-start | bytes 1474564
  146.0 71.9 %copy-start.2 = (bf16[512,15,32]{0,2,1:T(8,128)(2,1)}, bf16[512,15,32]{0,2,1:T(8,128)(2,1)S(1)}, u32[]{:S(2)}) copy-start(bf16[512,15,32]{0,2,1:T(8,128)(2,1)S(1)} %get-tuple-element.52) | copy-start | bytes 1474564
  146.0 78.3 %copy-start.32 = (bf16[512,3,64]{0,2,1:T(8,128)(2,1)}, bf16[512,3,64]{0,2,1:T(8,128)(2,1)S(1)}, u32[]{:S(2)}) copy-start(bf16[512,3,64]{0,2,1:T(8,128)(2,1)S(1)} %pad_maximum_fusion.10) | copy-start | bytes 589828
  204.5 63.2 %copy-start.9 = (f32[2048,512,3]{1,0,2:T(8,128)}, f32[2048,512,3]{1,0,2:T(8,128)S(1)}, u32[]{:S(2)}) copy-start(f32[2048,512,3]{1,0,2:T(8,128)S(1)} %fusion.138) | copy-start | bytes 37748740
  245.8 300.6 %copy-start.53 = (f32[3,512]{1,0:T(4,128)}, f32[3,512]{1,0:T(4,128)S(1)}, u32[]{:S(2)}) copy-start(f32[3,512]{1,0:T(4,128)S(1)} %log.36) | copy-start | bytes 18436
  247.1 290.2 %copy-start.55 = (f32[3,512]{1,0:T(4,128)}, f32[3,512]{1,0:T(4,128)S(1)}, u32[]{:S(2)}) copy-start(f32[3,512]{1,0:T(4,128)S(1)} %log.35) | copy-start | bytes 18436
  281.0 150.5 %copy-start.13 = (f32[512,960]{0,1:T(8,128)}, f32[512,960]{0,1:T(8,128)S(1)}, u32[]{:S(2)}) copy-start(f32[512,960]{0,1:T(8,128)S(1)} %get-tuple-element.68) | copy-start | bytes 5898244
  511.8 25.5 %slice-start.9 = ((s8[12582912]{0:T(1024)(128)(4,1)}), s8[4194304]{0:T(1024)(128)(4,1)S(1)}, s32[]{:S(2)}) async-start(s8[12582912]{0:T(1024)(128)(4,1)} %bitcast.359), calls=%async_computation.34 | async-start | bytes 8388608
  511.8 25.5 %slice-start.10 = ((s8[12582912]{0:T(1024)(128)(4,1)}), s8[4194304]{0:T(1024)(128)(4,1)S(1)}, s32[]{:S(2)}) async-start(s8[12582912]{0:T(1024)(128)(4,1)} %bitcast.359), calls=%async_computation.35 | async-start | bytes 8388608
  523.2 14.0 %slice-start.11 = ((s8[12582912]{0:T(1024)(128)(4,1)}), s8[4194304]{0:T(1024)(128)(4,1)S(1)}, s32[]{:S(2)}) async-start(s8[12582912]{0:T(1024)(128)(4,1)} %bitcast.359), calls=%async_computation.36 | async-start | bytes 8388608
  553.9 14.3 %slice-start.6 = ((s8[12582912]{0:T(1024)(128)(4,1)}), s8[4194304]{0:T(1024)(128)(4,1)S(1)}, s32[]{:S(2)}) async-start(s8[12582912]{0:T(1024)(128)(4,1)} %bitcast.357), calls=%async_computation.31 | async-start | bytes 8388608
  616.2 146.2 %reduce-scatter.30.cloned.1.call-start = ((), (), s32[]{:S(2)}) async-start(), calls=%async_computation.24 | async-start | bytes 4423680
  620.8 223.7 %reduce-scatter.24.cloned.1.call-start = ((), (), s32[]{:S(2)}) async-start(), calls=%async_computation.21 | async-start | bytes 11059200 | tf_op jit(solution)/shard_map/reduce_scatter | solution.py:287
  629.9 281.1 %reduce-scatter.16.cloned.1.call-start = ((), (), s32[]{:S(2)}) async-start(), calls=%async_computation.17 | async-start | bytes 7372800 | tf_op jit(solution)/shard_map/reduce_scatter | solution.py:284
  645.3 66.3 %copy-start.16 = (bf16[512,960]{0,1:T(8,128)(2,1)S(1)}, bf16[512,960]{0,1:T(8,128)(2,1)}, u32[]{:S(2)}) copy-start(bf16[512,960]{0,1:T(8,128)(2,1)} %param.19) | copy-start | bytes 2949124
  645.3 66.3 %copy-start.42 = (f32[1,960]{1,0:T(1,128)S(1)}, f32[1,960]{1,0:T(1,128)}, u32[]{:S(2)}) copy-start(f32[1,960]{1,0:T(1,128)} %copy-done.41) | copy-start | bytes 11524
  645.3 66.3 %copy-start.45 = (f32[512]{0:T(512)S(1)}, f32[512]{0:T(512)}, u32[]{:S(2)}) copy-start(f32[512]{0:T(512)} %copy-done.44) | copy-start | bytes 6148
  717.6 326.7 %reduce-scatter.20.cloned.1.call-start = ((), (), s32[]{:S(2)}) async-start(), calls=%async_computation.19 | async-start | bytes 22118400 | tf_op jit(solution)/shard_map/reduce_scatter | solution.py:286
  730.4 338.9 %reduce-scatter.18.cloned.1.call-start = ((), (), s32[]{:S(2)}) async-start(), calls=%async_computation.18 | async-start | bytes 614400 | tf_op jit(solution)/shard_map/reduce_scatter | solution.py:291
  764.4 356.0 %reduce-scatter.26.cloned.1.call-start = ((), (), s32[]{:S(2)}) async-start(), calls=%async_computation.22 | async-start | bytes 1536000 | tf_op jit(solution)/shard_map/reduce_scatter | solution.py:293
  844.5 284.0 %reduce-scatter.28.cloned.1.call-start = ((), (), s32[]{:S(2)}) async-start(), calls=%async_computation.23 | async-start | bytes 1228800
  913.4 266.1 %reduce-scatter.22.cloned.1.call-start = ((), (), s32[]{:S(2)}) async-start(), calls=%async_computation.20 | async-start | bytes 3072000 | tf_op jit(solution)/shard_map/reduce_scatter | solution.py:292
  1044.3 25.0 %copy-start.35 = (f32[240,120]{1,0:T(8,128)S(1)}, f32[240,120]{1,0:T(8,128)}, u32[]{:S(2)}) copy-start(f32[240,120]{1,0:T(8,128)} %param.25) | copy-start | bytes 345604
  1044.3 25.0 %copy-start.37 = (f32[240,120]{1,0:T(8,128)S(1)}, f32[240,120]{1,0:T(8,128)}, u32[]{:S(2)}) copy-start(f32[240,120]{1,0:T(8,128)} %param.32) | copy-start | bytes 345604
  1071.0 45.4 %copy-start.39 = (f32[2,960]{1,0:T(2,128)S(1)}, f32[2,960]{1,0:T(2,128)}, u32[]{:S(2)}) copy-start(f32[2,960]{1,0:T(2,128)} %param.23) | copy-start | bytes 23044
  1071.0 45.4 %copy-start.46 = (f32[2,960]{1,0:T(2,128)S(1)}, f32[2,960]{1,0:T(2,128)}, u32[]{:S(2)}) copy-start(f32[2,960]{1,0:T(2,128)} %param.28) | copy-start | bytes 23044
  1071.0 45.4 %copy-start.47 = (f32[2,960]{1,0:T(2,128)S(1)}, f32[2,960]{1,0:T(2,128)}, u32[]{:S(2)}) copy-start(f32[2,960]{1,0:T(2,128)} %param.29) | copy-start | bytes 23044
  1076.6 43.8 %copy-start.24 = (f32[640,120]{0,1:T(8,128)S(1)}, f32[640,120]{0,1:T(8,128)}, u32[]{:S(2)}) copy-start(f32[640,120]{0,1:T(8,128)} %param.27) | copy-start | bytes 921604
  1076.6 52.9 %copy-start.31 = (f32[240,200]{0,1:T(8,128)S(1)}, f32[240,200]{0,1:T(8,128)}, u32[]{:S(2)}) copy-start(f32[240,200]{0,1:T(8,128)} %param.24) | copy-start | bytes 576004
  1116.4 15.1 %copy-start.40 = (f32[2,960]{1,0:T(2,128)}, f32[2,960]{1,0:T(2,128)S(1)}, u32[]{:S(2)}) copy-start(f32[2,960]{1,0:T(2,128)S(1)} %psum.7) | copy-start | bytes 23044
  1129.5 53.1 %copy-start.30 = (f32[240,200]{0,1:T(8,128)}, f32[240,200]{0,1:T(8,128)S(1)}, u32[]{:S(2)}) copy-start(f32[240,200]{0,1:T(8,128)S(1)} %copy.127) | copy-start | bytes 576004
  (43 other events, 250.5 us)
Sparse Core Ops, SparseCore 0:
  21.8 64.5 all-gather.7
  88.8 29.3 all-gather.13
  120.7 24.1 all-gather.17
  146.8 54.7 all-gather.9
  203.6 42.2 all-gather.11
  247.3 172.0 all-gather.15
  420.9 90.8 all-gather.19
  616.3 92.1 reduce-scatter.13
  712.0 50.3 reduce-scatter.29
  765.8 78.6 reduce-scatter.23
  847.9 63.0 reduce-scatter.15
  914.5 129.7 reduce-scatter.19
  1047.7 21.5 reduce-scatter.17
  1072.0 29.2 reduce-scatter.25
  1103.4 24.9 reduce-scatter.27
  1131.2 48.2 reduce-scatter.21
where the time goes:
time: 1200 us; the launch traced here: 1190 us
  waiting for transfers between devices  811 us (68%)
  matrix products  253 us (21%)
  blocking collectives  64.3 us (5%)
  other arithmetic  25.5 us (2%)
  local copies, waits for them, and re-layouts  18.6 us (2%)
  between operations  15.3 us (1%)
    all_gather x1, waiting for transfers between devices, local(): lax.all_gather(sectioned[2], 'shard', axis=0, tiled=True)  138 us
    reduce_scatter x1, waiting for transfers between devices, local(): lax.psum_scatter(expand_term, 'dp', scatter_dimension=1, tiled=True)  131 us
    all_gather x1, waiting for transfers between devices, local(): lax.all_gather(sectioned[3], 'shard', axis=0, tiled=True)  80.2 us
    reduce_scatter x1, waiting for transfers between devices, local(): lax.psum_scatter(down_term, 'dp', scatter_dimension=1, tiled=True)  80 us
    reduce_scatter x1, waiting for transfers between devices, local(): lax.psum_scatter(heads_term, 'dp', scatter_dimension=1, tiled=True)  66.4 us
    reduce_scatter x1, waiting for transfers between devices, local(): lax.psum_scatter(packed_terms, 'shard', scatter_dimension=0, tiled=True)  61.8 us
    all_gather x1, waiting for transfers between devices, local(): lax.all_gather(sectioned[0], 'shard', axis=0, tiled=True)  60.3 us
    all_gather x1, waiting for transfers between devices, local(): all_keys = lax.all_gather(packed, 'shard', axis=0, tiled=True)  55.6 us
  transfers between devices with their start and end apart: 16, of which 14 were waited for; matrix products, arithmetic and copies ran while one was open for 15% of the time, Pallas kernels for 0%

commit v1 on v0

--- a/solution.py
+++ b/solution.py
@@ -1,7 +1,464 @@
+import functools
+import math
+
 import jax
 import jax.numpy as jnp
 from jax import lax
+from jax.experimental import pallas as pl
+from jax.experimental.pallas import tpu as pltpu
 from jax.sharding import PartitionSpec as P
+
+MESH = pl.DeviceIdType.MESH
+ANY = pl.BlockSpec(memory_space=pl.ANY)
+VMEM = pl.BlockSpec(memory_space=pltpu.VMEM)
+
+
+class Grid:
+    def __init__(self, mesh):
+        self.nd = mesh.shape["dp"]
+        self.nz = mesh.shape["shard"]
+        self.nx = math.isqrt(self.nd // 2)
+        self.ny = self.nd // 2 // self.nx
+        assert self.nx == self.ny and self.nx * self.ny * 2 == self.nd
+
+    def dp(self, y, x, c):
+        return (y * self.nx + x) * 2 + c
+
+
+class Here:
+    def __init__(self, grid):
+        self.grid = grid
+        d = lax.axis_index("dp")
+        self.z = lax.axis_index("shard")
+        self.d = d
+        self.c = lax.rem(d, 2)
+        self.x = lax.rem(d // 2, grid.nx)
+        self.y = d // (2 * grid.nx)
+        g = grid
+        self.xs = [lax.rem(self.x + k, g.nx) for k in range(1, g.nx)]
+        self.ys = [lax.rem(self.y + k, g.ny) for k in range(1, g.ny)]
+        self.zs = [lax.rem(self.z + k, g.nz) for k in range(1, g.nz)]
+        self.partner = (g.dp(self.y, self.x, 1 - self.c), self.z)
+
+    def on_x(self, x):
+        return (self.grid.dp(self.y, x, self.c), self.z)
+
+    def on_y(self, y):
+        return (self.grid.dp(y, self.x, self.c), self.z)
+
+    def on_z(self, z):
+        return (self.d, z)
+
+    def peers(self):
+        return (
+            [self.partner]
+            + [self.on_x(x) for x in self.xs]
+            + [self.on_y(y) for y in self.ys]
+            + [self.on_z(z) for z in self.zs]
+        )
+
+
+def greet(peers):
+    barrier = pltpu.get_barrier_semaphore()
+    for peer in peers:
+        pl.semaphore_signal(barrier, inc=1, device_id=peer, device_id_type=MESH)
+    pl.semaphore_wait(barrier, len(peers))
+
+
+def send(src, dst, send_sem, recv_sem, device):
+    pltpu.make_async_remote_copy(
+        src_ref=src,
+        dst_ref=dst,
+        send_sem=send_sem,
+        recv_sem=recv_sem,
+        device_id=device,
+        device_id_type=MESH,
+    ).start()
+
+
+def wait_bytes(ref, sem):
+    pltpu.make_async_copy(ref, ref, sem).wait()
+
+
+def half_rows(rows):
+    return max(16, int(rows / 32 + 0.5) * 16)
+
+
+class Gather:
+    def __init__(self, here, shard, out, sems, z_major):
+        self.h, self.shard, self.out, self.sems, self.z_major = here, shard, out, sems, z_major
+        self.rows = shard.shape[0]
+        self.cut = half_rows(self.rows)
+
+    def column(self, d, half=None):
+        rows = {None: slice(None), 0: pl.ds(0, self.cut), 1: pl.ds(self.cut, self.rows - self.cut)}[half]
+        if self.z_major:
+            return self.out.at[:, d, rows]
+        return self.out.at[d, :, rows]
+
+    def block(self, d, z):
+        return self.out.at[z, d] if self.z_major else self.out.at[d, z]
+
+    def columns(self, count):
+        return self.out.at[:, pl.ds(0, count)] if self.z_major else self.out.at[pl.ds(0, count)]
+
+    def blocks(self, count):
+        return self.out.at[pl.ds(0, count), 0] if self.z_major else self.out.at[0, pl.ds(0, count)]
+
+    def stage_z(self):
+        h, s = self.h, self.sems
+        for z in h.zs:
+            send(self.shard, self.block(h.d, h.z), s.at[0], s.at[1], h.on_z(z))
+        self.own = pltpu.make_async_copy(self.shard, self.block(h.d, h.z), s.at[8])
+        self.own.start()
+
+    def stage_one(self):
+        h, s = self.h, self.sems
+        wait_bytes(self.blocks(len(h.zs)), s.at[1])
+        self.own.wait()
+        for x in h.xs:
+            send(self.column(h.d, 0), self.column(h.d, 0), s.at[2], s.at[3], h.on_x(x))
+        for y in h.ys:
+            send(self.column(h.d, 1), self.column(h.d, 1), s.at[2], s.at[3], h.on_y(y))
+        send(self.column(h.d), self.column(h.d), s.at[6], s.at[7], h.partner)
+
+    def stage_two(self):
+        h, s, g = self.h, self.sems, self.h.grid
+        wait_bytes(self.columns(len(h.xs)), s.at[3])
+        for y in h.ys:
+            for x in [h.x] + h.xs:
+                col = self.column(g.dp(h.y, x, h.c), 0)
+                send(col, col, s.at[4], s.at[5], h.on_y(y))
+        for x in h.xs:
+            for y in [h.y] + h.ys:
+                col = self.column(g.dp(y, h.x, h.c), 1)
+                send(col, col, s.at[4], s.at[5], h.on_x(x))
+        for x in h.xs:
+            col = self.column(g.dp(h.y, x, h.c), 0)
+            send(col, col, s.at[6], s.at[7], h.partner)
+        for y in h.ys:
+            col = self.column(g.dp(y, h.x, h.c), 1)
+            send(col, col, s.at[6], s.at[7], h.partner)
+
+    def stage_three(self):
+        h, s, g = self.h, self.sems, self.h.grid
+        wait_bytes(self.columns(g.nx * len(h.ys)), s.at[5])
+        for y in h.ys:
+            for x in [h.x] + h.xs:
+                col = self.column(g.dp(y, x, h.c), 0)
+                send(col, col, s.at[6], s.at[7], h.partner)
+        for x in h.xs:
+            for y in [h.y] + h.ys:
+                col = self.column(g.dp(y, x, h.c), 1)
+                send(col, col, s.at[6], s.at[7], h.partner)
+
+    def arrive(self):
+        g = self.h.grid
+        wait_bytes(self.columns(g.nd // 2), self.sems.at[7])
+
+    def drain(self):
+        h, s, g = self.h, self.sems, self.h.grid
+        wait_bytes(self.blocks(len(h.zs)), s.at[0])
+        wait_bytes(self.columns(len(h.xs)), s.at[2])
+        wait_bytes(self.columns(g.nx * len(h.ys)), s.at[4])
+        wait_bytes(self.columns(g.nd // 2), s.at[6])
+
+
+GATHER_SEMS = 9
+
+
+def gather_kernel(grid, z_majors, *refs):
+    n = len(z_majors)
+    shards, outs, sems = refs[:n], refs[n : 2 * n], refs[2 * n]
+    here = Here(grid)
+    greet(here.peers())
+    jobs = [Gather(here, shards[i], outs[i], sems.at[i], z_majors[i]) for i in range(n)]
+    for job in jobs:
+        job.stage_z()
+    for step in range(n + 2):
+        if step < n:
+            jobs[step].stage_one()
+        if 0 <= step - 1 < n:
+            jobs[step - 1].stage_two()
+        if 0 <= step - 2 < n:
+            jobs[step - 2].stage_three()
+    for job in jobs:
+        job.arrive()
+        job.drain()
+
+
+def gather_weights(grid, shards, z_majors, collective_id):
+    shapes = []
+    for shard, z_major in zip(shards, z_majors):
+        lead = (grid.nz, grid.nd) if z_major else (grid.nd, grid.nz)
+        shapes.append(jax.ShapeDtypeStruct(lead + shard.shape, shard.dtype))
+    return pl.pallas_call(
+        functools.partial(gather_kernel, grid, tuple(z_majors)),
+        out_shape=shapes,
+        in_specs=[VMEM] * len(shards),
+        out_specs=[ANY] * len(shards),
+        scratch_shapes=[pltpu.SemaphoreType.DMA((len(shards), GATHER_SEMS))],
+        compiler_params=pltpu.CompilerParams(collective_id=collective_id, has_side_effects=True),
+        name="gather_weights",
+    )(*shards)
+
+
+class Reduce:
+    def __init__(self, here, terms, result, bufs, sems, z_major):
+        self.h, self.terms, self.result, self.sems, self.z_major = here, terms, result, sems, z_major
+        self.own, self.other, self.one_a, self.one_b, self.two_a, self.two_b, self.last = bufs
+        self.rows = self.own.shape[-2]
+        self.cut = half_rows(self.rows)
+
+    @staticmethod
+    def scratch(grid, rows, cols, z_major):
+        cut = half_rows(rows)
+        ny, nx, nz = grid.ny, grid.nx, grid.nz
+        full = (nz, ny, nx) if z_major else (ny, nx, nz)
+        row = (nz, nx) if z_major else (nx, nz)
+        bf = jnp.bfloat16
+        return [
+            pltpu.VMEM(full + (rows, cols), bf),
+            pltpu.VMEM(full + (rows, cols), bf),
+            pltpu.VMEM((ny,) + row + (cut, cols), bf),
+            pltpu.VMEM((nx,) + row + (rows - cut, cols), bf),
+            pltpu.VMEM((nx, nz, cut, cols), bf),
+            pltpu.VMEM((ny, nz, rows - cut, cols), bf),
+            pltpu.VMEM((nz, rows, cols), bf),
+        ]
+
+    def span(self, half):
+        return {None: slice(None), 0: pl.ds(0, self.cut), 1: pl.ds(self.cut, self.rows - self.cut)}[half]
+
+    def at(self, y, x, z, half):
+        y, x, z = (slice(None) if v is None else v for v in (y, x, z))
+        return (z, y, x, self.span(half)) if self.z_major else (y, x, z, self.span(half))
+
+    def side(self, c):
+        return self.terms.at[:, :, :, c] if self.z_major else self.terms.at[:, :, c]
+
+    def stage_core(self):
+        h, s = self.h, self.sems
+        send(self.side(1 - h.c), self.other, s.at[0], s.at[1], h.partner)
+        self.load = pltpu.make_async_copy(self.side(h.c), self.own, s.at[8])
+        self.load.start()
+
+    def add_loop(self, shape, body):
+        total = math.prod(shape)
+
+        def step(i, carry):
+            place = []
+            rest = i
+            for size in reversed(shape):
+                place.append(lax.rem(rest, size))
+                rest = rest // size
+            body(tuple(reversed(place)))
+            return carry
+
+        lax.fori_loop(0, total, step, 0)
+
+    def stage_one(self):
+        h, s, g = self.h, self.sems, self.h.grid
+        self.load.wait()
+        wait_bytes(self.other, s.at[1])
+
+        def body(place):
+            total = self.own[place].astype(jnp.float32) + self.other[place].astype(jnp.float32)
+            self.own[place] = total.astype(jnp.bfloat16)
+
+        self.add_loop(self.own.shape[:3], body)
+        for y in h.ys:
+            send(self.own.at[self.at(y, None, None, 0)], self.one_a.at[h.y], s.at[2], s.at[3], h.on_y(y))
+        for x in h.xs:
+            send(self.own.at[self.at(None, x, None, 1)], self.one_b.at[h.x], s.at[9], s.at[10], h.on_x(x))
+
+    def stage_two(self):
+        h, s, g = self.h, self.sems, self.h.grid
+        wait_bytes(self.one_a.at[pl.ds(0, g.ny - 1)], s.at[3])
+        wait_bytes(self.one_b.at[pl.ds(0, g.nx - 1)], s.at[10])
+
+        def body_a(place):
+            where = (place[1], place[0]) if self.z_major else place
+            spot = self.at(h.y, where[0], where[1], 0)
+            total = self.own[spot].astype(jnp.float32)
+            for y in h.ys:
+                total += self.one_a[(y,) + place].astype(jnp.float32)
+            self.own[spot] = total.astype(jnp.bfloat16)
+
+        self.add_loop(self.one_a.shape[1:3], body_a)
+
+        def body_b(place):
+            where = (place[1], place[0]) if self.z_major else place
+            spot = self.at(where[0], h.x, where[1], 1)
+            total = self.own[spot].astype(jnp.float32)
+            for x in h.xs:
+                total += self.one_b[(x,) + place].astype(jnp.float32)
+            self.own[spot] = total.astype(jnp.bfloat16)
+
+        self.add_loop(self.one_b.shape[1:3], body_b)
+        for x in h.xs:
+            send(self.own.at[self.at(h.y, x, None, 0)], self.two_a.at[h.x], s.at[4], s.at[5], h.on_x(x))
+        for y in h.ys:
+            send(self.own.at[self.at(y, h.x, None, 1)], self.two_b.at[h.y], s.at[11], s.at[12], h.on_y(y))
+
+    def stage_three(self):
+        h, s, g = self.h, self.sems, self.h.grid
+        wait_bytes(self.two_a.at[pl.ds(0, g.nx - 1)], s.at[5])
+        wait_bytes(self.two_b.at[pl.ds(0, g.ny - 1)], s.at[12])
+
+        def body(place):
+            (z,) = place
+            spot = self.at(h.y, h.x, z, 0)
+            total = self.own[spot].astype(jnp.float32)
+            for x in h.xs:
+                total += self.two_a[x, z].astype(jnp.float32)
+            self.own[spot] = total.astype(jnp.bfloat16)
+            spot = self.at(h.y, h.x, z, 1)
+            total = self.own[spot].astype(jnp.float32)
+            for y in h.ys:
+                total += self.two_b[y, z].astype(jnp.float32)
+            self.own[spot] = total.astype(jnp.bfloat16)
+
+        self.add_loop((g.nz,), body)
+        for z in h.zs:
+            send(self.own.at[self.at(h.y, h.x, z, None)], self.last.at[h.z], s.at[6], s.at[7], h.on_z(z))
+
+    def finish(self):
+        h, s, g = self.h, self.sems, self.h.grid
+        wait_bytes(self.last.at[pl.ds(0, g.nz - 1)], s.at[7])
+        total = self.own[self.at(h.y, h.x, h.z, None)].astype(jnp.float32)
+        for z in h.zs:
+            total += self.last[z].astype(jnp.float32)
+        self.result[...] = total
+
+    def drain(self):
+        g, s = self.h.grid, self.sems
+        wait_bytes(self.other, s.at[0])
+        wait_bytes(self.one_a.at[pl.ds(0, g.ny - 1)], s.at[2])
+        wait_bytes(self.one_b.at[pl.ds(0, g.nx - 1)], s.at[9])
+        wait_bytes(self.two_a.at[pl.ds(0, g.nx - 1)], s.at[4])
+        wait_bytes(self.two_b.at[pl.ds(0, g.ny - 1)], s.at[11])
+        wait_bytes(self.last.at[pl.ds(0, g.nz - 1)], s.at[6])
+
+
+REDUCE_SEMS = 13
+REDUCE_BUFS = 7
+
+
+class Share:
+    def __init__(self, here, value, result, bufs, sems):
+        self.h, self.value, self.result, self.sems = here, value, result, sems
+        self.bufs = bufs
+
+    @staticmethod
+    def scratch(grid, shape):
+        return [pltpu.VMEM((n,) + shape, jnp.float32) for n in (2, grid.nx, grid.ny, grid.nz)]
+
+    def axis(self, k):
+        h = self.h
+        return (
+            (h.c, [h.partner], 2),
+            (h.x, [h.on_x(x) for x in h.xs], h.grid.nx),
+            (h.y, [h.on_y(y) for y in h.ys], h.grid.ny),
+            (h.z, [h.on_z(z) for z in h.zs], h.grid.nz),
+        )[k]
+
+    def start(self, k):
+        me, peers, n = self.axis(k)
+        self.bufs[k][me] = self.value[...] if k == 0 else self.total
+        for peer in peers:
+            send(self.bufs[k].at[me], self.bufs[k].at[me], self.sems.at[2 * k], self.sems.at[2 * k + 1], peer)
+
+    def end(self, k):
+        me, peers, n = self.axis(k)
+        wait_bytes(self.bufs[k].at[pl.ds(0, n - 1)], self.sems.at[2 * k + 1])
+        total = self.bufs[k][0]
+        for i in range(1, n):
+            total = total + self.bufs[k][i]
+        self.total = total
+        if k == 3:
+            self.result[...] = total
+
+    def drain(self):
+        for k in range(4):
+            n = self.axis(k)[2]
+            wait_bytes(self.bufs[k].at[pl.ds(0, n - 1)], self.sems.at[2 * k])
+
+
+SHARE_SEMS = 8
+
+
+def reduce_kernel(grid, z_majors, shared, *refs):
+    n = len(z_majors)
+    terms, refs = refs[:n], refs[n:]
+    value, refs = (refs[0], refs[1:]) if shared else (None, refs)
+    results, refs = refs[:n], refs[n:]
+    value_sum, refs = (refs[0], refs[1:]) if shared else (None, refs)
+    here = Here(grid)
+    greet(here.peers())
+    jobs = []
+    for i in range(n):
+        bufs, refs = refs[:REDUCE_BUFS], refs[REDUCE_BUFS:]
+        jobs.append((bufs, i))
+    sems, refs = refs[0], refs[1:]
+    jobs = [Reduce(here, terms[i], results[i], bufs, sems.at[i], z_majors[i]) for bufs, i in jobs]
+    share = None
+    if shared:
+        share = Share(here, value, value_sum, refs[:4], refs[4])
+        share.start(0)
+    for job in jobs:
+        job.stage_core()
+    for step in range(n + 3):
+        if step < n:
+            jobs[step].stage_one()
+        if 0 <= step - 1 < n:
+            jobs[step - 1].stage_two()
+        if 0 <= step - 2 < n:
+            jobs[step - 2].stage_three()
+        if 0 <= step - 3 < n:
+            jobs[step - 3].finish()
+        if share is not None and step < 4:
+            share.end(step)
+            if step < 3:
+                share.start(step + 1)
+    if share is not None:
+        for step in range(n + 3, 4):
+            share.end(step)
+            if step < 3:
+                share.start(step + 1)
+        share.drain()
+    for job in jobs:
+        job.drain()
+
+
+def reduce_grads(grid, terms, z_majors, value, collective_id):
+    split, shapes, scratch = [], [], []
+    for term, z_major in zip(terms, z_majors):
+        rows, cols = term.shape[-2:]
+        lead = (grid.ny, grid.nx, 2)
+        lead = (grid.nz,) + lead if z_major else lead + (grid.nz,)
+        split.append(term.reshape(lead + (rows, cols)))
+        shapes.append(jax.ShapeDtypeStruct((rows, cols), jnp.float32))
+        scratch += Reduce.scratch(grid, rows, cols, z_major)
+    n = len(terms)
+    scratch.append(pltpu.SemaphoreType.DMA((n, REDUCE_SEMS)))
+    shared = value is not None
+    if shared:
+        shapes.append(jax.ShapeDtypeStruct(value.shape, jnp.float32))
+        scratch += Share.scratch(grid, value.shape)
+        scratch.append(pltpu.SemaphoreType.DMA((SHARE_SEMS,)))
+    return pl.pallas_call(
+        functools.partial(reduce_kernel, grid, tuple(z_majors), shared),
+        out_shape=shapes,
+        in_specs=[ANY] * n + [VMEM] * shared,
+        out_specs=[VMEM] * len(shapes),
+        scratch_shapes=scratch,
+        compiler_params=pltpu.CompilerParams(
+            collective_id=collective_id, has_side_effects=True, vmem_limit_bytes=62 << 20
+        ),
+        name="reduce_grads",
+    )(*split, *([value] if shared else []))
+
 
 QUERY_HEADS = 15
 KEY_VALUE_HEADS = 5
@@ -166,7 +623,11 @@
     return (jnp.concatenate(query_grads, axis=1), jnp.concatenate(key_grads + value_grads, axis=1))
 
 
+Z_MAJOR = (True, True, False, True)
+
+
 def local(
+    grid,
     hidden_in,
     out_grad,
     seg_ids,
@@ -190,18 +651,21 @@
     count_of_rows = hidden_in.shape[0]
     query_total_width = QUERY_HEADS * HEAD_SIZE
     key_total_width = KEY_VALUE_HEADS * HEAD_SIZE
-    sectioned = (
-        lax.all_gather(heads_weight.astype(jnp.bfloat16), "dp", axis=1, tiled=True),
-        lax.all_gather(output_weight.astype(jnp.bfloat16), "dp", axis=1, tiled=True),
-        lax.all_gather(expand_weight.astype(jnp.bfloat16), "dp", axis=1, tiled=True),
-        lax.all_gather(down_weight.astype(jnp.bfloat16), "dp", axis=1, tiled=True),
-    )
-    heads_half, output_half, expand_half, down_half = (
-        lax.all_gather(sectioned[0], "shard", axis=0, tiled=True),
-        lax.all_gather(sectioned[1], "shard", axis=0, tiled=True),
-        lax.all_gather(sectioned[2], "shard", axis=0, tiled=True),
-        lax.all_gather(sectioned[3], "shard", axis=0, tiled=True),
-    )
+    heads_stack, output_stack, expand_stack, down_stack = gather_weights(
+        grid,
+        [
+            heads_weight.astype(jnp.bfloat16).T,
+            output_weight.astype(jnp.bfloat16).T,
+            expand_weight.astype(jnp.bfloat16),
+            down_weight.astype(jnp.bfloat16).T,
+        ],
+        Z_MAJOR,
+        1,
+    )
+    heads_half = heads_stack.transpose(0, 3, 1, 2).reshape(-1, heads_weight.shape[1] * grid.nd)
+    output_half = output_stack.transpose(0, 3, 1, 2).reshape(-1, output_weight.shape[1] * grid.nd)
+    expand_half = expand_stack.transpose(1, 2, 0, 3).reshape(-1, expand_weight.shape[1] * grid.nd)
+    down_half = down_stack.transpose(0, 3, 1, 2).reshape(-1, down_weight.shape[1] * grid.nd)
     first_row = lax.axis_index("shard") * count_of_rows
     positions = first_row + jnp.arange(count_of_rows, dtype=jnp.int32)
     cosine_table, sine_table = rotary_tables(positions - doc_start)
@@ -279,19 +743,19 @@
     hidden_one_grad = times_transposed(heads_delta, heads_half)
     input_back, gain_one_term = rms_backward(hidden_one_grad, normed_one, inverse_one, gain_one)
     input_grad = residual_grad + input_back
-    gains_grad = lax.psum(jnp.stack([gain_one_term, gain_two_term], axis=0), ("dp", "shard"))
-    reduced = (
-        lax.psum_scatter(heads_term, "dp", scatter_dimension=1, tiled=True),
-        lax.psum_scatter(output_term, "dp", scatter_dimension=1, tiled=True),
-        lax.psum_scatter(expand_term, "dp", scatter_dimension=1, tiled=True),
-        lax.psum_scatter(down_term, "dp", scatter_dimension=1, tiled=True),
-    )
-    heads_grad, output_grad, expand_grad, down_grad = (
-        lax.psum_scatter(reduced[0], "shard", scatter_dimension=0, tiled=True),
-        lax.psum_scatter(reduced[1], "shard", scatter_dimension=0, tiled=True),
-        lax.psum_scatter(reduced[2], "shard", scatter_dimension=0, tiled=True),
-        lax.psum_scatter(reduced[3], "shard", scatter_dimension=0, tiled=True),
-    )
+    def stacked(term, z_major):
+        rows, cols = term.shape[0] // grid.nz, term.shape[1] // grid.nd
+        term = term.astype(jnp.bfloat16).reshape(grid.nz, rows, grid.nd, cols)
+        return term.transpose(0, 2, 3, 1) if z_major else term.transpose(2, 0, 1, 3)
+
+    down_grad, expand_grad, output_grad, heads_grad, gains_grad = reduce_grads(
+        grid,
+        [stacked(down_term, True), stacked(expand_term, False), stacked(output_term, True), stacked(heads_term, True)],
+        (True, False, True, True),
+        jnp.stack([gain_one_term, gain_two_term], axis=0),
+        2,
+    )
+    heads_grad, output_grad, down_grad = heads_grad.T, output_grad.T, down_grad.T
     gains_new, gains_first_new, gains_second_new = adamw(
         norm_gains, gains_grad, gains_first, gains_second, gain_rate, 0.0
     )
@@ -335,7 +799,7 @@
 
 def solution(mesh):
     return jax.shard_map(
-        local,
+        functools.partial(local, Grid(mesh)),
         mesh=mesh,
         in_specs=(
             P(("dp", "shard"), None),

time: 1200 us -> 681 us (0.57)
  waiting for transfers between devices: 811 us -> 29.3 us
  Pallas kernels: 0 us -> 240 us
  local copies, waits for them, and re-layouts: 18.6 us -> 128 us
  blocking collectives: 64.3 us -> 0 us
  matrix products: 253 us -> 236 us
    reduce_scatter x6 -> x0, waiting for transfers between devices: 342 us -> none  [the longest x1 131 us: local(): lax.psum_scatter(expand_term, 'dp', scatter_dimension=1, tiled=True)]
    all_gather x6 -> x0, waiting for transfers between devices: 313 us -> none  [the longest x1 138 us: local(): lax.all_gather(sectioned[2], 'shard', axis=0, tiled=True)]
    pallas_call x0 -> x2, Pallas kernels: none -> 240 us  [the longest x1 121 us: reduce_grads(): pl.pallas_call(functools.partial(reduce_kernel, grid, tuple(z_majors), sh...]
    reshape x0 -> x9, local copies, waits for them, and re-layouts: none -> 54.7 us  [the longest x7 45.9 us: stacked(): term = term.astype(jnp.bfloat16).reshape(grid.nz, rows, grid.nd, cols)]
    reduce_scatter x1, waiting for transfers between devices: 61.8 us -> 12 us  [local(): lax.psum_scatter(packed_terms, 'shard', scatter_dimension=0, tiled=True)]
    psum x1 -> x0, blocking collectives: 39.8 us -> none  [local(): lax.psum(jnp.stack([gain_one_term, gain_two_term], axis=0), ('dp', 'shard'))]
    all_gather x1, waiting for transfers between devices: 55.6 us -> 17.3 us  [local(): all_keys = lax.all_gather(packed, 'shard', axis=0, tiled=True)]
    unnamed x18 -> x2, waiting for transfers between devices: 38.1 us -> 0.03 us
  transfers between devices with their start and end apart: 16 -> 2, of which waited for: 14 -> 2; matrix products, arithmetic and copies ran while one was open for 15% -> 18% of each run, Pallas kernels for 0% -> 0%
where the time goes in v1:
time: 681 us; the launch traced here: 673 us
  Pallas kernels  240 us (35%)
  matrix products  236 us (35%)
  local copies, waits for them, and re-layouts  128 us (19%)
  waiting for transfers between devices  29.3 us (4%)
  other arithmetic  24 us (4%)
  between operations  15.5 us (2%)
    pallas_call x1, Pallas kernels, reduce_grads(): pl.pallas_call(functools.partial(reduce_kernel, grid, tuple(z_majors), sh...  121 us
    pallas_call x1, Pallas kernels, gather_weights(): pl.pallas_call(functools.partial(gather_kernel, grid, tuple(z_majors)), o...  119 us
    reshape x7, local copies, waits for them, and re-layouts, stacked(): term = term.astype(jnp.bfloat16).reshape(grid.nz, rows, grid.nd, cols)  45.9 us
    dot_general x5, matrix products, attend_forward(): jnp.einsum('qhd,kd->hqk', query_group, key_group, preferred_element_type=...  43.1 us
    unnamed x188, local copies, waits for them, and re-layouts  36 us
    dot_general x5, matrix products, attend_backward(): jnp.einsum('qhd,kd->hqk', grad_group, value_group, preferred_element_type...  36 us
    dot_general x5, matrix products, attend_forward(): jnp.einsum('hqk,kd->qhd', probs, value_group, preferred_element_type=jnp....  32.3 us
    dot_general x5, matrix products, attend_backward(): jnp.einsum('hqk,qhd->kd', probs_half, grad_group, preferred_element_type=...  31.1 us
  transfers between devices with their start and end apart: 2, of which 2 were waited for; matrix products, arithmetic and copies ran while one was open for 18% of the time, Pallas kernels for 0%

profile of v1, /device:TPU:0, one launch (start us, length us, event | category | flops | bytes accessed | tf_op | source)
XLA Modules:
  0.0 673.3 jit_solution(18081182238046947685)
XLA Ops:
  16.8 118.8 %gather_weights.1 = (bf16[4,8,200,240]{3,2,1,0:T(8,128)(2,1)}, bf16[4,8,120,240]{3,2,1,0:T(8,128)(2,1)}, bf16[8,4,240,640]{3,2,1,0:T(8,128)(2,1)}, bf16[4,8,120,640]{3,2,1,0:T(8,128)(2,1)}) custom-call(bf16[200,240]{1,0:T(8,128)(2,1)} %convert_bitcast_fusion.1.refs_0_, bf16[120,240]{1,0:T(8,128)(2,1)} %convert_bitcast_fusion.2.refs_1_, ...), custom_call_target="tpu_custom_call" | custom-call | tf_op jit(solution)/shard_map/gather_weights/pallas_call | solution.py:195
  135.7 4.5 copy.76
  140.1 4.2 reshape.270
  144.4 4.1 fusion.134
  154.1 4.2 copy.82
  158.3 4.6 reshape.273
  162.9 6.2 copy.84
  172.1 13.1 %copy.83 = bf16[4,240,8,640]{3,2,1,0:T(8,128)(2,1)} copy(bf16[4,240,8,640]{3,1,0,2:T(8,128)(2,1)} %bitcast.428) | data formatting | bytes 19660800 | tf_op jit(solution)/shard_map/transpose | solution.py:667
  185.3 10.5 %copy.136 = bf16[120,8,8,640]{3,1,2,0:T(8,128)(2,1)} copy(bf16[120,8,8,640]{3,2,1,0:T(8,128)(2,1)} %bitcast.410) | data formatting | bytes 19660800
  197.1 17.3 %all-gather.2.cloned.1.call-done = bf16[2048,640]{0,1:T(8,128)(2,1)} async-done(((bf16[512,640]{0,1:T(8,128)(2,1)}), bf16[2048,640]{0,1:T(8,128)(2,1)}) %all-gather.2.cloned.1.call-update) | async-done | bytes 2621456 | tf_op jit(solution)/shard_map/all_gather | solution.py:695
  217.4 6.9 %fusion.139 = f32[2048,512,3]{1,0,2:T(8,128)} fusion(bf16[2048,640]{0,1:T(8,128)(2,1)S(1)} %copy-done.20, bf16[512,15,32]{0,2,1:T(8,128)(2,1)S(1)} %get-tuple-element.114, bf16[512,15,32]{0,2,1:T(8,128)(2,1)S(1)} %get-tuple-element.113), kind=kOutput, calls=%fused_computation.205 | convolution fusion | flops 403046400 | bytes 13828096 | tf_op jit(solution)/shard_map/qhd,kd->hqk/dot_general | solution.py:567
  224.3 6.4 fusion.138
  230.7 6.4 fusion.137
  237.1 20.5 %fusion.34 = (f32[3,512]{1,0:T(4,128)S(1)}, f32[3,512]{1,0:T(4,128)S(1)}, f32[3,512]{1,0:T(4,128)S(1)}, f32[3,512]{1,0:T(4,128)S(1)}, f32[3,512]{1,0:T(4,128)S(1)}, /*index=5*/f32[2048,512,3]{1,0,2:T(8,128)}) fusion(pred[512,2048]{0,1:T(8,128)(4,1)S(1)} %fusion.65, f32[2048,512,3]{1,0,2:T(8,128)} %fusion.138, f32[2048,512,3]{1,0,2:T(8,128)} %fusion.139, ...), kind=kOutput, calls=%fused_computation.54 | convolution fusion | flops 449831424 | bytes 64452608 | tf_op jit(solution)/shard_map/qhd,kd->hqk/dot_general | solution.py:567
  259.4 6.7 %fusion.127 = bf16[512,15,64]{0,2,1:T(8,128)(2,1)S(1)} fusion(f32[2048,512,3]{1,0,2:T(8,128)} %fusion.137, f32[3,512]{1,0:T(4,128)S(1)} %get-tuple-element.92, pred[512,2048]{0,1:T(8,128)(4,1)S(1)} %fusion.65, bf16[2048,640]{0,1:T(8,128)(2,1)S(1)} %copy-done.20), kind=kOutput, calls=%fused_computation.162 | convolution fusion | flops 415236096 | bytes 14295040 | tf_op jit(solution)/shard_map/hqk,kd->qhd/dot_general | solution.py:574
  266.2 8.2 %fusion.125 = bf16[512,15,64]{0,2,1:T(8,128)(2,1)S(1)} fusion(bf16[512,15,64]{0,2,1:T(8,128)(2,1)S(1)} %fusion.127, f32[2048,512,3]{1,0,2:T(8,128)} %fusion.138, f32[3,512]{1,0:T(4,128)S(1)} %get-tuple-element.89, pred[512,2048]{0,1:T(8,128)(4,1)S(1)} %fusion.65, bf16[2048,640]{0,1:T(8,128)(2,1)} %all-gather.2.cloned.1.call-done), kind=kOutput, calls=%fused_computation.160 | convolution fusion | flops 415236096 | bytes 14295040 | tf_op jit(solution)/shard_map/hqk,kd->qhd/dot_general | solution.py:574
  274.4 4.4 fusion.123
  278.9 4.8 fusion.121
  283.7 8.2 %fusion.119 = bf16[512,15,64]{0,2,1:T(8,128)(2,1)S(1)} fusion(bf16[512,15,64]{0,2,1:T(8,128)(2,1)S(1)} %fusion.121, f32[2048,512,3]{1,0,2:T(8,128)} %get-tuple-element.128, f32[3,512]{1,0:T(4,128)S(1)} %get-tuple-element.88, pred[512,2048]{0,1:T(8,128)(4,1)S(1)} %fusion.65, bf16[2048,640]{0,1:T(8,128)(2,1)} %all-gather.2.cloned.1.call-done), kind=kOutput, calls=%fused_computation.154 | convolution fusion | flops 415236096 | bytes 14295040 | tf_op jit(solution)/shard_map/hqk,kd->qhd/dot_general | solution.py:574
  295.3 5.8 fusion.190
  301.2 10.0 %fusion.62 = (bf16[512,2560]{1,0:T(8,128)(2,1)}, bf16[512,2560]{1,0:T(8,128)(2,1)}, bf16[512,2560]{1,0:T(8,128)(2,1)}) fusion(f32[512,5120]{1,0:T(8,128)S(1)} %fusion.190, bf16[2560,960]{0,1:T(8,128)(2,1)} %bitcast.432, bf16[512,960]{0,1:T(8,128)(2,1)S(1)} %copy-done.29), kind=kOutput, calls=%fused_computation.82 | convolution fusion | flops 2536243200 | bytes 24248320 | tf_op jit(solution)/shard_map/dot_general | solution.py:531
  311.2 8.9 %multiply_reduce_fusion = (f32[960]{0:T(1024)}, f32[512]{0:T(512)S(1)}, f32[512,960]{0,1:T(8,128)S(1)}) fusion(f32[512,960]{0,1:T(8,128)S(1)} %get-tuple-element.130, f32[512]{0:T(512)S(1)} %add_rsqrt_fusion, f32[960]{0:T(1024)S(1)} %bitcast.461, bf16[960,5120]{1,0:T(8,128)(2,1)S(1)} %bitcast.408, bf16[512,2560]{1,0:T(8,128)(2,1)} %get-tuple-element.109, ...), kind=kOutput, calls=%fused_computation.125 | convolution fusion | flops 5046598144 | bytes 19017216 | tf_op jit(solution)/shard_map/dot_general | solution.py:531
  322.9 8.0 %fusion.14 = bf16[3,512,2048]{1,2,0:T(8,128)(2,1)S(1)} fusion(f32[2048,512,3]{1,0,2:T(8,128)} %fusion.137, f32[3,512]{1,0:T(4,128)S(1)} %get-tuple-element.123, f32[3,512]{1,0:T(4,128)S(1)} %log.35, pred[512,2048]{0,1:T(8,128)(4,1)S(1)} %fusion.65, bf16[2048,640]{0,1:T(8,128)(2,1)} %all-gather.2.cloned.1.call-done, bf16[512,15,64]{0,2,1:T(8,128)(2,1)S(1)} %bitcast.444), kind=kOutput, calls=%fused_computation.19 | convolution fusion | flops 424673280 | bytes 20398080 | tf_op jit(solution)/shard_map/qhd,kd->hqk/dot_general | solution.py:606
  333.7 5.9 fusion.11
  342.5 8.5 %fusion.8 = bf16[3,512,2048]{1,2,0:T(8,128)(2,1)S(1)} fusion(f32[2048,512,3]{1,0,2:T(8,128)} %fusion.139, f32[3,512]{1,0:T(4,128)S(1)} %get-tuple-element.121, f32[3,512]{1,0:T(4,128)S(1)} %copy-done.61, pred[512,2048]{0,1:T(8,128)(4,1)S(1)} %fusion.65, bf16[2048,640]{0,1:T(8,128)(2,1)} %all-gather.2.cloned.1.call-done, bf16[512,15,64]{0,2,1:T(8,128)(2,1)} %bitcast.446), kind=kOutput, calls=%fused_computation.11 | convolution fusion | flops 424673280 | bytes 20393984 | tf_op jit(solution)/shard_map/qhd,kd->hqk/dot_general | solution.py:606
  353.9 5.7 fusion.5
  362.5 7.9 %fusion.2 = bf16[3,512,2048]{1,2,0:T(8,128)(2,1)S(1)} fusion(f32[2048,512,3]{1,0,2:T(8,128)} %get-tuple-element.128, f32[3,512]{1,0:T(4,128)S(1)} %get-tuple-element.119, f32[3,512]{1,0:T(4,128)S(1)} %copy-done.59, pred[512,2048]{0,1:T(8,128)(4,1)S(1)} %fusion.65, bf16[2048,640]{0,1:T(8,128)(2,1)} %all-gather.2.cloned.1.call-done, ...), kind=kOutput, calls=%fused_computation.3 | convolution fusion | flops 424673280 | bytes 20393984 | tf_op jit(solution)/shard_map/qhd,kd->hqk/dot_general | solution.py:606
  370.4 4.0 fusion.101
  374.5 6.9 %fusion.74 = f32[2048,640]{0,1:T(8,128)} fusion(f32[2048,640]{0,1:T(8,128)} %fusion.101, f32[2048,512,3]{1,0,2:T(8,128)} %fusion.137, f32[3,512]{1,0:T(4,128)S(1)} %log.35, pred[512,2048]{0,1:T(8,128)(4,1)S(1)} %fusion.65, bf16[512,15,64]{0,2,1:T(8,128)(2,1)S(1)} %bitcast.449), kind=kOutput, calls=%fused_computation.99 | convolution fusion | flops 415236096 | bytes 14360576 | tf_op jit(solution)/shard_map/hqk,qhd->kd/dot_general | solution.py:621
  381.4 6.9 %fusion.80 = f32[2048,640]{0,1:T(8,128)} fusion(f32[2048,640]{0,1:T(8,128)} %fusion.74, f32[2048,512,3]{1,0,2:T(8,128)} %fusion.138, f32[3,512]{1,0:T(4,128)S(1)} %log.36, pred[512,2048]{0,1:T(8,128)(4,1)S(1)} %fusion.65, bf16[512,15,64]{0,2,1:T(8,128)(2,1)S(1)} %bitcast.450), kind=kOutput, calls=%fused_computation.101 | convolution fusion | flops 415236096 | bytes 14360576 | tf_op jit(solution)/shard_map/hqk,qhd->kd/dot_general | solution.py:621
  388.3 6.9 %fusion.86 = f32[2048,640]{0,1:T(8,128)} fusion(f32[2048,640]{0,1:T(8,128)} %fusion.80, f32[2048,512,3]{1,0,2:T(8,128)} %fusion.139, f32[3,512]{1,0:T(4,128)S(1)} %copy-done.61, pred[512,2048]{0,1:T(8,128)(4,1)S(1)} %fusion.65, bf16[512,15,64]{0,2,1:T(8,128)(2,1)S(1)} %bitcast.451), kind=kOutput, calls=%fused_computation.103 | convolution fusion | flops 415236096 | bytes 14360576 | tf_op jit(solution)/shard_map/hqk,qhd->kd/dot_general | solution.py:621
  398.7 6.9 %fusion.98 = f32[2048,640]{0,1:T(8,128)} fusion(f32[2048,640]{0,1:T(8,128)} %fusion.92, f32[2048,512,3]{1,0,2:T(8,128)} %get-tuple-element.128, f32[3,512]{1,0:T(4,128)S(1)} %copy-done.59, pred[512,2048]{0,1:T(8,128)(4,1)S(1)} %fusion.65, bf16[512,15,64]{0,2,1:T(8,128)(2,1)S(1)} %bitcast.453), kind=kOutput, calls=%fused_computation.107 | convolution fusion | flops 415236096 | bytes 14360576 | tf_op jit(solution)/shard_map/hqk,qhd->kd/dot_general | solution.py:621
  410.5 4.3 reshape.284
  417.3 6.1 convolution_convert_fusion.1
  423.5 9.3 %reshape.280 = bf16[4,640,8,120]{1,0,3,2:T(4,128)(2,1)} reshape(bf16[2560,960]{0,1:T(8,128)(2,1)} %convolution_convert_fusion.1) | data formatting | bytes 9830400 | tf_op jit(solution)/shard_map/reshape | solution.py:748
  432.8 5.4 copy.101
  438.8 8.2 %convolution_convert_fusion = bf16[960,5120]{1,0:T(8,128)(2,1)} fusion(bf16[512,2560]{1,0:T(8,128)(2,1)S(1)} %copy-done.66, bf16[512,2560]{1,0:T(8,128)(2,1)S(1)} %copy-done.65, f32[512,960]{0,1:T(8,128)S(1)} %copy-done.11, f32[960]{0:T(1024)S(1)} %bitcast.463, f32[512]{0:T(512)S(1)} %add_rsqrt_fusion), kind=kOutput, calls=%fused_computation.60 | convolution fusion | flops 5050040320 | bytes 17045248 | tf_op jit(solution)/shard_map/dot_general | solution.py:537
  447.0 9.8 %copy.138 = bf16[120,8,8,640]{3,2,1,0:T(8,128)(2,1)} copy(bf16[120,8,8,640]{3,1,2,0:T(8,128)(2,1)} %bitcast.429) | data formatting | bytes 19660800
  456.8 8.9 %copy.102 = bf16[4,240,8,640]{3,1,0,2:T(8,128)(2,1)} copy(bf16[4,240,8,640]{3,2,1,0:T(8,128)(2,1)} %bitcast.411) | data formatting | bytes 19660800 | tf_op jit(solution)/shard_map/reshape | solution.py:748
  465.7 4.3 fusion.117
  470.0 4.2 fusion.116
  486.4 12.0 %reduce-scatter.2.cloned.1.call-done = f32[512,640]{0,1:T(8,128)} async-done(((f32[2048,640]{0,1:T(8,128)}), f32[512,640]{0,1:T(8,128)}) %reduce-scatter.2.cloned.1.call-update) | async-done | bytes 1310736 | tf_op jit(solution)/shard_map/reduce_scatter | solution.py:730
  500.8 5.7 fusion.111
  506.6 3.9 convolution_convert_fusion.2
  510.5 9.2 %reshape.308 = bf16[4,240,8,200]{3,2,1,0:T(8,128)(2,1)} reshape(bf16[960,1600]{1,0:T(8,128)(2,1)} %convolution_convert_fusion.2) | data formatting | bytes 6144000 | tf_op jit(solution)/shard_map/reshape | solution.py:748
  519.7 6.1 copy.135
  528.7 121.5 %reduce_grads.1 = (f32[120,640]{1,0:T(8,128)}, f32[240,640]{1,0:T(8,128)}, f32[120,240]{1,0:T(8,128)}, f32[200,240]{1,0:T(8,128)}, f32[2,960]{1,0:T(2,128)}) custom-call(bf16[4,2,2,2,120,640]{5,4,3,2,1,0:T(8,128)(2,1)} %bitcast.424, bf16[2,2,2,4,240,640]{5,4,3,2,1,0:T(8,128)(2,1)} %bitcast.409, bf16[4,2,2,2,120,240]{5,4,3,2,1,0:T(8,128)(2,1)} %bitcast.430, ...), custom_call_target="tpu_custom_call" | custom-call | tf_op jit(solution)/shard_map/reduce_grads/pallas_call | solution.py:450
  655.4 3.7 fusion.110
  (258 shorter events, 82.9 us)
Async XLA Ops:
  7.2 207.2 %all-gather.2.cloned.1.call-start = ((), (), s32[]{:S(2)}) async-start(), calls=%async_computation.1 | async-start | bytes 3276800 | tf_op jit(solution)/shard_map/all_gather | solution.py:695
  8.7 135.7 %copy-start.55 = (f32[512]{0:T(512)}, f32[512]{0:T(512)S(1)}, u32[]{:S(2)}) copy-start(f32[512]{0:T(512)S(1)} %add_rsqrt_fusion.1) | copy-start | bytes 6148
  10.1 134.3 %copy-start.52 = (f32[1,960]{1,0:T(1,128)}, f32[1,960]{1,0:T(1,128)S(1)}, u32[]{:S(2)}) copy-start(f32[1,960]{1,0:T(1,128)S(1)} %get-tuple-element.125) | copy-start | bytes 11524
  12.7 123.0 %copy-start.28 = (f32[240,120]{0,1:T(8,128)}, f32[240,120]{0,1:T(8,128)S(1)}, u32[]{:S(2)}) copy-start(f32[240,120]{0,1:T(8,128)S(1)} %copy.75) | copy-start | bytes 345604
  148.5 9.7 %copy-start.12 = (f32[512,1600]{0,1:T(8,128)}, f32[512,1600]{0,1:T(8,128)S(1)}, u32[]{:S(2)}) copy-start(f32[512,1600]{0,1:T(8,128)S(1)} %fusion.134) | copy-start | bytes 9830404
  150.9 44.9 %copy-start.22 = (f32[512,32]{0,1:T(8,128)}, f32[512,32]{0,1:T(8,128)S(1)}, u32[]{:S(2)}) copy-start(f32[512,32]{0,1:T(8,128)S(1)} %get-tuple-element.126) | copy-start | bytes 196612
  150.9 44.9 %copy-start.24 = (f32[512,32]{0,1:T(8,128)}, f32[512,32]{0,1:T(8,128)S(1)}, u32[]{:S(2)}) copy-start(f32[512,32]{0,1:T(8,128)S(1)} %get-tuple-element.127) | copy-start | bytes 196612
  154.0 344.4 %reduce-scatter.2.cloned.1.call-start = ((), (), s32[]{:S(2)}) async-start(), calls=%async_computation.2 | async-start | bytes 6553600 | tf_op jit(solution)/shard_map/reduce_scatter | solution.py:730
  185.3 10.5 %copy-start.54 = (s32[1,2048]{1,0:T(1,128)S(1)}, s32[1,2048]{1,0:T(1,128)}, u32[]{:S(2)}) copy-start(s32[1,2048]{1,0:T(1,128)} %param.21) | copy-start | bytes 24580
  185.3 10.5 %slice-start.18 = ((f32[512,1600]{0,1:T(8,128)}), f32[512,960]{0,1:T(8,128)S(1)}, s32[]{:S(2)}) async-start(f32[512,1600]{0,1:T(8,128)} %copy-done.12), calls=%async_computation.21 | async-start | bytes 3932160 | tf_op jit(solution)/shard_map/slice | solution.py:682
  196.1 34.5 %copy-start = (bf16[512,15,32]{0,2,1:T(8,128)(2,1)}, bf16[512,15,32]{0,2,1:T(8,128)(2,1)S(1)}, u32[]{:S(2)}) copy-start(bf16[512,15,32]{0,2,1:T(8,128)(2,1)S(1)} %get-tuple-element.113) | copy-start | bytes 1474564
  196.1 34.5 %copy-start.2 = (bf16[512,15,32]{0,2,1:T(8,128)(2,1)}, bf16[512,15,32]{0,2,1:T(8,128)(2,1)S(1)}, u32[]{:S(2)}) copy-start(bf16[512,15,32]{0,2,1:T(8,128)(2,1)S(1)} %get-tuple-element.114) | copy-start | bytes 1474564
  196.2 40.9 %copy-start.40 = (bf16[512,3,64]{0,2,1:T(8,128)(2,1)}, bf16[512,3,64]{0,2,1:T(8,128)(2,1)S(1)}, u32[]{:S(2)}) copy-start(bf16[512,3,64]{0,2,1:T(8,128)(2,1)S(1)} %pad_maximum_fusion.10) | copy-start | bytes 589828
  217.4 61.4 %copy-start.9 = (f32[2048,512,3]{1,0,2:T(8,128)}, f32[2048,512,3]{1,0,2:T(8,128)S(1)}, u32[]{:S(2)}) copy-start(f32[2048,512,3]{1,0,2:T(8,128)S(1)} %fusion.140) | copy-start | bytes 37748740
  259.4 14.9 %slice-start.12 = ((s8[12582912]{0:T(1024)(128)(4,1)}), s8[4194304]{0:T(1024)(128)(4,1)S(1)}, s32[]{:S(2)}) async-start(s8[12582912]{0:T(1024)(128)(4,1)} %bitcast.420), calls=%async_computation.15 | async-start | bytes 8388608
  259.4 14.9 %slice-start.13 = ((s8[12582912]{0:T(1024)(128)(4,1)}), s8[4194304]{0:T(1024)(128)(4,1)S(1)}, s32[]{:S(2)}) async-start(s8[12582912]{0:T(1024)(128)(4,1)} %bitcast.420), calls=%async_computation.16 | async-start | bytes 8388608
  278.8 16.5 %slice-start = ((s8[9830400]{0:T(1024)(128)(4,1)}), s8[4194304]{0:T(1024)(128)(4,1)S(1)}, s32[]{:S(2)}) async-start(s8[9830400]{0:T(1024)(128)(4,1)} %bitcast.405), calls=%async_computation.3 | async-start | bytes 8388608
  278.8 16.5 %slice-start.1 = ((s8[9830400]{0:T(1024)(128)(4,1)}), s8[4194304]{0:T(1024)(128)(4,1)S(1)}, s32[]{:S(2)}) async-start(s8[9830400]{0:T(1024)(128)(4,1)} %bitcast.405), calls=%async_computation.4 | async-start | bytes 8388608
  283.6 9.2 %copy-start.16 = (bf16[512,960]{0,1:T(8,128)(2,1)S(1)}, bf16[512,960]{0,1:T(8,128)(2,1)}, u32[]{:S(2)}) copy-start(bf16[512,960]{0,1:T(8,128)(2,1)} %param.19) | copy-start | bytes 2949124
  283.7 9.1 %copy-start.21 = (bf16[960,960]{1,0:T(8,128)(2,1)S(1)}, bf16[960,960]{1,0:T(8,128)(2,1)}, u32[]{:S(2)}) copy-start(bf16[960,960]{1,0:T(8,128)(2,1)} %reshape.273) | copy-start | bytes 5529604
  283.7 11.6 %slice-start.2 = ((s8[9830400]{0:T(1024)(128)(4,1)}), s8[1441792]{0:T(1024)(128)(4,1)S(1)}, s32[]{:S(2)}) async-start(s8[9830400]{0:T(1024)(128)(4,1)} %bitcast.405), calls=%async_computation.5 | async-start | bytes 2883584
  295.3 24.8 %copy-start.10 = (f32[512,960]{0,1:T(8,128)}, f32[512,960]{0,1:T(8,128)S(1)}, u32[]{:S(2)}) copy-start(f32[512,960]{0,1:T(8,128)S(1)} %get-tuple-element.130) | copy-start | bytes 5898244
  311.2 8.9 %copy-start.30 = (bf16[512,960]{0,1:T(8,128)(2,1)S(1)}, bf16[512,960]{0,1:T(8,128)(2,1)}, u32[]{:S(2)}) copy-start(bf16[512,960]{0,1:T(8,128)(2,1)} %param.20) | copy-start | bytes 2949124
  320.6 13.1 %slice-start.15 = ((s8[12582912]{0:T(1024)(128)(4,1)}), s8[4194304]{0:T(1024)(128)(4,1)S(1)}, s32[]{:S(2)}) async-start(s8[12582912]{0:T(1024)(128)(4,1)} %bitcast.422), calls=%async_computation.18 | async-start | bytes 8388608
  321.9 8.9 %copy-start.32 = (bf16[512,960]{0,1:T(8,128)(2,1)}, bf16[512,960]{0,1:T(8,128)(2,1)S(1)}, u32[]{:S(2)}) copy-start(bf16[512,960]{0,1:T(8,128)(2,1)S(1)} %convolution_convert_fusion.4) | copy-start | bytes 2949124
  322.9 10.8 %slice-start.16 = ((s8[12582912]{0:T(1024)(128)(4,1)}), s8[4194304]{0:T(1024)(128)(4,1)S(1)}, s32[]{:S(2)}) async-start(s8[12582912]{0:T(1024)(128)(4,1)} %bitcast.422), calls=%async_computation.19 | async-start | bytes 8388608
  322.9 10.8 %slice-start.17 = ((s8[12582912]{0:T(1024)(128)(4,1)}), s8[4194304]{0:T(1024)(128)(4,1)S(1)}, s32[]{:S(2)}) async-start(s8[12582912]{0:T(1024)(128)(4,1)} %bitcast.422), calls=%async_computation.20 | async-start | bytes 8388608
  330.9 8.7 %copy-start.4 = (bf16[3,512,2048]{1,2,0:T(8,128)(2,1)}, bf16[3,512,2048]{1,2,0:T(8,128)(2,1)S(1)}, u32[]{:S(2)}) copy-start(bf16[3,512,2048]{1,2,0:T(8,128)(2,1)S(1)} %fusion.14) | copy-start | bytes 18874372
  339.6 11.3 %copy-start.5 = (bf16[3,512,2048]{1,2,0:T(8,128)(2,1)}, bf16[3,512,2048]{1,2,0:T(8,128)(2,1)S(1)}, u32[]{:S(2)}) copy-start(bf16[3,512,2048]{1,2,0:T(8,128)(2,1)S(1)} %fusion.11) | copy-start | bytes 18874372
  339.6 14.2 %slice-start.9 = ((s8[12582912]{0:T(1024)(128)(4,1)}), s8[4194304]{0:T(1024)(128)(4,1)S(1)}, s32[]{:S(2)}) async-start(s8[12582912]{0:T(1024)(128)(4,1)} %bitcast.418), calls=%async_computation.12 | async-start | bytes 8388608
  342.5 11.4 %slice-start.10 = ((s8[12582912]{0:T(1024)(128)(4,1)}), s8[4194304]{0:T(1024)(128)(4,1)S(1)}, s32[]{:S(2)}) async-start(s8[12582912]{0:T(1024)(128)(4,1)} %bitcast.418), calls=%async_computation.13 | async-start | bytes 8388608
  342.5 11.4 %slice-start.11 = ((s8[12582912]{0:T(1024)(128)(4,1)}), s8[4194304]{0:T(1024)(128)(4,1)S(1)}, s32[]{:S(2)}) async-start(s8[12582912]{0:T(1024)(128)(4,1)} %bitcast.418), calls=%async_computation.14 | async-start | bytes 8388608
  350.9 8.7 %copy-start.6 = (bf16[3,512,2048]{1,2,0:T(8,128)(2,1)}, bf16[3,512,2048]{1,2,0:T(8,128)(2,1)S(1)}, u32[]{:S(2)}) copy-start(bf16[3,512,2048]{1,2,0:T(8,128)(2,1)S(1)} %fusion.8) | copy-start | bytes 18874372
  359.6 10.8 %copy-start.7 = (bf16[3,512,2048]{1,2,0:T(8,128)(2,1)}, bf16[3,512,2048]{1,2,0:T(8,128)(2,1)S(1)}, u32[]{:S(2)}) copy-start(bf16[3,512,2048]{1,2,0:T(8,128)(2,1)S(1)} %fusion.5) | copy-start | bytes 18874372
  370.4 11.0 %copy-start.8 = (bf16[3,512,2048]{1,2,0:T(8,128)(2,1)}, bf16[3,512,2048]{1,2,0:T(8,128)(2,1)S(1)}, u32[]{:S(2)}) copy-start(bf16[3,512,2048]{1,2,0:T(8,128)(2,1)S(1)} %fusion.2) | copy-start | bytes 18874372
  465.7 8.5 %slice-start.3 = ((s8[6291456]{0:T(1024)(128)(4,1)}), s8[4194304]{0:T(1024)(128)(4,1)S(1)}, s32[]{:S(2)}) async-start(s8[6291456]{0:T(1024)(128)(4,1)} %bitcast.412), calls=%async_computation.6 | async-start | bytes 8388608
  482.7 18.1 %copy-start.17 = (bf16[512,960]{0,1:T(8,128)(2,1)S(1)}, bf16[512,960]{0,1:T(8,128)(2,1)}, u32[]{:S(2)}) copy-start(bf16[512,960]{0,1:T(8,128)(2,1)} %param.19) | copy-start | bytes 2949124
  482.7 18.1 %copy-start.53 = (f32[1,960]{1,0:T(1,128)S(1)}, f32[1,960]{1,0:T(1,128)}, u32[]{:S(2)}) copy-start(f32[1,960]{1,0:T(1,128)} %copy-done.52) | copy-start | bytes 11524
  482.7 18.1 %copy-start.56 = (f32[512]{0:T(512)S(1)}, f32[512]{0:T(512)}, u32[]{:S(2)}) copy-start(f32[512]{0:T(512)} %copy-done.55) | copy-start | bytes 6148
  528.6 126.8 %copy-start.15 = (f32[512,960]{0,1:T(8,128)S(1)}, f32[512,960]{0,1:T(8,128)}, u32[]{:S(2)}) copy-start(f32[512,960]{0,1:T(8,128)} %copy-done.13) | copy-start | bytes 5898244
  650.1 9.1 %copy-start.50 = (f32[2,960]{1,0:T(2,128)S(1)}, f32[2,960]{1,0:T(2,128)}, u32[]{:S(2)}) copy-start(f32[2,960]{1,0:T(2,128)} %param.23) | copy-start | bytes 23044
  650.1 9.1 %copy-start.51 = (f32[2,960]{1,0:T(2,128)S(1)}, f32[2,960]{1,0:T(2,128)}, u32[]{:S(2)}) copy-start(f32[2,960]{1,0:T(2,128)} %get-tuple-element.157) | copy-start | bytes 23044
  650.2 9.1 %copy-start.57 = (f32[2,960]{1,0:T(2,128)S(1)}, f32[2,960]{1,0:T(2,128)}, u32[]{:S(2)}) copy-start(f32[2,960]{1,0:T(2,128)} %param.28) | copy-start | bytes 23044
  650.2 9.0 %copy-start.58 = (f32[2,960]{1,0:T(2,128)S(1)}, f32[2,960]{1,0:T(2,128)}, u32[]{:S(2)}) copy-start(f32[2,960]{1,0:T(2,128)} %param.29) | copy-start | bytes 23044
  650.2 9.7 %copy-start.38 = (f32[240,200]{0,1:T(8,128)S(1)}, f32[240,200]{0,1:T(8,128)}, u32[]{:S(2)}) copy-start(f32[240,200]{0,1:T(8,128)} %param.24) | copy-start | bytes 576004
  650.2 9.7 %copy-start.39 = (f32[200,240]{1,0:T(8,128)S(1)}, f32[200,240]{1,0:T(8,128)}, u32[]{:S(2)}) copy-start(f32[200,240]{1,0:T(8,128)} %get-tuple-element.36) | copy-start | bytes 576004
  650.2 10.6 %copy-start.26 = (f32[640,120]{0,1:T(8,128)S(1)}, f32[640,120]{0,1:T(8,128)}, u32[]{:S(2)}) copy-start(f32[640,120]{0,1:T(8,128)} %param.27) | copy-start | bytes 921604
  650.2 10.6 %copy-start.27 = (f32[120,640]{1,0:T(8,128)S(1)}, f32[120,640]{1,0:T(8,128)}, u32[]{:S(2)}) copy-start(f32[120,640]{1,0:T(8,128)} %get-tuple-element.39) | copy-start | bytes 921604
  (42 other events, 190.1 us)
Sparse Core Ops, SparseCore 0:
  154.1 60.2 all-gather.1
  405.8 92.5 reduce-scatter.1

commit v2 on v1

--- a/solution.py
+++ b/solution.py
@@ -460,12 +460,17 @@
     )(*split, *([value] if shared else []))
 
 
+D = 960
 QUERY_HEADS = 15
 KEY_VALUE_HEADS = 5
-HEAD_SIZE = 64
+GROUP = QUERY_HEADS // KEY_VALUE_HEADS
+HEAD = 64
 FF = 2560
+QKV = (QUERY_HEADS + 2 * KEY_VALUE_HEADS) * HEAD
 ADAM_STEP = 10
-
+DOCS = 16
+HIDE = -1e30
+VALUE_SCALE = 2.0**-9
 
 norm_epsilon = 1e-05
 beta_one = 0.9
@@ -476,67 +481,666 @@
 gain_rate = 0.5
 decay_rate = 0.1
 
-
-def rotary_tables(relative):
-    half_width = HEAD_SIZE // 2
-    freq_table = jnp.power(10000.0, -jnp.arange(half_width).astype(jnp.float32) / half_width)
-    angle_table = relative.astype(jnp.float32)[:, None] * freq_table[None, :]
-    return (jnp.cos(angle_table), jnp.sin(angle_table))
-
-
-def apply_rotary(values, cosine_table, sine_table):
-    half_width = HEAD_SIZE // 2
-    first_half = values[..., :half_width]
-    second_half = values[..., half_width:]
-    cos_part = cosine_table[:, None, :]
-    sin_part = sine_table[:, None, :]
-    return jnp.concatenate(
-        [
-            first_half * cos_part - second_half * sin_part,
-            second_half * cos_part + first_half * sin_part,
+f32 = jnp.float32
+bf16 = jnp.bfloat16
+DEPTH = 4
+SLICE = D // DEPTH
+
+
+def mm(a, b):
+    return lax.dot_general(a, b, (((1,), (0,)), ((), ())), preferred_element_type=f32)
+
+
+def mm_nt(a, b):
+    return lax.dot_general(a, b, (((1,), (1,)), ((), ())), preferred_element_type=f32)
+
+
+def mm_tn(a, b):
+    return lax.dot_general(a, b, (((0,), (0,)), ((), ())), preferred_element_type=f32)
+
+
+def lanes_below(shape, n):
+    return lax.broadcasted_iota(jnp.int32, shape, len(shape) - 1) < n
+
+
+def inverse_rms(ref):
+    total = jnp.zeros((1, ref.shape[1]), f32)
+    for k in range(DEPTH):
+        x = ref[pl.ds(k * SLICE, SLICE)].astype(f32)
+        total += jnp.sum(x * x, axis=0, keepdims=True)
+    return lax.rsqrt(total * (1.0 / D) + norm_epsilon)
+
+
+def three_pieces(row):
+    hi = row.astype(bf16).astype(f32)
+    mid = (row - hi).astype(bf16).astype(f32)
+    low = row - hi - mid
+    place = lax.broadcasted_iota(jnp.int32, (16, row.shape[1]), 0)
+    block = jnp.where(place == 0, hi, jnp.where(place == 1, mid, jnp.where(place == 2, low, 0.0)))
+    return block.astype(bf16)
+
+
+class KeyChain:
+    def __init__(self, here, kv, sems):
+        self.h, self.kv, self.sems = here, kv, sems
+
+    def up(self, slot):
+        h = self.h
+        to = lax.rem(h.z + 1, h.grid.nz)
+
+        @pl.when(h.z < h.grid.nz - 1)
+        def _():
+            send(self.kv.at[slot], self.kv.at[slot], self.sems.at[0, slot], self.sems.at[1, slot], h.on_z(to))
+
+    def take(self, slot):
+        wait_bytes(self.kv.at[slot], self.sems.at[1, slot])
+        self.up(slot)
+
+    def drain(self):
+        h = self.h
+        for s in range(h.grid.nz):
+
+            @pl.when(jnp.logical_and(h.z >= s, h.z < h.grid.nz - 1))
+            def _():
+                wait_bytes(self.kv.at[h.z - s], self.sems.at[0, h.z - s])
+
+
+def front_kernel(grid, z_majors, *refs):
+    n = len(z_majors)
+    shards, refs = refs[:n], refs[n:]
+    heads, x, gain, cos, sin, qext, kext = refs[:7]
+    refs = refs[7:]
+    outs, refs = refs[:n], refs[n:]
+    qx, kv, att, lse = refs[:4]
+    h1, proj, kx, vt, acc, sems, kv_sems = refs[4:]
+    here = Here(grid)
+    tokens = x.shape[1]
+    half = tokens // 2
+    greet(here.peers())
+    jobs = [Gather(here, shards[i], outs[i], sems.at[i], z_majors[i]) for i in range(n)]
+    for job in jobs[:-1]:
+        job.stage_z()
+
+    inverse = inverse_rms(x)
+    for k in range(DEPTH):
+        rows = pl.ds(k * SLICE, SLICE)
+        h1[rows] = (x[rows].astype(f32) * inverse * gain[rows]).astype(bf16)
+
+    part = QKV // 5
+
+    def project(m, carry):
+        rows = pl.ds(pl.multiple_of(m * part, 16), part)
+        total = mm(heads[0, rows], h1[pl.ds(0, SLICE)])
+        for k in range(1, DEPTH):
+            total += mm(heads[k, rows], h1[pl.ds(k * SLICE, SLICE)])
+        proj[rows] = total
+        return carry
+
+    lax.fori_loop(0, 5, project, 0)
+
+    def turned(h):
+        base = h * HEAD
+        a = proj[pl.ds(pl.multiple_of(base, 8), HEAD // 2)]
+        b = proj[pl.ds(pl.multiple_of(base + HEAD // 2, 8), HEAD // 2)]
+        c, s = cos[...], sin[...]
+        return a * c - b * s, b * c + a * s
+
+    def keys(g, carry):
+        a, b = turned(QUERY_HEADS + g)
+        v = proj[pl.ds(pl.multiple_of((QUERY_HEADS + KEY_VALUE_HEADS + g) * HEAD, 8), HEAD)]
+        both = jnp.concatenate([a, b, v], axis=0)
+        kv[here.z, g] = both.T.astype(bf16)
+        return carry
+
+    lax.fori_loop(0, KEY_VALUE_HEADS, keys, 0)
+    chain = KeyChain(here, kv, kv_sems)
+    chain.up(here.z)
+    jobs[-1].stage_z()
+
+    def queries(h, carry):
+        a, b = turned(h)
+        scale = HEAD**-0.5
+        qx[h, pl.ds(0, 32)] = (a.astype(bf16).astype(f32) * scale).astype(bf16)
+        qx[h, pl.ds(32, 32)] = (b.astype(bf16).astype(f32) * scale).astype(bf16)
+        qx[h, pl.ds(64, 64)] = qext[...]
+        return carry
+
+    lax.fori_loop(0, QUERY_HEADS, queries, 0)
+
+    def prepare(slot):
+        ext = kext[pl.ds(pl.multiple_of(slot * tokens, 16), tokens)]
+
+        def body(g, carry):
+            block = kv[slot, g]
+            kx[g] = jnp.where(lanes_below(block.shape, HEAD), block, ext)
+            turned_block = block.astype(f32).T
+            vt[g, pl.ds(0, 16)] = jnp.ones((16, tokens), bf16)
+            vt[g, pl.ds(16, HEAD)] = (turned_block[HEAD:] * VALUE_SCALE).astype(bf16)
+            return carry
+
+        lax.fori_loop(0, KEY_VALUE_HEADS, body, 0)
+
+    def below(key, query):
+        row = lax.broadcasted_iota(jnp.int32, (half, half), 0)
+        col = lax.broadcasted_iota(jnp.int32, (half, half), 1)
+        return row <= col
+
+    def diagonal():
+        prepare(here.z)
+
+        def body(g, carry):
+            for i in range(GROUP):
+                h = g * GROUP + i
+                mask = below(0, 0)
+                s = mm(kx[g, pl.ds(0, half)], qx[h])
+                low = jnp.exp(jnp.where(mask, s[:, :half], HIDE)).astype(bf16)
+                high = jnp.exp(s[:, half:]).astype(bf16)
+                acc[h, :, pl.ds(0, half)] = mm(vt[g, :, pl.ds(0, half)], low)
+                total = mm(vt[g, :, pl.ds(0, half)], high)
+                s = mm(kx[g, pl.ds(half, half)], qx[h, :, pl.ds(half, half)])
+                p = jnp.exp(jnp.where(mask, s, HIDE)).astype(bf16)
+                acc[h, :, pl.ds(half, half)] = total + mm(vt[g, :, pl.ds(half, half)], p)
+            return carry
+
+        lax.fori_loop(0, KEY_VALUE_HEADS, body, 0)
+
+    def whole(slot):
+        prepare(slot)
+
+        def body(g, carry):
+            for i in range(GROUP):
+                h = g * GROUP + i
+                total = acc[h]
+                for k in range(2):
+                    s = mm(kx[g, pl.ds(k * half, half)], qx[h])
+                    total += mm(vt[g, :, pl.ds(k * half, half)], jnp.exp(s).astype(bf16))
+                acc[h] = total
+            return carry
+
+        lax.fori_loop(0, KEY_VALUE_HEADS, body, 0)
+
+    def earlier(s):
+        @pl.when(here.z >= s)
+        def _():
+            chain.take(here.z - s)
+            whole(here.z - s)
+
+    ticks = []
+    for step in range(n + 2):
+        if step < n:
+            ticks.append(jobs[step].stage_one)
+        if 0 <= step - 1 < n:
+            ticks.append(jobs[step - 1].stage_two)
+        if 0 <= step - 2 < n:
+            ticks.append(jobs[step - 2].stage_three)
+    diagonal()
+    steps = grid.nz - 1
+    share = -(-len(ticks) // (steps + 1))
+    for s in range(1, grid.nz):
+        for tick in ticks[(s - 1) * share : s * share]:
+            tick()
+        earlier(s)
+    for tick in ticks[steps * share :]:
+        tick()
+
+    def close(h, carry):
+        totals = acc[h, pl.ds(0, 1)]
+        scale = (1.0 / VALUE_SCALE) / totals
+        att[pl.ds(pl.multiple_of(h * HEAD, 16), HEAD)] = (acc[h, pl.ds(16, HEAD)] * scale).astype(bf16)
+        lse[h] = jnp.log(totals)
+        return carry
+
+    lax.fori_loop(0, QUERY_HEADS, close, 0)
+    for job in jobs:
+        job.arrive()
+        job.drain()
+    chain.drain()
+
+
+def front(grid, shards, z_majors, heads, x, gain, cos, sin, qext, kext, collective_id):
+    tokens = x.shape[1]
+    shapes = []
+    for shard, z_major in zip(shards, z_majors):
+        lead = (grid.nz, grid.nd) if z_major else (grid.nd, grid.nz)
+        shapes.append(jax.ShapeDtypeStruct(lead + shard.shape, shard.dtype))
+    n = len(shards)
+    shapes += [
+        jax.ShapeDtypeStruct((QUERY_HEADS, 128, tokens), bf16),
+        jax.ShapeDtypeStruct((grid.nz, KEY_VALUE_HEADS, tokens, 128), bf16),
+        jax.ShapeDtypeStruct((D, tokens), bf16),
+        jax.ShapeDtypeStruct((QUERY_HEADS, 1, tokens), f32),
+    ]
+    return pl.pallas_call(
+        functools.partial(front_kernel, grid, tuple(z_majors)),
+        out_shape=shapes,
+        in_specs=[VMEM] * (n + 7),
+        out_specs=[ANY] * n + [VMEM] * 4,
+        scratch_shapes=[
+            pltpu.VMEM((D, tokens), bf16),
+            pltpu.VMEM((QKV, tokens), f32),
+            pltpu.VMEM((KEY_VALUE_HEADS, tokens, 128), bf16),
+            pltpu.VMEM((KEY_VALUE_HEADS, 80, tokens), bf16),
+            pltpu.VMEM((QUERY_HEADS, 80, tokens), f32),
+            pltpu.SemaphoreType.DMA((n, GATHER_SEMS)),
+            pltpu.SemaphoreType.DMA((2, grid.nz)),
         ],
-        axis=-1,
-    )
-
-
-def reverse_rotary(values, cosine_table, sine_table):
-    half_width = HEAD_SIZE // 2
-    first_half = values[..., :half_width]
-    second_half = values[..., half_width:]
-    cos_part = cosine_table[:, None, :]
-    sin_part = sine_table[:, None, :]
-    return jnp.concatenate(
-        [
-            first_half * cos_part + second_half * sin_part,
-            second_half * cos_part - first_half * sin_part,
+        compiler_params=pltpu.CompilerParams(
+            collective_id=collective_id, has_side_effects=True, vmem_limit_bytes=60 << 20
+        ),
+        name="front",
+    )(*shards, heads, x, gain, cos, sin, qext, kext)
+
+
+def middle_kernel(blocks, att, wo, x, ogt, gain, eg, eu, dn, out, rg, gsum, dexp, ddn, dwo, dot, delta,
+                  res, inv, h2, h2t, og, acc_o, acc_h, mixed, dgate, dup):
+    f = pl.program_id(0)
+    tokens = x.shape[1]
+    half = tokens // 2
+
+    @pl.when(f == 0)
+    def _():
+        total = jnp.zeros((1, tokens), f32)
+        for m in range(DEPTH):
+            rows = pl.ds(m * SLICE, SLICE)
+            r = x[rows].astype(f32)
+            for k in range(DEPTH):
+                r += mm(wo[k, rows], att[pl.ds(k * SLICE, SLICE)])
+            res[rows] = r
+            total += jnp.sum(r * r, axis=0, keepdims=True)
+        inverse = lax.rsqrt(total * (1.0 / D) + norm_epsilon)
+        inv[...] = inverse
+        for m in range(DEPTH):
+            rows = pl.ds(m * SLICE, SLICE)
+            h2t[rows] = (res[rows] * inverse * gain[rows]).astype(bf16)
+        h2[...] = h2t[...].astype(f32).T.astype(bf16)
+        og[...] = ogt[...].astype(f32).T.astype(bf16)
+        acc_o[...] = jnp.zeros_like(acc_o)
+        acc_h[...] = jnp.zeros_like(acc_h)
+
+    def activate(i, carry):
+        rows = pl.ds(pl.multiple_of(i * 128, 128), 128)
+        gate = mm(h2[rows], eg[...])
+        up = mm(h2[rows], eu[...])
+        back = mm(og[rows], dn[...])
+        s = 1.0 / (1.0 + jnp.exp(-gate))
+        silu = gate * s
+        mixed[rows] = (silu * up).astype(bf16)
+        dgate[rows] = (back * up * s * (1.0 + gate * (1.0 - s))).astype(bf16)
+        dup[rows] = (back * silu).astype(bf16)
+        return carry
+
+    lax.fori_loop(0, tokens // 128, activate, 0)
+    for m in range(DEPTH):
+        rows = pl.ds(m * SLICE, SLICE)
+        acc_o[rows] += mm_nt(dn[rows], mixed[...])
+        acc_h[rows] += mm_nt(eg[rows], dgate[...]) + mm_nt(eu[rows], dup[...])
+        dexp[0, rows] = mm(h2t[rows], dgate[...]).astype(bf16)
+        dexp[1, rows] = mm(h2t[rows], dup[...]).astype(bf16)
+        ddn[rows] = mm(ogt[rows], mixed[...]).astype(bf16)
+
+    @pl.when(f == blocks - 1)
+    def _():
+        inverse = inv[...]
+        total = jnp.zeros((1, tokens), f32)
+        for m in range(DEPTH):
+            rows = pl.ds(m * SLICE, SLICE)
+            out[rows] = (res[rows] + acc_o[rows]).astype(bf16)
+            normed = res[rows] * inverse
+            up = acc_h[rows]
+            gsum[rows] = jnp.sum(up * normed, axis=1, keepdims=True)
+            total += jnp.sum(up * gain[rows] * normed, axis=0, keepdims=True)
+        mean = total * (1.0 / D)
+        for m in range(DEPTH):
+            rows = pl.ds(m * SLICE, SLICE)
+            normed = res[rows] * inverse
+            r = ogt[rows].astype(f32) + inverse * (acc_h[rows] * gain[rows] - normed * mean)
+            rg[rows] = r
+            h2t[rows] = r.astype(bf16)
+        for k in range(DEPTH):
+            rows = pl.ds(k * SLICE, SLICE)
+            dwo[k] = mm_nt(h2t[...], att[rows]).astype(bf16)
+            dot[rows] = mm_tn(wo[k], h2t[...]).astype(bf16)
+
+        def rows_of(h, carry):
+            rows = pl.ds(pl.multiple_of(h * HEAD, 16), HEAD)
+            delta[h] = jnp.sum(dot[rows].astype(f32) * att[rows].astype(f32), axis=0, keepdims=True)
+            return carry
+
+        lax.fori_loop(0, QUERY_HEADS, rows_of, 0)
+
+
+def middle(att, wo, x, ogt, gain, expand, down):
+    tokens = x.shape[1]
+    blocks, _, width = down.shape
+    full = pl.BlockSpec(memory_space=pltpu.VMEM)
+
+    def spec(offset):
+        return pl.BlockSpec((None, D, width), lambda f: (f + offset, 0, 0))
+
+    return pl.pallas_call(
+        functools.partial(middle_kernel, blocks),
+        grid=(blocks,),
+        out_shape=[
+            jax.ShapeDtypeStruct((D, tokens), bf16),
+            jax.ShapeDtypeStruct((D, tokens), f32),
+            jax.ShapeDtypeStruct((D, 1), f32),
+            jax.ShapeDtypeStruct((2, blocks, D, width), bf16),
+            jax.ShapeDtypeStruct((blocks, D, width), bf16),
+            jax.ShapeDtypeStruct((DEPTH, D, SLICE), bf16),
+            jax.ShapeDtypeStruct((D, tokens), bf16),
+            jax.ShapeDtypeStruct((QUERY_HEADS, 1, tokens), f32),
         ],
-        axis=-1,
-    )
-
-
-def rms_forward(values, gain):
-    inverse = lax.rsqrt(jnp.mean(values * values, axis=-1, keepdims=True) + norm_epsilon)
-    normed = values * inverse
-    return (normed, inverse, (normed * gain).astype(jnp.bfloat16))
-
-
-def rms_backward(upstream, normed, inverse, gain):
-    scaled = upstream * gain
-    gain_term = jnp.sum(upstream * normed, axis=0)
-    back = inverse * (scaled - normed * jnp.mean(scaled * normed, axis=-1, keepdims=True))
-    return (back, gain_term)
-
-
-def times_transposed(left, right):
-    return lax.dot_general(
-        left, right, (((1,), (1,)), ((), ())), preferred_element_type=jnp.float32
-    )
-
-
-def transposed_times(left, right):
-    return lax.dot_general(
-        left, right, (((0,), (0,)), ((), ())), preferred_element_type=jnp.float32
-    )
+        in_specs=[full] * 5 + [spec(0), spec(blocks), spec(0)],
+        out_specs=[
+            full,
+            full,
+            full,
+            pl.BlockSpec((2, None, D, width), lambda f: (0, f, 0, 0)),
+            spec(0),
+            full,
+            full,
+            full,
+        ],
+        scratch_shapes=[
+            pltpu.VMEM((D, tokens), f32),
+            pltpu.VMEM((1, tokens), f32),
+            pltpu.VMEM((tokens, D), bf16),
+            pltpu.VMEM((D, tokens), bf16),
+            pltpu.VMEM((tokens, D), bf16),
+            pltpu.VMEM((D, tokens), f32),
+            pltpu.VMEM((D, tokens), f32),
+            pltpu.VMEM((tokens, width), bf16),
+            pltpu.VMEM((tokens, width), bf16),
+            pltpu.VMEM((tokens, width), bf16),
+        ],
+        compiler_params=pltpu.CompilerParams(vmem_limit_bytes=62 << 20),
+        name="middle",
+    )(att, wo, x, ogt, gain, expand, expand, down)
+
+
+class GradChain:
+    def __init__(self, here, part, sent, got, sems):
+        self.h, self.part, self.sent, self.got, self.sems = here, part, sent, got, sems
+
+    def summed(self, slot, write):
+        h = self.h
+
+        @pl.when(h.z < h.grid.nz - 1)
+        def _():
+            wait_bytes(self.got.at[slot], self.sems.at[1, slot])
+
+            def body(g, carry):
+                write(g, self.part[slot, g] + self.got[slot, g].astype(f32))
+                return carry
+
+            lax.fori_loop(0, KEY_VALUE_HEADS, body, 0)
+
+        @pl.when(h.z == h.grid.nz - 1)
+        def _():
+            def body(g, carry):
+                write(g, self.part[slot, g])
+                return carry
+
+            lax.fori_loop(0, KEY_VALUE_HEADS, body, 0)
+
+    def relay(self, slot):
+        h = self.h
+
+        @pl.when(slot < h.z)
+        def _():
+            def write(g, value):
+                self.sent[slot, g] = value.astype(bf16)
+
+            self.summed(slot, write)
+            to = lax.rem(h.z + h.grid.nz - 1, h.grid.nz)
+            send(self.sent.at[slot], self.got.at[slot], self.sems.at[0, slot], self.sems.at[1, slot], h.on_z(to))
+
+    def drain(self):
+        h = self.h
+        for slot in range(h.grid.nz - 1):
+
+            @pl.when(slot < h.z)
+            def _():
+                wait_bytes(self.sent.at[slot], self.sems.at[0, slot])
+
+
+def back_kernel(grid, z_majors, *refs):
+    n = len(z_majors)
+    terms, refs = refs[:n], refs[n:]
+    qx_in, lse, dot, delta, kv, kext, cos, sin = refs[:8]
+    refs = refs[8:]
+    results, refs = refs[:n], refs[n:]
+    hd, refs = refs[0], refs[1:]
+    jobs = []
+    here = Here(grid)
+    for i in range(n):
+        jobs.append(refs[:REDUCE_BUFS])
+        refs = refs[REDUCE_BUFS:]
+    qx, dox, kx, vx, kt, dq, part, sent, got, sems, kv_sems = refs
+    jobs = [Reduce(here, terms[i], results[i], jobs[i], sems.at[i], z_majors[i]) for i in range(n)]
+    tokens = dot.shape[1]
+    half = tokens // 2
+    greet(here.peers())
+    for job in jobs:
+        job.stage_core()
+    ticks = []
+    for step in range(n + 3):
+        if step < n:
+            ticks.append(jobs[step].stage_one)
+        if 0 <= step - 1 < n:
+            ticks.append(jobs[step - 1].stage_two)
+        if 0 <= step - 2 < n:
+            ticks.append(jobs[step - 2].stage_three)
+        if 0 <= step - 3 < n:
+            ticks.append(jobs[step - 3].finish)
+
+    def gather_queries(h, carry):
+        qx[h, pl.ds(0, 80)] = qx_in[h, pl.ds(0, 80)]
+        qx[h, pl.ds(80, 16)] = three_pieces(-lse[h])
+        qx[h, pl.ds(96, 32)] = jnp.zeros((32, tokens), bf16)
+        dox[h, pl.ds(0, 16)] = three_pieces(-delta[h])
+        dox[h, pl.ds(16, 48)] = jnp.zeros((48, tokens), bf16)
+        dox[h, pl.ds(64, 64)] = dot[pl.ds(pl.multiple_of(h * HEAD, 16), HEAD)]
+        dq[h] = jnp.zeros((HEAD, tokens), f32)
+        return carry
+
+    lax.fori_loop(0, QUERY_HEADS, gather_queries, 0)
+
+    def prepare(slot):
+        ext = kext[pl.ds(pl.multiple_of(slot * tokens, 16), tokens)]
+
+        def body(g, carry):
+            block = kv[slot, g]
+            low = lanes_below(block.shape, HEAD)
+            kx[g] = jnp.where(low, block, ext)
+            ones = jnp.where(lanes_below(block.shape, 3), 1.0, 0.0).astype(bf16)
+            vx[g] = jnp.where(low, ones, block)
+            kt[g] = block.astype(f32).T[:HEAD].astype(bf16)
+            return carry
+
+        lax.fori_loop(0, KEY_VALUE_HEADS, body, 0)
+
+    def tile(g, h, k, queries, masked):
+        keys = pl.ds(k * half, half)
+        start, count = queries
+        cols = pl.ds(start, count)
+        s = mm(kx[g, keys], qx[h, :, cols])
+        if masked:
+            row = lax.broadcasted_iota(jnp.int32, s.shape, 0) + k * half
+            col = lax.broadcasted_iota(jnp.int32, s.shape, 1) + start
+            s = jnp.where(row <= col, s, HIDE)
+        p = jnp.exp(s)
+        ds = (p * mm(vx[g, keys], dox[h, :, cols])).astype(bf16)
+        dq[h, :, cols] += mm(kt[g, :, keys], ds)
+        dk = mm_nt(ds, qx[h, :, cols])
+        dv = mm_nt(p.astype(bf16), dox[h, :, cols])
+        return jnp.where(lanes_below(dk.shape, HEAD), dk, dv)
+
+    def whole(slot):
+        prepare(slot)
+
+        def body(g, carry):
+            for k in range(2):
+                total = tile(g, g * GROUP, k, (0, tokens), False)
+                for i in range(1, GROUP):
+                    total += tile(g, g * GROUP + i, k, (0, tokens), False)
+                part[slot, g, pl.ds(k * half, half)] = total
+            return carry
+
+        lax.fori_loop(0, KEY_VALUE_HEADS, body, 0)
+
+    def diagonal():
+        prepare(here.z)
+
+        def body(g, carry):
+            for k in range(2):
+                span = (k * half, tokens - k * half)
+                total = tile(g, g * GROUP, k, span, True)
+                for i in range(1, GROUP):
+                    total += tile(g, g * GROUP + i, k, span, True)
+                part[here.z, g, pl.ds(k * half, half)] = total
+            return carry
+
+        lax.fori_loop(0, KEY_VALUE_HEADS, body, 0)
+
+    chain = GradChain(here, part, sent, got, kv_sems)
+    steps = grid.nz
+    share = -(-len(ticks) // (steps + 1))
+    for slot in range(grid.nz - 1):
+        for tick in ticks[slot * share : (slot + 1) * share]:
+            tick()
+
+        @pl.when(slot < here.z)
+        def _():
+            whole(slot)
+
+        if slot > 0:
+            chain.relay(slot - 1)
+    for tick in ticks[(steps - 1) * share : steps * share]:
+        tick()
+    diagonal()
+    chain.relay(grid.nz - 2)
+    for tick in ticks[steps * share :]:
+        tick()
+
+    def turn_back(a, b):
+        c, s = cos[...], sin[...]
+        return a * c + b * s, b * c - a * s
+
+    def queries(h, carry):
+        scale = HEAD**-0.5
+        a, b = turn_back(dq[h, pl.ds(0, 32)] * scale, dq[h, pl.ds(32, 32)] * scale)
+        hd[pl.ds(pl.multiple_of(h * HEAD, 16), 32)] = a.astype(bf16)
+        hd[pl.ds(pl.multiple_of(h * HEAD + 32, 16), 32)] = b.astype(bf16)
+        return carry
+
+    lax.fori_loop(0, QUERY_HEADS, queries, 0)
+
+    def write(g, value):
+        turned = value.T
+        a, b = turn_back(turned[:32], turned[32:64])
+        base = (QUERY_HEADS + g) * HEAD
+        hd[pl.ds(pl.multiple_of(base, 16), 32)] = a.astype(bf16)
+        hd[pl.ds(pl.multiple_of(base + 32, 16), 32)] = b.astype(bf16)
+        base = (QUERY_HEADS + KEY_VALUE_HEADS + g) * HEAD
+        hd[pl.ds(pl.multiple_of(base, 16), HEAD)] = turned[64:].astype(bf16)
+
+    chain.summed(here.z, write)
+    chain.drain()
+    for job in jobs:
+        job.drain()
+
+
+def split_terms(grid, terms, z_majors):
+    split = []
+    for term, z_major in zip(terms, z_majors):
+        lead = (grid.ny, grid.nx, 2)
+        lead = (grid.nz,) + lead if z_major else lead + (grid.nz,)
+        split.append(term.reshape(lead + term.shape[-2:]))
+    return split
+
+
+def back(grid, terms, z_majors, qx, lse, dot, delta, kv, kext, cos, sin, collective_id):
+    tokens = dot.shape[1]
+    n = len(terms)
+    scratch, shapes = [], []
+    for term, z_major in zip(terms, z_majors):
+        rows, cols = term.shape[-2:]
+        shapes.append(jax.ShapeDtypeStruct((rows, cols), f32))
+        scratch += Reduce.scratch(grid, rows, cols, z_major)
+    shapes.append(jax.ShapeDtypeStruct((QKV, tokens), bf16))
+    blocks = (grid.nz, KEY_VALUE_HEADS, tokens, 128)
+    scratch += [
+        pltpu.VMEM((QUERY_HEADS, 128, tokens), bf16),
+        pltpu.VMEM((QUERY_HEADS, 128, tokens), bf16),
+        pltpu.VMEM((KEY_VALUE_HEADS, tokens, 128), bf16),
+        pltpu.VMEM((KEY_VALUE_HEADS, tokens, 128), bf16),
+        pltpu.VMEM((KEY_VALUE_HEADS, HEAD, tokens), bf16),
+        pltpu.VMEM((QUERY_HEADS, HEAD, tokens), f32),
+        pltpu.VMEM(blocks, f32),
+        pltpu.VMEM((grid.nz - 1,) + blocks[1:], bf16),
+        pltpu.VMEM(blocks, bf16),
+        pltpu.SemaphoreType.DMA((n, REDUCE_SEMS)),
+        pltpu.SemaphoreType.DMA((2, grid.nz)),
+    ]
+    return pl.pallas_call(
+        functools.partial(back_kernel, grid, tuple(z_majors)),
+        out_shape=shapes,
+        in_specs=[ANY] * n + [VMEM] * 8,
+        out_specs=[VMEM] * (n + 1),
+        scratch_shapes=scratch,
+        compiler_params=pltpu.CompilerParams(
+            collective_id=collective_id, has_side_effects=True, vmem_limit_bytes=63 << 20
+        ),
+        name="back",
+    )(*split_terms(grid, terms, z_majors), qx, lse, dot, delta, kv, kext, cos, sin)
+
+
+def ending_kernel(hd, heads, x, gain, rg, ig, gsum, dheads, h1, og, inv):
+    tokens = x.shape[1]
+    inverse = inverse_rms(x)
+    for k in range(DEPTH):
+        rows = pl.ds(k * SLICE, SLICE)
+        normed = x[rows].astype(f32) * inverse
+        h1[rows] = (normed * gain[rows]).astype(bf16)
+    for k in range(DEPTH):
+        rows = pl.ds(k * SLICE, SLICE)
+        for m in range(5):
+            part = pl.ds(m * (QKV // 5), QKV // 5)
+            dheads[k, part] = mm_nt(hd[part], h1[rows]).astype(bf16)
+        og[rows] = mm_tn(heads[k], hd[...])
+    total = jnp.zeros((1, tokens), f32)
+    for k in range(DEPTH):
+        rows = pl.ds(k * SLICE, SLICE)
+        normed = x[rows].astype(f32) * inverse
+        gsum[rows] = jnp.sum(og[rows] * normed, axis=1, keepdims=True)
+        total += jnp.sum(og[rows] * gain[rows] * normed, axis=0, keepdims=True)
+    mean = total * (1.0 / D)
+    for k in range(DEPTH):
+        rows = pl.ds(k * SLICE, SLICE)
+        normed = x[rows].astype(f32) * inverse
+        ig[rows] = rg[rows] + inverse * (og[rows] * gain[rows] - normed * mean)
+
+
+def ending(hd, heads, x, gain, rg):
+    tokens = x.shape[1]
+    return pl.pallas_call(
+        ending_kernel,
+        out_shape=[
+            jax.ShapeDtypeStruct((D, tokens), f32),
+            jax.ShapeDtypeStruct((D, 1), f32),
+            jax.ShapeDtypeStruct((DEPTH, QKV, SLICE), bf16),
+        ],
+        in_specs=[VMEM] * 5,
+        out_specs=[VMEM] * 3,
+        scratch_shapes=[
+            pltpu.VMEM((D, tokens), bf16),
+            pltpu.VMEM((D, tokens), f32),
+            pltpu.VMEM((1, tokens), f32),
+        ],
+        compiler_params=pltpu.CompilerParams(vmem_limit_bytes=60 << 20),
+        name="ending",
+    )(hd, heads, x, gain, rg)
 
 
 def adamw(weight, grad, first, second, rate, decay):
@@ -550,80 +1154,7 @@
     return (weight_new, first_new, second_new)
 
 
-def attend_forward(queries, all_keys, allowed):
-    group_width = QUERY_HEADS // KEY_VALUE_HEADS
-    key_total_width = KEY_VALUE_HEADS * HEAD_SIZE
-    outputs = []
-    logsums = []
-    for group_of_head in range(KEY_VALUE_HEADS):
-        query_group = queries[:, group_of_head * group_width : (group_of_head + 1) * group_width, :]
-        key_group = all_keys[:, group_of_head * HEAD_SIZE : (group_of_head + 1) * HEAD_SIZE]
-        value_group = all_keys[
-            :,
-            key_total_width
-            + group_of_head * HEAD_SIZE : key_total_width
-            + (group_of_head + 1) * HEAD_SIZE,
-        ]
-        scores = jnp.einsum(
-            "qhd,kd->hqk", query_group, key_group, preferred_element_type=jnp.float32
-        ) * HEAD_SIZE ** (-0.5)
-        exponent = jnp.where(allowed[None], jnp.exp(scores), 0.0)
-        totals = jnp.sum(exponent, axis=-1)
-        probs = (exponent / totals[..., None]).astype(jnp.bfloat16)
-        outputs.append(
-            jnp.einsum("hqk,kd->qhd", probs, value_group, preferred_element_type=jnp.float32)
-        )
-        logsums.append(jnp.log(totals))
-    return (jnp.concatenate(outputs, axis=1), jnp.concatenate(logsums, axis=0))
-
-
-def attend_backward(queries, all_keys, allowed, logsums, attended, attended_grad):
-    group_width = QUERY_HEADS // KEY_VALUE_HEADS
-    key_total_width = KEY_VALUE_HEADS * HEAD_SIZE
-    row_delta = jnp.sum(attended_grad.astype(jnp.float32) * attended.astype(jnp.float32), axis=-1)
-    query_grads = []
-    key_grads = []
-    value_grads = []
-    for group_of_head in range(KEY_VALUE_HEADS):
-        lower_head = group_of_head * group_width
-        upper_head = lower_head + group_width
-        query_group = queries[:, lower_head:upper_head, :]
-        grad_group = attended_grad[:, lower_head:upper_head, :]
-        key_group = all_keys[:, group_of_head * HEAD_SIZE : (group_of_head + 1) * HEAD_SIZE]
-        value_group = all_keys[
-            :,
-            key_total_width
-            + group_of_head * HEAD_SIZE : key_total_width
-            + (group_of_head + 1) * HEAD_SIZE,
-        ]
-        scores = jnp.einsum(
-            "qhd,kd->hqk", query_group, key_group, preferred_element_type=jnp.float32
-        ) * HEAD_SIZE ** (-0.5)
-        probs = jnp.where(
-            allowed[None], jnp.exp(scores - logsums[lower_head:upper_head][..., None]), 0.0
-        )
-        probs_half = probs.astype(jnp.bfloat16)
-        prob_grad = jnp.einsum(
-            "qhd,kd->hqk", grad_group, value_group, preferred_element_type=jnp.float32
-        )
-        score_grad = (
-            probs
-            * (prob_grad - jnp.transpose(row_delta[:, lower_head:upper_head])[..., None])
-            * HEAD_SIZE ** (-0.5)
-        ).astype(jnp.bfloat16)
-        query_grads.append(
-            jnp.einsum("hqk,kd->qhd", score_grad, key_group, preferred_element_type=jnp.float32)
-        )
-        key_grads.append(
-            jnp.einsum("hqk,qhd->kd", score_grad, query_group, preferred_element_type=jnp.float32)
-        )
-        value_grads.append(
-            jnp.einsum("hqk,qhd->kd", probs_half, grad_group, preferred_element_type=jnp.float32)
-        )
-    return (jnp.concatenate(query_grads, axis=1), jnp.concatenate(key_grads + value_grads, axis=1))
-
-
-Z_MAJOR = (True, True, False, True)
+EXPAND_BLOCKS = 8
 
 
 def local(
@@ -648,114 +1179,57 @@
     down_first,
     down_second,
 ):
-    count_of_rows = hidden_in.shape[0]
-    query_total_width = QUERY_HEADS * HEAD_SIZE
-    key_total_width = KEY_VALUE_HEADS * HEAD_SIZE
-    heads_stack, output_stack, expand_stack, down_stack = gather_weights(
+    tokens = hidden_in.shape[0]
+    first_row = lax.axis_index("shard") * tokens
+    positions = first_row + jnp.arange(tokens, dtype=jnp.int32)
+    freq = jnp.power(10000.0, -jnp.arange(HEAD // 2).astype(f32) / (HEAD // 2))
+    angle = (positions - doc_start).astype(f32)[None, :] * freq[:, None]
+    cos, sin = jnp.cos(angle), jnp.sin(angle)
+    seg_row = seg_ids[0]
+    seg_query = lax.dynamic_slice_in_dim(seg_row, first_row, tokens)
+    doc = jnp.arange(HEAD, dtype=jnp.int32)
+    qext = jnp.where((doc[:, None] < DOCS) & (seg_query[None, :] == doc[:, None]), HIDE, 0.0).astype(bf16)
+    lane = jnp.arange(128, dtype=jnp.int32) - HEAD
+    other_doc = (lane[None, :] >= 0) & (lane[None, :] < DOCS) & (seg_row[:, None] != lane[None, :])
+    kext = jnp.where(other_doc | ((lane >= DOCS) & (lane < DOCS + 3))[None, :], 1.0, 0.0).astype(bf16)
+    x, ogt = hidden_in.T, out_grad.T
+    gain_one, gain_two = norm_gains[0][:, None], norm_gains[1][:, None]
+
+    (heads_stack,) = gather_weights(grid, [heads_weight.astype(bf16).T], (True,), 1)
+    heads = heads_stack.reshape(DEPTH, QKV, SLICE)
+    shards = [output_weight.astype(bf16).T, down_weight.astype(bf16).T, expand_weight.astype(bf16)]
+    z_majors = (True, True, False)
+    output_stack, down_stack, expand_stack, qx, kv, att, lse = front(
+        grid, shards, z_majors, heads, x, gain_one, cos, sin, qext, kext, 2
+    )
+    wo = output_stack.reshape(DEPTH, D, SLICE)
+    down = down_stack.reshape(DEPTH, D, FF // DEPTH)
+    expand = expand_stack.reshape(grid.nd, D, 2 * FF // grid.nd)
+    pieces = grid.nd // EXPAND_BLOCKS
+    if pieces > 1:
+        expand = expand.reshape(EXPAND_BLOCKS, pieces, D, -1).transpose(0, 2, 1, 3)
+        expand = expand.reshape(EXPAND_BLOCKS, D, 2 * FF // EXPAND_BLOCKS)
+    out, rg, gain_two_term, dexpand, ddn, dwo, dot, delta = middle(att, wo, x, ogt, gain_two, expand, down)
+    if pieces > 1:
+        dexpand = dexpand.reshape(EXPAND_BLOCKS, D, pieces, -1).transpose(0, 2, 1, 3)
+    terms = [
+        ddn.reshape(down_stack.shape),
+        dexpand.reshape(expand_stack.shape),
+        dwo.reshape(output_stack.shape),
+    ]
+    down_grad, expand_grad, output_grad, hd = back(
+        grid, terms, (True, False, True), qx, lse, dot, delta, kv, kext, cos, sin, 3
+    )
+    ig, gain_one_term, dheads = ending(hd, heads, x, gain_one, rg)
+    heads_grad, gains_grad = reduce_grads(
         grid,
-        [
-            heads_weight.astype(jnp.bfloat16).T,
-            output_weight.astype(jnp.bfloat16).T,
-            expand_weight.astype(jnp.bfloat16),
-            down_weight.astype(jnp.bfloat16).T,
-        ],
-        Z_MAJOR,
-        1,
-    )
-    heads_half = heads_stack.transpose(0, 3, 1, 2).reshape(-1, heads_weight.shape[1] * grid.nd)
-    output_half = output_stack.transpose(0, 3, 1, 2).reshape(-1, output_weight.shape[1] * grid.nd)
-    expand_half = expand_stack.transpose(1, 2, 0, 3).reshape(-1, expand_weight.shape[1] * grid.nd)
-    down_half = down_stack.transpose(0, 3, 1, 2).reshape(-1, down_weight.shape[1] * grid.nd)
-    first_row = lax.axis_index("shard") * count_of_rows
-    positions = first_row + jnp.arange(count_of_rows, dtype=jnp.int32)
-    cosine_table, sine_table = rotary_tables(positions - doc_start)
-    seg_row = seg_ids[0]
-    seg_query = lax.dynamic_slice_in_dim(seg_row, first_row, count_of_rows)
-    key_places = jnp.arange(seg_row.shape[0], dtype=jnp.int32)
-    allowed = (seg_query[:, None] == seg_row[None, :]) & (key_places[None, :] <= positions[:, None])
-    gain_one = norm_gains[0]
-    gain_two = norm_gains[1]
-    inputs = hidden_in.astype(jnp.float32)
-    normed_one, inverse_one, hidden_one = rms_forward(inputs, gain_one)
-    projected_rows = jnp.dot(hidden_one, heads_half, preferred_element_type=jnp.float32)
-    queries = apply_rotary(
-        projected_rows[:, :query_total_width].reshape(count_of_rows, QUERY_HEADS, HEAD_SIZE),
-        cosine_table,
-        sine_table,
-    ).astype(jnp.bfloat16)
-    key_rotated = apply_rotary(
-        projected_rows[:, query_total_width : query_total_width + key_total_width].reshape(
-            count_of_rows, KEY_VALUE_HEADS, HEAD_SIZE
-        ),
-        cosine_table,
-        sine_table,
-    ).astype(jnp.bfloat16)
-    values = projected_rows[:, query_total_width + key_total_width :].astype(jnp.bfloat16)
-    packed = jnp.concatenate([key_rotated.reshape(count_of_rows, key_total_width), values], axis=1)
-    all_keys = lax.all_gather(packed, "shard", axis=0, tiled=True)
-    attended, logsums = attend_forward(queries, all_keys, allowed)
-    attended_half = attended.astype(jnp.bfloat16)
-    attended_flat = attended_half.reshape(count_of_rows, query_total_width)
-    residual = inputs + jnp.dot(attended_flat, output_half, preferred_element_type=jnp.float32)
-    normed_two, inverse_two, hidden_two = rms_forward(residual, gain_two)
-    gate_up = jnp.dot(hidden_two, expand_half, preferred_element_type=jnp.float32)
-    gate_part = gate_up[:, :FF]
-    up_part = gate_up[:, FF:]
-    sigmoid_gate = jax.nn.sigmoid(gate_part)
-    silu_gate = gate_part * sigmoid_gate
-    mixed_act = (silu_gate * up_part).astype(jnp.bfloat16)
-    hidden_out = (
-        residual + jnp.dot(mixed_act, down_half, preferred_element_type=jnp.float32)
-    ).astype(jnp.bfloat16)
-    upstream = out_grad.astype(jnp.float32)
-    mixed_grad = times_transposed(out_grad, down_half)
-    down_term = transposed_times(mixed_act, out_grad)
-    gate_grad = mixed_grad * up_part * sigmoid_gate * (1.0 + gate_part * (1.0 - sigmoid_gate))
-    up_grad = mixed_grad * silu_gate
-    expand_delta = jnp.concatenate([gate_grad, up_grad], axis=1).astype(jnp.bfloat16)
-    expand_term = transposed_times(hidden_two, expand_delta)
-    hidden_two_grad = times_transposed(expand_delta, expand_half)
-    residual_back, gain_two_term = rms_backward(hidden_two_grad, normed_two, inverse_two, gain_two)
-    residual_grad = upstream + residual_back
-    residual_delta = residual_grad.astype(jnp.bfloat16)
-    output_term = transposed_times(attended_flat, residual_delta)
-    attended_grad = (
-        times_transposed(residual_delta, output_half)
-        .astype(jnp.bfloat16)
-        .reshape(count_of_rows, QUERY_HEADS, HEAD_SIZE)
-    )
-    query_grad, packed_terms = attend_backward(
-        queries, all_keys, allowed, logsums, attended_half, attended_grad
-    )
-    packed_gradient = lax.psum_scatter(packed_terms, "shard", scatter_dimension=0, tiled=True)
-    key_backward = reverse_rotary(
-        packed_gradient[:, :key_total_width].reshape(count_of_rows, KEY_VALUE_HEADS, HEAD_SIZE),
-        cosine_table,
-        sine_table,
-    ).reshape(count_of_rows, key_total_width)
-    query_back = reverse_rotary(query_grad, cosine_table, sine_table).reshape(
-        count_of_rows, query_total_width
-    )
-    heads_delta = jnp.concatenate(
-        [query_back, key_backward, packed_gradient[:, key_total_width:]], axis=1
-    ).astype(jnp.bfloat16)
-    heads_term = transposed_times(hidden_one, heads_delta)
-    hidden_one_grad = times_transposed(heads_delta, heads_half)
-    input_back, gain_one_term = rms_backward(hidden_one_grad, normed_one, inverse_one, gain_one)
-    input_grad = residual_grad + input_back
-    def stacked(term, z_major):
-        rows, cols = term.shape[0] // grid.nz, term.shape[1] // grid.nd
-        term = term.astype(jnp.bfloat16).reshape(grid.nz, rows, grid.nd, cols)
-        return term.transpose(0, 2, 3, 1) if z_major else term.transpose(2, 0, 1, 3)
-
-    down_grad, expand_grad, output_grad, heads_grad, gains_grad = reduce_grads(
-        grid,
-        [stacked(down_term, True), stacked(expand_term, False), stacked(output_term, True), stacked(heads_term, True)],
-        (True, False, True, True),
-        jnp.stack([gain_one_term, gain_two_term], axis=0),
-        2,
+        [dheads.reshape(heads_stack.shape)],
+        (True,),
+        jnp.concatenate([gain_one_term, gain_two_term], axis=1).T,
+        4,
     )
     heads_grad, output_grad, down_grad = heads_grad.T, output_grad.T, down_grad.T
+    hidden_out, input_grad = out.T, ig.T
     gains_new, gains_first_new, gains_second_new = adamw(
         norm_gains, gains_grad, gains_first, gains_second, gain_rate, 0.0
     )

time: 681 us -> 458 us (0.67); the launches traced: 673 us -> 457 us
  matrix products: 236 us -> 0 us
  Pallas kernels: 240 us -> 429 us
  local copies, waits for them, and re-layouts: 128 us -> 11.1 us
  waiting for transfers between devices: 29.3 us -> 0 us
  between operations: 15.5 us -> 0.9 us
  other arithmetic: 24 us -> 16.2 us
    pallas_call x0 -> x4, Pallas kernels: none -> 357 us  [the longest x1 191 us: back(): pl.pallas_call(functools.partial(back_kernel, grid, tuple(z_majors)), out...]
    dot_general x42 -> x0, matrix products: 236 us -> none  [the longest x5 43.1 us: attend_forward(): jnp.einsum('qhd,kd->hqk', query_group, key_group, preferred_element_type=...]
    pallas_call x1, Pallas kernels: 119 us -> 33.3 us  [gather_weights(): pl.pallas_call(functools.partial(gather_kernel, grid, tuple(z_majors)), o...]
    pallas_call x1, Pallas kernels: 121 us -> 38.4 us  [reduce_grads(): pl.pallas_call(functools.partial(reduce_kernel, grid, tuple(z_majors), sh...]
    reshape x9 -> x0, local copies, waits for them, and re-layouts: 54.7 us -> none  [the longest x7 45.9 us: stacked(): term = term.astype(jnp.bfloat16).reshape(grid.nz, rows, grid.nd, cols)]
    transpose x6 -> x0, local copies, waits for them, and re-layouts: 30.2 us -> none  [the longest x1 13.1 us: local(): expand_stack.transpose(1, 2, 0, 3)]
    unnamed x188 -> x47, local copies, waits for them, and re-layouts: 36 us -> 6.17 us
    all_gather x1 -> x0, waiting for transfers between devices: 17.3 us -> none  [local(): all_keys = lax.all_gather(packed, 'shard', axis=0, tiled=True)]
  transfers between devices with their start and end apart: 2 -> 0, of which waited for: 2 -> 0; matrix products, arithmetic and copies ran while one was open for 18% -> 0% of each run, Pallas kernels for 0% -> 0%
where the time goes in v2:
time: 458 us; the launch traced here: 457 us
  Pallas kernels  429 us (94%)
  other arithmetic  16.2 us (4%)
  local copies, waits for them, and re-layouts  11.1 us (2%)
    pallas_call x1, Pallas kernels, back(): pl.pallas_call(functools.partial(back_kernel, grid, tuple(z_majors)), out...  191 us
    pallas_call x1, Pallas kernels, front(): pl.pallas_call(functools.partial(front_kernel, grid, tuple(z_majors)), ou...  109 us
    pallas_call x1, Pallas kernels, middle(): pl.pallas_call(functools.partial(middle_kernel, blocks), grid=(blocks,),...  46.8 us
    pallas_call x1, Pallas kernels, reduce_grads(): pl.pallas_call(functools.partial(reduce_kernel, grid, tuple(z_majors), sh...  38.4 us
    pallas_call x1, Pallas kernels, gather_weights(): pl.pallas_call(functools.partial(gather_kernel, grid, tuple(z_majors)), o...  33.3 us
    pallas_call x1, Pallas kernels, ending(): pl.pallas_call(ending_kernel, out_shape=[jax.ShapeDtypeStruct((D, tokens)...  10.7 us

profile of v2, /device:TPU:0, one launch (start us, length us, event | category | flops | bytes accessed | tf_op | source)
XLA Modules:
  0.0 457.3 jit_solution(18391258405002423851)
XLA Ops:
  0.7 0.7 constant_dynamic-slice_fusion
  1.4 0.7 select_convert_fusion.1.refs_8_
  2.1 0.7 subtract_convert_fusion
  2.8 1.0 multiply_sine_fusion
  3.8 1.9 select_convert_fusion.refs_9_.refs_8_
  5.7 0.8 slice_bitcast_fusion
  6.5 1.0 copy.53.refs_5_.gain
  7.5 1.6 convert_bitcast_fusion.1.refs_0_
  9.1 33.3 %gather_weights.1 = bf16[4,8,200,240]{3,2,1,0:T(8,128)(2,1)} custom-call(bf16[200,240]{1,0:T(8,128)(2,1)} %convert_bitcast_fusion.1.refs_0_), custom_call_target="tpu_custom_call" | custom-call | tf_op jit(solution)/shard_map/gather_weights/pallas_call | solution.py:195
  42.4 0.1 copy.52
  42.5 0.0 copy-start.4
  42.5 0.7 convert_bitcast_fusion.2.refs_0_
  43.2 0.0 copy-done
  43.2 0.8 convert_element_type.30.refs_2_
  43.9 0.7 convert_bitcast_fusion.refs_1_
  44.6 108.9 %front.1 = (bf16[4,8,120,240]{3,2,1,0:T(8,128)(2,1)}, bf16[4,8,120,640]{3,2,1,0:T(8,128)(2,1)}, bf16[8,4,240,640]{3,2,1,0:T(8,128)(2,1)}, bf16[15,128,512]{2,1,0...) custom-call(bf16[120,240]{1,0:T(8,128)(2,1)} %convert_bitcast_fusion.2.refs_0_, ...), custom_call_target="tpu_custom_call" | custom-call | tf_op jit(solution)/shard_map/front/pallas_call | solution.py:713
  153.6 1.0 copy.54.gain
  154.6 46.8 %middle.1 = (bf16[960,512]{1,0:T(8,128)(2,1)}, f32[960,512]{1,0:T(8,128)}, f32[960,1]{1,0:T(8,128)}, bf16[2,4,960,640]{3,2,1,0:T(8,128)(2,1)}, bf16[4,960,640]{2...) custom-call(bf16[960,512]{1,0:T(8,128)(2,1)} %get-tuple-element.46.att, ...), custom_call_target="tpu_custom_call" | custom-call | tf_op jit(solution)/shard_map/middle/pallas_call | solution.py:820
  201.4 190.9 %back.1 = (f32[120,640]{1,0:T(8,128)}, f32[240,640]{1,0:T(8,128)}, f32[120,240]{1,0:T(8,128)}, bf16[1600,512]{1,0:T(8,128)(2,1)}) custom-call(bf16[4,2,2,2,120,640]{5,4,3,2,1,0:T(8,128)(2,1)} %bitcast.43, bf16[2,2,2,4,240,640]{5,4,3,2,1,0:T(8,128)(2,1)} %bitcast.39, bf16[4,2,2,2,120,240]{5,4,3,2,1,0:T(8,128)(2,1)} %bitcast.46, ...), custom_call_target="tpu_custom_call" | custom-call | tf_op jit(solution)/shard_map/back/pallas_call | solution.py:1086
  392.4 0.0 copy-start.7
  392.4 10.7 %ending.1 = (f32[960,512]{1,0:T(8,128)}, f32[960,1]{1,0:T(8,128)}, bf16[4,1600,240]{2,1,0:T(8,128)(2,1)}) custom-call(bf16[1600,512]{1,0:T(8,128)(2,1)} %get-tuple-element.59.hd, bf16[4,1600,240]{2,1,0:T(8,128)(2,1)} %bitcast.38, bf16[960,512]{1,0:T(8,128)(2,1)} %bitcast.42, f32[960,1]{1,0:T(8,128)} %copy.53.refs_5_.gain, f32[960,512]{1,0:T(8,128)} %get-tuple-element.60.rg), custom_call_target="tpu_custom_call" | custom-call | tf_op jit(solution)/shard_map/ending/pallas_call | solution.py:1127
  403.0 1.2 copy.56
  404.3 0.0 copy-done.7
  404.3 0.0 copy-start.16
  404.3 0.0 copy-start.17
  404.3 0.0 copy-start.1
  404.3 0.2 copy.57
  404.5 0.6 maximum_bitcast_fusion.refs_1_
  405.1 38.4 %reduce_grads.1 = (f32[200,240]{1,0:T(8,128)}, f32[2,960]{1,0:T(2,128)}) custom-call(bf16[4,2,2,2,200,240]{5,4,3,2,1,0:T(8,128)(2,1)} %bitcast.45, f32[2,960]{1,0:T(2,128)} %maximum_bitcast_fusion.refs_1_), custom_call_target="tpu_custom_call" | custom-call | tf_op jit(solution)/shard_map/reduce_grads/pallas_call | solution.py:450
  443.5 0.0 copy-start.3
  443.6 0.0 copy-start.9
  443.6 0.0 copy-start.10
  443.6 2.2 multiply_subtract_fusion.2
  445.8 1.3 multiply_subtract_fusion.4
  447.2 2.9 multiply_subtract_fusion
  450.0 1.1 multiply_subtract_fusion.1
  451.1 0.1 copy.58
  451.2 0.0 copy-done.13
  451.2 0.1 copy.59
  451.3 0.1 multiply_subtract_fusion.3
  451.5 0.7 copy.63
  452.2 0.7 copy.64
  453.0 0.7 copy.65
  453.7 0.7 copy.62
  454.5 0.6 copy.70
  455.1 0.7 copy.71
  455.7 0.8 copy.72
  456.6 0.7 copy.73
  (29 shorter events, 0.1 us)
Async XLA Ops:
  0.7 41.7 %copy-start.11 = (f32[240,120]{1,0:T(8,128)S(1)}, f32[240,120]{1,0:T(8,128)}, u32[]{:S(2)}) copy-start(f32[240,120]{1,0:T(8,128)} %param.25) | copy-start | bytes 345604
  3.8 39.4 %copy-start = (f32[240,640]{1,0:T(8,128)S(1)}, f32[240,640]{1,0:T(8,128)}, u32[]{:S(2)}) copy-start(f32[240,640]{1,0:T(8,128)} %param.26) | copy-start | bytes 1843204
  7.5 36.5 %copy-start.2 = (f32[640,120]{0,1:T(8,128)S(1)}, f32[640,120]{0,1:T(8,128)}, u32[]{:S(2)}) copy-start(f32[640,120]{0,1:T(8,128)} %param.27) | copy-start | bytes 921604
  42.5 111.1 %copy-start.4 = (f32[240,120]{0,1:T(8,128)}, f32[240,120]{0,1:T(8,128)S(1)}, u32[]{:S(2)}) copy-start(f32[240,120]{0,1:T(8,128)S(1)} %copy.52) | copy-start | bytes 345604
  392.4 11.9 %copy-start.7 = (f32[960,1]{1,0:T(8,128)S(1)}, f32[960,1]{1,0:T(8,128)}, u32[]{:S(2)}) copy-start(f32[960,1]{1,0:T(8,128)} %get-tuple-element.64) | copy-start | bytes 11524
  404.3 41.5 %copy-start.14 = (f32[2,960]{1,0:T(2,128)S(1)}, f32[2,960]{1,0:T(2,128)}, u32[]{:S(2)}) copy-start(f32[2,960]{1,0:T(2,128)} %param.23) | copy-start | bytes 23044
  404.3 41.5 %copy-start.16 = (f32[2,960]{1,0:T(2,128)S(1)}, f32[2,960]{1,0:T(2,128)}, u32[]{:S(2)}) copy-start(f32[2,960]{1,0:T(2,128)} %param.28) | copy-start | bytes 23044
  404.3 41.5 %copy-start.17 = (f32[2,960]{1,0:T(2,128)S(1)}, f32[2,960]{1,0:T(2,128)}, u32[]{:S(2)}) copy-start(f32[2,960]{1,0:T(2,128)} %param.29) | copy-start | bytes 23044
  404.3 42.8 %copy-start.1 = (f32[240,640]{1,0:T(8,128)S(1)}, f32[240,640]{1,0:T(8,128)}, u32[]{:S(2)}) copy-start(f32[240,640]{1,0:T(8,128)} %get-tuple-element.162) | copy-start | bytes 1843204
  443.5 6.5 %copy-start.3 = (f32[120,640]{1,0:T(8,128)S(1)}, f32[120,640]{1,0:T(8,128)}, u32[]{:S(2)}) copy-start(f32[120,640]{1,0:T(8,128)} %get-tuple-element.69) | copy-start | bytes 921604
  443.6 6.5 %copy-start.9 = (f32[640,120]{0,1:T(8,128)S(1)}, f32[640,120]{0,1:T(8,128)}, u32[]{:S(2)}) copy-start(f32[640,120]{0,1:T(8,128)} %param.36) | copy-start | bytes 921604
  443.6 6.5 %copy-start.10 = (f32[640,120]{0,1:T(8,128)S(1)}, f32[640,120]{0,1:T(8,128)}, u32[]{:S(2)}) copy-start(f32[640,120]{0,1:T(8,128)} %param.37) | copy-start | bytes 921604
  447.1 4.0 copy-start.12
  447.1 4.1 copy-start.13
  447.1 4.2 copy-start.5
  447.1 4.2 copy-start.8
  450.0 4.4 copy-start.15
  450.0 5.0 %copy-start.6 = (f32[200,240]{1,0:T(8,128)S(1)}, f32[200,240]{1,0:T(8,128)}, u32[]{:S(2)}) copy-start(f32[200,240]{1,0:T(8,128)} %get-tuple-element.66) | copy-start | bytes 576004

commit v3 on v2

v3 whole, which is shorter than its diff:
```python
import functools
import math

import jax
import jax.numpy as jnp
from jax import lax
from jax.experimental import pallas as pl
from jax.experimental.pallas import tpu as pltpu
from jax.sharding import PartitionSpec as P

MESH = pl.DeviceIdType.MESH
ANY = pl.BlockSpec(memory_space=pl.ANY)
VMEM = pl.BlockSpec(memory_space=pltpu.VMEM)


class Grid:
    def __init__(self, mesh):
        self.nd = mesh.shape["dp"]
        self.nz = mesh.shape["shard"]
        self.nx = math.isqrt(self.nd // 2)
        self.ny = self.nd // 2 // self.nx
        assert self.nx == self.ny and self.nx * self.ny * 2 == self.nd

    def dp(self, y, x, c):
        return (y * self.nx + x) * 2 + c


class Here:
    def __init__(self, grid):
        self.grid = grid
        d = lax.axis_index("dp")
        self.z = lax.axis_index("shard")
        self.d = d
        self.c = lax.rem(d, 2)
        self.x = lax.rem(d // 2, grid.nx)
        self.y = d // (2 * grid.nx)
        g = grid
        self.xs = [lax.rem(self.x + k, g.nx) for k in range(1, g.nx)]
        self.ys = [lax.rem(self.y + k, g.ny) for k in range(1, g.ny)]
        self.zs = [lax.rem(self.z + k, g.nz) for k in range(1, g.nz)]
        self.partner = (g.dp(self.y, self.x, 1 - self.c), self.z)

    def on_x(self, x):
        return (self.grid.dp(self.y, x, self.c), self.z)

    def on_y(self, y):
        return (self.grid.dp(y, self.x, self.c), self.z)

    def on_z(self, z):
        return (self.d, z)

    def peers(self):
        return (
            [self.partner]
            + [self.on_x(x) for x in self.xs]
            + [self.on_y(y) for y in self.ys]
            + [self.on_z(z) for z in self.zs]
        )


def greet(peers):
    barrier = pltpu.get_barrier_semaphore()
    for peer in peers:
        pl.semaphore_signal(barrier, inc=1, device_id=peer, device_id_type=MESH)
    pl.semaphore_wait(barrier, len(peers))


def send(src, dst, send_sem, recv_sem, device):
    pltpu.make_async_remote_copy(
        src_ref=src,
        dst_ref=dst,
        send_sem=send_sem,
        recv_sem=recv_sem,
        device_id=device,
        device_id_type=MESH,
    ).start()


def wait_bytes(ref, sem):
    pltpu.make_async_copy(ref, ref, sem).wait()


def half_rows(rows):
    return max(16, int(rows / 32 + 0.5) * 16)


def chunks_of(rows, size=64):
    starts = list(range(0, rows, size))
    if len(starts) > 1 and rows - starts[-1] < size // 2:
        starts.pop()
    return [(start, stop - start) for start, stop in zip(starts, starts[1:] + [rows])]


class Gather:
    def __init__(self, here, shard, out, sems, z_major, rows):
        self.h, self.shard, self.out, self.sems, self.z_major = here, shard, out, sems, z_major
        self.start, self.rows = rows
        self.cut = half_rows(self.rows)

    def span(self, half=None):
        if half is None:
            return pl.ds(self.start, self.rows)
        return pl.ds(self.start, self.cut) if half == 0 else pl.ds(self.start + self.cut, self.rows - self.cut)

    def column(self, d, half=None):
        return self.out.at[:, d, self.span(half)] if self.z_major else self.out.at[d, :, self.span(half)]

    def block(self, d, z):
        return self.out.at[z, d, self.span()] if self.z_major else self.out.at[d, z, self.span()]

    def columns(self, count):
        some = pl.ds(0, count)
        return self.out.at[:, some, self.span()] if self.z_major else self.out.at[some, :, self.span()]

    def blocks(self, count):
        some = pl.ds(0, count)
        return self.out.at[some, 0, self.span()] if self.z_major else self.out.at[0, some, self.span()]

    def own(self):
        h = self.h
        return pltpu.make_async_copy(self.shard.at[self.span()], self.block(h.d, h.z), self.sems.at[8])

    def stage_z(self):
        h, s = self.h, self.sems
        for z in h.zs:
            send(self.shard.at[self.span()], self.block(h.d, h.z), s.at[0], s.at[1], h.on_z(z))
        self.own().start()

    def stage_one(self):
        h, s = self.h, self.sems
        wait_bytes(self.blocks(len(h.zs)), s.at[1])
        self.own().wait()
        for x in h.xs:
            send(self.column(h.d, 0), self.column(h.d, 0), s.at[2], s.at[3], h.on_x(x))
        for y in h.ys:
            send(self.column(h.d, 1), self.column(h.d, 1), s.at[2], s.at[3], h.on_y(y))
        send(self.column(h.d), self.column(h.d), s.at[6], s.at[7], h.partner)

    def stage_two(self):
        h, s, g = self.h, self.sems, self.h.grid
        wait_bytes(self.columns(len(h.xs)), s.at[3])
        for y in h.ys:
            for x in [h.x] + h.xs:
                col = self.column(g.dp(h.y, x, h.c), 0)
                send(col, col, s.at[4], s.at[5], h.on_y(y))
        for x in h.xs:
            for y in [h.y] + h.ys:
                col = self.column(g.dp(y, h.x, h.c), 1)
                send(col, col, s.at[4], s.at[5], h.on_x(x))
        for x in h.xs:
            col = self.column(g.dp(h.y, x, h.c), 0)
            send(col, col, s.at[6], s.at[7], h.partner)
        for y in h.ys:
            col = self.column(g.dp(y, h.x, h.c), 1)
            send(col, col, s.at[6], s.at[7], h.partner)

    def stage_three(self):
        h, s, g = self.h, self.sems, self.h.grid
        wait_bytes(self.columns(g.nx * len(h.ys)), s.at[5])
        for y in h.ys:
            for x in [h.x] + h.xs:
                col = self.column(g.dp(y, x, h.c), 0)
                send(col, col, s.at[6], s.at[7], h.partner)
        for x in h.xs:
            for y in [h.y] + h.ys:
                col = self.column(g.dp(y, x, h.c), 1)
                send(col, col, s.at[6], s.at[7], h.partner)

    def arrive(self):
        g = self.h.grid
        wait_bytes(self.columns(g.nd // 2), self.sems.at[7])

    def drain(self):
        h, s, g = self.h, self.sems, self.h.grid
        wait_bytes(self.blocks(len(h.zs)), s.at[0])
        wait_bytes(self.columns(len(h.xs)), s.at[2])
        wait_bytes(self.columns(g.nx * len(h.ys)), s.at[4])
        wait_bytes(self.columns(g.nd // 2), s.at[6])

    stages = ("stage_z", "stage_one", "stage_two", "stage_three")


def pipelined(jobs, ahead=0):
    ticks = [getattr(job, job.stages[0]) for job in jobs[:ahead]]
    depth = len(jobs[0].stages) if jobs else 0
    for step in range(len(jobs) + depth - 1):
        for k in range(depth):
            i = step - k
            if 0 <= i < len(jobs) and not (k == 0 and i < ahead):
                ticks.append(getattr(jobs[i], jobs[i].stages[k]))
    return ticks


def chunk_list(shards, leads=None):
    pieces = []
    for i, shard in enumerate(shards):
        if leads is not None and leads[i]:
            pieces += [(i, k, (0, shard.shape[-2])) for k in leads[i]]
        else:
            pieces += [(i, None, rows) for rows in chunks_of(shard.shape[-2])]
    return pieces


def piece_of(ref, lead):
    return ref if lead is None else ref.at[lead]


def gather_jobs(here, shards, outs, sems, z_majors, pieces):
    return [
        Gather(here, piece_of(shards[i], lead), piece_of(outs[i], lead), sems.at[k], z_majors[i], rows)
        for k, (i, lead, rows) in enumerate(pieces)
    ]


GATHER_SEMS = 9


def gather_kernel(grid, z_majors, pieces, *refs):
    n = len(z_majors)
    shards, outs, sems = refs[:n], refs[n : 2 * n], refs[2 * n]
    here = Here(grid)
    greet(here.peers())
    jobs = gather_jobs(here, shards, outs, sems, z_majors, pieces)
    for tick in pipelined(jobs, len(jobs)):
        tick()
    for job in jobs:
        job.arrive()
        job.drain()


def gather_weights(grid, shards, z_majors, collective_id):
    shapes = []
    for shard, z_major in zip(shards, z_majors):
        lead = (grid.nz, grid.nd) if z_major else (grid.nd, grid.nz)
        shapes.append(jax.ShapeDtypeStruct(lead + shard.shape, shard.dtype))
    pieces = chunk_list(shards)
    return pl.pallas_call(
        functools.partial(gather_kernel, grid, tuple(z_majors), pieces),
        out_shape=shapes,
        in_specs=[VMEM] * len(shards),
        out_specs=[ANY] * len(shards),
        scratch_shapes=[pltpu.SemaphoreType.DMA((len(pieces), GATHER_SEMS))],
        compiler_params=pltpu.CompilerParams(collective_id=collective_id, has_side_effects=True),
        name="gather_weights",
    )(*shards)


class Reduce:
    def __init__(self, here, terms, result, bufs, sems, z_major, rows):
        self.h, self.terms, self.result, self.sems, self.z_major = here, terms, result, sems, z_major
        self.own, self.other, self.one_a, self.one_b, self.two_a, self.two_b, self.last = bufs
        self.start, self.rows = rows
        self.cut = half_rows(self.rows)

    @staticmethod
    def scratch(grid, rows, cols, z_major):
        cut = half_rows(rows)
        ny, nx, nz = grid.ny, grid.nx, grid.nz
        full = (nz, ny, nx) if z_major else (ny, nx, nz)
        row = (nz, nx) if z_major else (nx, nz)
        bf = jnp.bfloat16
        return [
            pltpu.VMEM(full + (rows, cols), bf),
            pltpu.VMEM(full + (rows, cols), bf),
            pltpu.VMEM((ny,) + row + (cut, cols), bf),
            pltpu.VMEM((nx,) + row + (rows - cut, cols), bf),
            pltpu.VMEM((nx, nz, cut, cols), bf),
            pltpu.VMEM((ny, nz, rows - cut, cols), bf),
            pltpu.VMEM((nz, rows, cols), bf),
        ]

    def span(self, half):
        return {None: slice(None), 0: pl.ds(0, self.cut), 1: pl.ds(self.cut, self.rows - self.cut)}[half]

    def at(self, y, x, z, half):
        y, x, z = (slice(None) if v is None else v for v in (y, x, z))
        return (z, y, x, self.span(half)) if self.z_major else (y, x, z, self.span(half))

    def side(self, c):
        rows = pl.ds(self.start, self.rows)
        return self.terms.at[:, :, :, c, rows] if self.z_major else self.terms.at[:, :, c, :, rows]

    def load(self):
        return pltpu.make_async_copy(self.side(self.h.c), self.own, self.sems.at[8])

    def stage_core(self):
        h, s = self.h, self.sems
        send(self.side(1 - h.c), self.other, s.at[0], s.at[1], h.partner)
        self.load().start()

    def add_loop(self, shape, body):
        total = math.prod(shape)

        def step(i, carry):
            place = []
            rest = i
            for size in reversed(shape):
                place.append(lax.rem(rest, size))
                rest = rest // size
            body(tuple(reversed(place)))
            return carry

        lax.fori_loop(0, total, step, 0)

    def stage_one(self):
        h, s, g = self.h, self.sems, self.h.grid
        self.load().wait()
        wait_bytes(self.other, s.at[1])

        def body(place):
            self.own[place] = self.own[place] + self.other[place]

        self.add_loop(self.own.shape[:3], body)
        for y in h.ys:
            send(self.own.at[self.at(y, None, None, 0)], self.one_a.at[h.y], s.at[2], s.at[3], h.on_y(y))
        for x in h.xs:
            send(self.own.at[self.at(None, x, None, 1)], self.one_b.at[h.x], s.at[9], s.at[10], h.on_x(x))

    def stage_two(self):
        h, s, g = self.h, self.sems, self.h.grid
        wait_bytes(self.one_a.at[pl.ds(0, g.ny - 1)], s.at[3])
        wait_bytes(self.one_b.at[pl.ds(0, g.nx - 1)], s.at[10])

        def body_a(place):
            where = (place[1], place[0]) if self.z_major else place
            spot = self.at(h.y, where[0], where[1], 0)
            total = self.own[spot].astype(jnp.float32)
            for y in h.ys:
                total += self.one_a[(y,) + place].astype(jnp.float32)
            self.own[spot] = total.astype(jnp.bfloat16)

        self.add_loop(self.one_a.shape[1:3], body_a)

        def body_b(place):
            where = (place[1], place[0]) if self.z_major else place
            spot = self.at(where[0], h.x, where[1], 1)
            total = self.own[spot].astype(jnp.float32)
            for x in h.xs:
                total += self.one_b[(x,) + place].astype(jnp.float32)
            self.own[spot] = total.astype(jnp.bfloat16)

        self.add_loop(self.one_b.shape[1:3], body_b)
        for x in h.xs:
            send(self.own.at[self.at(h.y, x, None, 0)], self.two_a.at[h.x], s.at[4], s.at[5], h.on_x(x))
        for y in h.ys:
            send(self.own.at[self.at(y, h.x, None, 1)], self.two_b.at[h.y], s.at[11], s.at[12], h.on_y(y))

    def stage_three(self):
        h, s, g = self.h, self.sems, self.h.grid
        wait_bytes(self.two_a.at[pl.ds(0, g.nx - 1)], s.at[5])
        wait_bytes(self.two_b.at[pl.ds(0, g.ny - 1)], s.at[12])

        def body(place):
            (z,) = place
            spot = self.at(h.y, h.x, z, 0)
            total = self.own[spot].astype(jnp.float32)
            for x in h.xs:
                total += self.two_a[x, z].astype(jnp.float32)
            self.own[spot] = total.astype(jnp.bfloat16)
            spot = self.at(h.y, h.x, z, 1)
            total = self.own[spot].astype(jnp.float32)
            for y in h.ys:
                total += self.two_b[y, z].astype(jnp.float32)
            self.own[spot] = total.astype(jnp.bfloat16)

        self.add_loop((g.nz,), body)
        for z in h.zs:
            send(self.own.at[self.at(h.y, h.x, z, None)], self.last.at[h.z], s.at[6], s.at[7], h.on_z(z))

    def finish(self):
        h, s, g = self.h, self.sems, self.h.grid
        wait_bytes(self.last.at[pl.ds(0, g.nz - 1)], s.at[7])
        total = self.own[self.at(h.y, h.x, h.z, None)].astype(jnp.float32)
        for z in h.zs:
            total += self.last[z].astype(jnp.float32)
        self.result[pl.ds(self.start, self.rows)] = total

    stages = ("stage_core", "stage_one", "stage_two", "stage_three", "finish")

    def drain(self):
        g, s = self.h.grid, self.sems
        wait_bytes(self.other, s.at[0])
        wait_bytes(self.one_a.at[pl.ds(0, g.ny - 1)], s.at[2])
        wait_bytes(self.one_b.at[pl.ds(0, g.nx - 1)], s.at[9])
        wait_bytes(self.two_a.at[pl.ds(0, g.nx - 1)], s.at[4])
        wait_bytes(self.two_b.at[pl.ds(0, g.ny - 1)], s.at[11])
        wait_bytes(self.last.at[pl.ds(0, g.nz - 1)], s.at[6])


REDUCE_SEMS = 13
REDUCE_BUFS = 7


class Share:
    def __init__(self, here, value, result, bufs, sems):
        self.h, self.value, self.result, self.sems = here, value, result, sems
        self.bufs = bufs

    @staticmethod
    def scratch(grid, shape):
        return [pltpu.VMEM((n,) + shape, jnp.float32) for n in (2, grid.nx, grid.ny, grid.nz)]

    def axis(self, k):
        h = self.h
        return (
            (h.c, [h.partner], 2),
            (h.x, [h.on_x(x) for x in h.xs], h.grid.nx),
            (h.y, [h.on_y(y) for y in h.ys], h.grid.ny),
            (h.z, [h.on_z(z) for z in h.zs], h.grid.nz),
        )[k]

    def start(self, k):
        me, peers, n = self.axis(k)
        self.bufs[k][me] = self.value[...] if k == 0 else self.total
        for peer in peers:
            send(self.bufs[k].at[me], self.bufs[k].at[me], self.sems.at[2 * k], self.sems.at[2 * k + 1], peer)

    def end(self, k):
        me, peers, n = self.axis(k)
        wait_bytes(self.bufs[k].at[pl.ds(0, n - 1)], self.sems.at[2 * k + 1])
        total = self.bufs[k][0]
        for i in range(1, n):
            total = total + self.bufs[k][i]
        self.total = total
        if k == 3:
            self.result[...] = total

    def drain(self):
        for k in range(4):
            n = self.axis(k)[2]
            wait_bytes(self.bufs[k].at[pl.ds(0, n - 1)], self.sems.at[2 * k])


SHARE_SEMS = 8


def reduce_kernel(grid, z_majors, pieces, shared, *refs):
    n = len(z_majors)
    terms, refs = refs[:n], refs[n:]
    value, refs = (refs[0], refs[1:]) if shared else (None, refs)
    results, refs = refs[:n], refs[n:]
    value_sum, refs = (refs[0], refs[1:]) if shared else (None, refs)
    here = Here(grid)
    greet(here.peers())
    jobs, refs = reduce_jobs(here, terms, results, refs, z_majors, pieces)
    share = None
    if shared:
        share = Share(here, value, value_sum, refs[:4], refs[4])
        share.start(0)
    ticks = pipelined(jobs, len(jobs))
    for k, tick in enumerate(ticks):
        tick()
        if share is not None and k >= len(jobs) and k - len(jobs) < 4:
            step = k - len(jobs)
            share.end(step)
            if step < 3:
                share.start(step + 1)
    if share is not None:
        share.drain()
    for job in jobs:
        job.drain()


def reduce_jobs(here, terms, results, refs, z_majors, pieces):
    n = len(pieces)
    sems = refs[n * REDUCE_BUFS]
    jobs = []
    for k, (i, lead, rows) in enumerate(pieces):
        bufs = refs[k * REDUCE_BUFS : (k + 1) * REDUCE_BUFS]
        term, result = piece_of(terms[i], lead), piece_of(results[i], lead)
        jobs.append(Reduce(here, term, result, bufs, sems.at[k], z_majors[i], rows))
    return jobs, refs[n * REDUCE_BUFS + 1 :]


def reduce_scratch(grid, terms, z_majors, pieces):
    scratch = []
    for i, _, (_, rows) in pieces:
        scratch += Reduce.scratch(grid, rows, terms[i].shape[-1], z_majors[i])
    return scratch + [pltpu.SemaphoreType.DMA((max(len(pieces), 1), REDUCE_SEMS))]


def split_terms(grid, terms, z_majors):
    split = []
    for term, z_major in zip(terms, z_majors):
        lead = (grid.ny, grid.nx, 2)
        lead = (grid.nz,) + lead if z_major else lead + (grid.nz,)
        split.append(term.reshape(term.shape[:-4] + lead + term.shape[-2:]))
    return split


def reduce_grads(grid, terms, z_majors, value, collective_id):
    shapes = [jax.ShapeDtypeStruct(term.shape[-2:], jnp.float32) for term in terms]
    pieces = chunk_list(terms)
    scratch = reduce_scratch(grid, terms, z_majors, pieces)
    n = len(terms)
    shared = value is not None
    if shared:
        shapes.append(jax.ShapeDtypeStruct(value.shape, jnp.float32))
        scratch += Share.scratch(grid, value.shape)
        scratch.append(pltpu.SemaphoreType.DMA((SHARE_SEMS,)))
    return pl.pallas_call(
        functools.partial(reduce_kernel, grid, tuple(z_majors), pieces, shared),
        out_shape=shapes,
        in_specs=[ANY] * n + [VMEM] * shared,
        out_specs=[VMEM] * len(shapes),
        scratch_shapes=scratch,
        compiler_params=pltpu.CompilerParams(
            collective_id=collective_id, has_side_effects=True, vmem_limit_bytes=62 << 20
        ),
        name="reduce_grads",
    )(*split_terms(grid, terms, z_majors), *([value] if shared else []))


D = 960
QUERY_HEADS = 15
KEY_VALUE_HEADS = 5
GROUP = QUERY_HEADS // KEY_VALUE_HEADS
HEAD = 64
FF = 2560
QKV = (QUERY_HEADS + 2 * KEY_VALUE_HEADS) * HEAD
ADAM_STEP = 10
DOCS = 16
HIDE = -1e30
VALUE_SCALE = 2.0**-9

norm_epsilon = 1e-05
beta_one = 0.9
beta_two = 0.95
adam_epsilon = 1e-08
matrix_rate = 0.03
output_rate = 0.15
gain_rate = 0.5
decay_rate = 0.1

f32 = jnp.float32
bf16 = jnp.bfloat16
DEPTH = 4
SLICE = D // DEPTH


def mm(a, b):
    return lax.dot_general(a, b, (((1,), (0,)), ((), ())), preferred_element_type=f32)


def mm_nt(a, b):
    return lax.dot_general(a, b, (((1,), (1,)), ((), ())), preferred_element_type=f32)


def mm_tn(a, b):
    return lax.dot_general(a, b, (((0,), (0,)), ((), ())), preferred_element_type=f32)


def lanes_below(shape, n):
    return lax.broadcasted_iota(jnp.int32, shape, len(shape) - 1) < n


def inverse_rms(ref):
    total = jnp.zeros((1, ref.shape[1]), f32)
    for k in range(DEPTH):
        x = ref[pl.ds(k * SLICE, SLICE)].astype(f32)
        total += jnp.sum(x * x, axis=0, keepdims=True)
    return lax.rsqrt(total * (1.0 / D) + norm_epsilon)


def three_pieces(row):
    hi = row.astype(bf16).astype(f32)
    mid = (row - hi).astype(bf16).astype(f32)
    low = row - hi - mid
    place = lax.broadcasted_iota(jnp.int32, (16, row.shape[1]), 0)
    block = jnp.where(place == 0, hi, jnp.where(place == 1, mid, jnp.where(place == 2, low, 0.0)))
    return block.astype(bf16)


class KeyChain:
    def __init__(self, here, kv, sems):
        self.h, self.kv, self.sems = here, kv, sems

    def up(self, slot):
        h = self.h
        to = lax.rem(h.z + 1, h.grid.nz)

        @pl.when(h.z < h.grid.nz - 1)
        def _():
            send(self.kv.at[slot], self.kv.at[slot], self.sems.at[0, slot], self.sems.at[1, slot], h.on_z(to))

    def take(self, slot):
        wait_bytes(self.kv.at[slot], self.sems.at[1, slot])
        self.up(slot)

    def drain(self):
        h = self.h
        for s in range(h.grid.nz):

            @pl.when(jnp.logical_and(h.z >= s, h.z < h.grid.nz - 1))
            def _():
                wait_bytes(self.kv.at[h.z - s], self.sems.at[0, h.z - s])


def front_kernel(grid, z_majors, pieces, *refs):
    n = len(z_majors)
    shards, refs = refs[:n], refs[n:]
    heads, x, gain, cos, sin, qext, kext = refs[:7]
    refs = refs[7:]
    outs, refs = refs[:n], refs[n:]
    qx, qn, kv, att = refs[:4]
    h1, proj, kx, vt, acc, sems, kv_sems = refs[4:]
    here = Here(grid)
    tokens = x.shape[1]
    half = tokens // 2
    greet(here.peers())
    jobs = gather_jobs(here, shards, outs, sems, z_majors, pieces)
    ticks = pipelined(jobs, 3)
    for tick in ticks[:3]:
        tick()

    inverse = inverse_rms(x)
    for k in range(DEPTH):
        rows = pl.ds(k * SLICE, SLICE)
        h1[rows] = (x[rows].astype(f32) * inverse * gain[rows]).astype(bf16)

    part = QKV // 5

    def project(m, carry):
        rows = pl.ds(pl.multiple_of(m * part, 16), part)
        total = mm(heads[0, rows], h1[pl.ds(0, SLICE)])
        for k in range(1, DEPTH):
            total += mm(heads[k, rows], h1[pl.ds(k * SLICE, SLICE)])
        proj[rows] = total
        return carry

    lax.fori_loop(0, 5, project, 0)

    def turned(h):
        base = h * HEAD
        a = proj[pl.ds(pl.multiple_of(base, 8), HEAD // 2)]
        b = proj[pl.ds(pl.multiple_of(base + HEAD // 2, 8), HEAD // 2)]
        c, s = cos[...], sin[...]
        return a * c - b * s, b * c + a * s

    def keys(g, carry):
        a, b = turned(QUERY_HEADS + g)
        v = proj[pl.ds(pl.multiple_of((QUERY_HEADS + KEY_VALUE_HEADS + g) * HEAD, 8), HEAD)]
        both = jnp.concatenate([a, b, v], axis=0)
        kv[here.z, g] = both.T.astype(bf16)
        return carry

    lax.fori_loop(0, KEY_VALUE_HEADS, keys, 0)
    chain = KeyChain(here, kv, kv_sems)
    chain.up(here.z)

    def queries(h, carry):
        a, b = turned(h)
        scale = HEAD**-0.5
        qx[h, pl.ds(0, 32)] = (a.astype(bf16).astype(f32) * scale).astype(bf16)
        qx[h, pl.ds(32, 32)] = (b.astype(bf16).astype(f32) * scale).astype(bf16)
        qx[h, pl.ds(64, 64)] = qext[...]
        qn[h] = qx[h].astype(f32).T.astype(bf16)
        return carry

    lax.fori_loop(0, QUERY_HEADS, queries, 0)

    def prepare(slot):
        ext = kext[pl.ds(pl.multiple_of(slot * tokens, 16), tokens)]

        def body(g, carry):
            block = kv[slot, g]
            kx[g] = jnp.where(lanes_below(block.shape, HEAD), block, ext)
            turned_block = block.astype(f32).T
            vt[g, pl.ds(0, 16)] = jnp.ones((16, tokens), bf16)
            vt[g, pl.ds(16, HEAD)] = (turned_block[HEAD:] * VALUE_SCALE).astype(bf16)
            return carry

        lax.fori_loop(0, KEY_VALUE_HEADS, body, 0)

    def below(shape, shift):
        return lax.broadcasted_iota(jnp.int32, shape, 0) <= lax.broadcasted_iota(jnp.int32, shape, 1) + shift

    def diagonal(g):
        for i in range(GROUP):
            h = g * GROUP + i
            s = mm(kx[g, pl.ds(0, half)], qx[h, :, pl.ds(0, half)])
            p = jnp.exp(jnp.where(below(s.shape, 0), s, HIDE)).astype(bf16)
            acc[h, :, pl.ds(0, half)] = mm(vt[g, :, pl.ds(0, half)], p)
            s = mm(kx[g], qx[h, :, pl.ds(half, half)])
            p = jnp.exp(jnp.where(below(s.shape, half), s, HIDE)).astype(bf16)
            acc[h, :, pl.ds(half, half)] = mm(vt[g], p)

    def whole(g):
        for i in range(GROUP):
            h = g * GROUP + i
            for k in range(2):
                cols = pl.ds(k * half, half)
                p = jnp.exp(mm(kx[g], qx[h, :, cols])).astype(bf16)
                acc[h, :, cols] += mm(vt[g], p)

    ticks = ticks[3:]

    def micro(t, carry):
        s = t // KEY_VALUE_HEADS
        g = lax.rem(t, KEY_VALUE_HEADS)

        @pl.when(s <= here.z)
        def _():
            slot = here.z - s

            @pl.when(g == 0)
            def _():
                @pl.when(s > 0)
                def _():
                    chain.take(slot)

                prepare(slot)

            @pl.when(s == 0)
            def _():
                diagonal(g)

            @pl.when(s > 0)
            def _():
                whole(g)

        for k, tick in enumerate(ticks):
            pl.when(t == k * micros // len(ticks))(tick)
        return carry

    micros = grid.nz * KEY_VALUE_HEADS
    lax.fori_loop(0, micros, micro, 0)

    def close(h, carry):
        totals = acc[h, pl.ds(0, 1)]
        scale = (1.0 / VALUE_SCALE) / totals
        att[pl.ds(pl.multiple_of(h * HEAD, 16), HEAD)] = (acc[h, pl.ds(16, HEAD)] * scale).astype(bf16)
        qx[h, pl.ds(HEAD + DOCS, 16)] = three_pieces(-jnp.log(totals))
        return carry

    lax.fori_loop(0, QUERY_HEADS, close, 0)
    for job in jobs:
        job.arrive()
        job.drain()
    chain.drain()


def front(grid, shards, z_majors, leads, heads, x, gain, cos, sin, qext, kext, collective_id):
    tokens = x.shape[1]
    shapes = []
    for shard, z_major, chosen in zip(shards, z_majors, leads):
        lead = (grid.nz, grid.nd) if z_major else (grid.nd, grid.nz)
        lead = (len(chosen),) + lead if chosen else lead
        shapes.append(jax.ShapeDtypeStruct(lead + shard.shape[-2:], shard.dtype))
    n = len(shards)
    pieces = chunk_list(shards, leads)
    shapes += [
        jax.ShapeDtypeStruct((QUERY_HEADS, 128, tokens), bf16),
        jax.ShapeDtypeStruct((QUERY_HEADS, tokens, 128), bf16),
        jax.ShapeDtypeStruct((grid.nz, KEY_VALUE_HEADS, tokens, 128), bf16),
        jax.ShapeDtypeStruct((D, tokens), bf16),
    ]
    return pl.pallas_call(
        functools.partial(front_kernel, grid, tuple(z_majors), pieces),
        out_shape=shapes,
        in_specs=[VMEM] * (n + 7),
        out_specs=[ANY] * n + [VMEM] * 4,
        scratch_shapes=[
            pltpu.VMEM((D, tokens), bf16),
            pltpu.VMEM((QKV, tokens), f32),
            pltpu.VMEM((KEY_VALUE_HEADS, tokens, 128), bf16),
            pltpu.VMEM((KEY_VALUE_HEADS, 80, tokens), bf16),
            pltpu.VMEM((QUERY_HEADS, 80, tokens), f32),
            pltpu.SemaphoreType.DMA((max(len(pieces), 1), GATHER_SEMS)),
            pltpu.SemaphoreType.DMA((2, grid.nz)),
        ],
        compiler_params=pltpu.CompilerParams(
            collective_id=collective_id, has_side_effects=True, vmem_limit_bytes=60 << 20
        ),
        name="front",
    )(*shards, heads, x, gain, cos, sin, qext, kext)


STEPS = 5
WIDTH = 128
PARTS = 6


def middle_kernel(grid, ready, summed, *refs):
    att, wo, x, ogt, gain, exp_in, dn_in = refs[:7]
    refs = refs[7:]
    late = STEPS - ready
    if late:
        shard, refs = refs[0], refs[1:]
    out, rg, gsum, dwo, dox, dexp, ddn = refs[:7]
    refs = refs[7:]
    if late:
        exp_late, refs = refs[0], refs[1:]
    if summed:
        gexp, refs = refs[0], refs[1:]
    (res, inv, h2, h2t, og, acc_o, acc_h, mixed, dgate, dup, wg, wu, wd, sg, sd, w_sems, o_sems) = refs[:17]
    refs = refs[17:]
    tokens = x.shape[1]
    half = 2 * WIDTH
    schedule = {}
    gathers, sums = [], []
    if late or summed:
        here = Here(grid)
        greet(here.peers())
    if late:
        pieces = [(0, k, (0, SLICE)) for k in range(late)]
        g_sems, refs = refs[0], refs[1:]
        gathers = [
            Gather(here, shard.at[ready + k], exp_late.at[k], g_sems.at[k], False, (0, SLICE)) for k in range(late)
        ]
        for job in gathers:
            job.stage_z()
        for k, job in enumerate(gathers):
            for i, stage in enumerate(job.stages[1:]):
                schedule.setdefault(5 * i + 2 * k, []).append(getattr(job, stage))
            schedule.setdefault((ready + k - 1) * PARTS + 1, []).append(job.arrive)
    if summed:
        pieces = [(0, k, (0, SLICE)) for k in range(summed)]
        sums, refs = reduce_jobs(here, [dexp], [gexp], refs, (False,), pieces)
        for k, job in enumerate(sums):
            for i, stage in enumerate(job.stages):
                place = min((k + 1) * PARTS + 3 + 4 * i, STEPS * PARTS - 1)
                schedule.setdefault(place, []).append(getattr(job, stage))

    def fetch_from(source, index, step, slot, go):
        for d in range(4):
            lanes = pl.ds(d * WIDTH, WIDTH)
            go(pltpu.make_async_copy(source.at[index, d], wg.at[slot, :, :, lanes], w_sems.at[slot, 0]))
            go(pltpu.make_async_copy(source.at[index, 4 + d], wu.at[slot, :, :, lanes], w_sems.at[slot, 1]))
            columns = pl.ds(pl.multiple_of(step * WIDTH, WIDTH), WIDTH)
            go(pltpu.make_async_copy(dn_in.at[d, :, columns], wd.at[slot, :, lanes], w_sems.at[slot, 2]))

    def fetch(step):
        slot = lax.rem(step, 2)

        @pl.when(step < ready)
        def _():
            fetch_from(exp_in, step, step, slot, lambda copy: copy.start())

        if late:

            @pl.when(step >= ready)
            def _():
                fetch_from(exp_late, step - ready, step, slot, lambda copy: copy.start())

    def put_expand(step, go):
        for k in range(2):
            for d in range(4):
                lanes = pl.ds(d * WIDTH, WIDTH)
                to = dexp.at[step, 4 * k + d] if not sums_split else dexp.at[(step,) + sums_place(4 * k + d)]
                go(pltpu.make_async_copy(sg.at[k, :, :, lanes], to, o_sems.at[0]))

    def put_down(step, go):
        for d in range(4):
            columns = pl.ds(pl.multiple_of(step * WIDTH, WIDTH), WIDTH)
            go(pltpu.make_async_copy(sd.at[:, pl.ds(d * WIDTH, WIDTH)], ddn.at[d, :, columns], o_sems.at[1]))

    sums_split = len(dexp.shape) == 7

    def sums_place(d):
        return (d // (2 * grid.nx), d // 2 % grid.nx, d % 2)

    fetch(jnp.int32(0))
    total = jnp.zeros((1, tokens), f32)
    for m in range(DEPTH):
        rows = pl.ds(m * SLICE, SLICE)
        r = x[rows].astype(f32)
        for k in range(DEPTH):
            r += mm(wo[k, rows], att[pl.ds(k * SLICE, SLICE)])
        res[rows] = r
        total += jnp.sum(r * r, axis=0, keepdims=True)
    inverse = lax.rsqrt(total * (1.0 / D) + norm_epsilon)
    inv[...] = inverse
    for m in range(DEPTH):
        rows = pl.ds(m * SLICE, SLICE)
        h2t[rows] = (res[rows] * inverse * gain[rows]).astype(bf16)
    h2[...] = h2t[...].astype(f32).T.astype(bf16)
    og[...] = ogt[...].astype(f32).T.astype(bf16)
    acc_o[...] = jnp.zeros_like(acc_o)
    acc_h[...] = jnp.zeros_like(acc_h)

    def activate(slot, k):
        cols = pl.ds(k * half, half)
        gate = mm(h2[...], wg[slot, :, :, cols].reshape(D, half))
        up = mm(h2[...], wu[slot, :, :, cols].reshape(D, half))
        back = mm(og[...], wd[slot, :, cols])
        s = 1.0 / (1.0 + jnp.exp(-gate))
        silu = gate * s
        mixed[:, cols] = (silu * up).astype(bf16)
        dgate[:, cols] = (back * up * s * (1.0 + gate * (1.0 - s))).astype(bf16)
        dup[:, cols] = (back * silu).astype(bf16)

    def micro(t, carry):
        step = t // PARTS
        part = lax.rem(t, PARTS)
        slot = lax.rem(step, 2)

        for place, ticks in schedule.items():

            @pl.when(t == place)
            def _():
                for tick in ticks:
                    tick()

        @pl.when(part == 0)
        def _():
            wait_bytes(wg.at[slot], w_sems.at[slot, 0])
            wait_bytes(wu.at[slot], w_sems.at[slot, 1])
            wait_bytes(wd.at[slot], w_sems.at[slot, 2])
            activate(slot, 0)

        @pl.when(part == 1)
        def _():
            @pl.when(step > 0)
            def _():
                wait_bytes(sg, o_sems.at[0])
                wait_bytes(sd, o_sems.at[1])

            pl.when(step + 1 < STEPS)(lambda: fetch(step + 1))
            activate(slot, 1)

        @pl.when(part == 2)
        def _():
            acc_o[...] += mm_nt(wd[slot], mixed[...])

        @pl.when(part == 3)
        def _():
            for m in range(DEPTH):
                sg[0, m] = mm(h2t[pl.ds(m * SLICE, SLICE)], dgate[...]).astype(bf16)
                sg[1, m] = mm(h2t[pl.ds(m * SLICE, SLICE)], dup[...]).astype(bf16)
            put_expand(step, lambda copy: copy.start())

        @pl.when(part == 4)
        def _():
            sd[...] = mm(ogt[...], mixed[...]).astype(bf16)
            put_down(step, lambda copy: copy.start())

        @pl.when(part == 5)
        def _():
            acc_h[...] += mm_nt(wg[slot].reshape(D, 2 * half), dgate[...])
            acc_h[...] += mm_nt(wu[slot].reshape(D, 2 * half), dup[...])

        return carry

    lax.fori_loop(0, STEPS * PARTS, micro, 0)
    wait_bytes(sg, o_sems.at[0])
    wait_bytes(sd, o_sems.at[1])
    inverse = inv[...]
    total = jnp.zeros((1, tokens), f32)
    for m in range(DEPTH):
        rows = pl.ds(m * SLICE, SLICE)
        out[rows] = (res[rows] + acc_o[rows]).astype(bf16)
        normed = res[rows] * inverse
        up = acc_h[rows]
        gsum[rows] = jnp.sum(up * normed, axis=1, keepdims=True)
        total += jnp.sum(up * gain[rows] * normed, axis=0, keepdims=True)
    mean = total * (1.0 / D)
    for m in range(DEPTH):
        rows = pl.ds(m * SLICE, SLICE)
        normed = res[rows] * inverse
        r = ogt[rows].astype(f32) + inverse * (acc_h[rows] * gain[rows] - normed * mean)
        rg[rows] = r
        h2t[rows] = r.astype(bf16)
    for k in range(DEPTH):
        rows = pl.ds(k * SLICE, SLICE)
        dwo[k] = mm_nt(h2t[...], att[rows]).astype(bf16)
        acc_h[rows] = mm_tn(wo[k], h2t[...])

    def rows_of(h, carry):
        rows = pl.ds(pl.multiple_of(h * HEAD, 16), HEAD)
        grad = acc_h[rows].astype(bf16)
        dox[h, pl.ds(HEAD, HEAD)] = grad
        delta = jnp.sum(grad.astype(f32) * att[rows].astype(f32), axis=0, keepdims=True)
        dox[h, pl.ds(0, 16)] = three_pieces(-delta)
        dox[h, pl.ds(16, 48)] = jnp.zeros((48, tokens), bf16)
        return carry

    lax.fori_loop(0, QUERY_HEADS, rows_of, 0)
    for job in gathers + sums:
        job.drain()


def middle(grid, att, wo, x, ogt, gain, expand, down, shard, summed, collective_id):
    tokens = x.shape[1]
    ready = expand.shape[0]
    late = STEPS - ready
    blocks = expand.shape[1:]
    if summed:
        grads = (STEPS, grid.ny, grid.nx, 2) + blocks[1:]
    else:
        grads = (STEPS,) + blocks
    shapes = [
        jax.ShapeDtypeStruct((D, tokens), bf16),
        jax.ShapeDtypeStruct((D, tokens), f32),
        jax.ShapeDtypeStruct((D, 1), f32),
        jax.ShapeDtypeStruct((DEPTH, D, SLICE), bf16),
        jax.ShapeDtypeStruct((QUERY_HEADS, 128, tokens), bf16),
        jax.ShapeDtypeStruct(grads, bf16),
        jax.ShapeDtypeStruct(down.shape, bf16),
    ]
    out_specs = [VMEM] * 5 + [ANY] * 2
    inputs = [att, wo, x, ogt, gain, expand, down]
    in_specs = [VMEM] * 5 + [ANY] * 2
    scratch = [
        pltpu.VMEM((D, tokens), f32),
        pltpu.VMEM((1, tokens), f32),
        pltpu.VMEM((tokens, D), bf16),
        pltpu.VMEM((D, tokens), bf16),
        pltpu.VMEM((tokens, D), bf16),
        pltpu.VMEM((D, tokens), f32),
        pltpu.VMEM((D, tokens), f32),
        pltpu.VMEM((tokens, 4 * WIDTH), bf16),
        pltpu.VMEM((tokens, 4 * WIDTH), bf16),
        pltpu.VMEM((tokens, 4 * WIDTH), bf16),
        pltpu.VMEM((2, DEPTH, SLICE, 4 * WIDTH), bf16),
        pltpu.VMEM((2, DEPTH, SLICE, 4 * WIDTH), bf16),
        pltpu.VMEM((2, D, 4 * WIDTH), bf16),
        pltpu.VMEM((2, DEPTH, SLICE, 4 * WIDTH), bf16),
        pltpu.VMEM((D, 4 * WIDTH), bf16),
        pltpu.SemaphoreType.DMA((2, 3)),
        pltpu.SemaphoreType.DMA((2,)),
    ]
    if late:
        inputs.append(shard)
        in_specs.append(VMEM)
        shapes.append(jax.ShapeDtypeStruct((late,) + blocks, bf16))
        out_specs.append(ANY)
        scratch.append(pltpu.SemaphoreType.DMA((late, GATHER_SEMS)))
    if summed:
        shapes.append(jax.ShapeDtypeStruct((summed,) + blocks[2:], f32))
        out_specs.append(VMEM)
        pieces = [(0, k, (0, SLICE)) for k in range(summed)]
        term = jax.ShapeDtypeStruct(blocks, bf16)
        scratch += reduce_scratch(grid, [term], (False,), pieces)
    params = dict(collective_id=collective_id, has_side_effects=True) if late or summed else {}
    return pl.pallas_call(
        functools.partial(middle_kernel, grid, ready, summed),
        out_shape=shapes,
        in_specs=in_specs,
        out_specs=out_specs,
        scratch_shapes=scratch,
        compiler_params=pltpu.CompilerParams(vmem_limit_bytes=62 << 20, **params),
        name="middle",
    )(*inputs)


class GradChain:
    def __init__(self, here, part, sent, got, sems):
        self.h, self.part, self.sent, self.got, self.sems = here, part, sent, got, sems

    def summed(self, slot, g, write):
        h = self.h

        @pl.when(h.z < h.grid.nz - 1)
        def _():
            wait_bytes(self.got.at[slot, g], self.sems.at[1, slot, g])
            write(g, self.part[slot, g] + self.got[slot, g].astype(f32))

        @pl.when(h.z == h.grid.nz - 1)
        def _():
            write(g, self.part[slot, g])

    def relay(self, slot, g):
        h = self.h

        def write(g, value):
            self.sent[slot, g] = value.astype(bf16)

        self.summed(slot, g, write)
        to = lax.rem(h.z + h.grid.nz - 1, h.grid.nz)
        sems = self.sems
        send(self.sent.at[slot, g], self.got.at[slot, g], sems.at[0, slot, g], sems.at[1, slot, g], h.on_z(to))

    def drain(self):
        h = self.h

        def body(t, carry):
            slot, g = t // KEY_VALUE_HEADS, lax.rem(t, KEY_VALUE_HEADS)
            wait_bytes(self.sent.at[slot, g], self.sems.at[0, slot, g])
            return carry

        lax.fori_loop(0, h.z * KEY_VALUE_HEADS, body, 0)


def back_kernel(grid, z_majors, pieces, *refs):
    n = len(z_majors)
    terms, refs = refs[:n], refs[n:]
    qx, qn, dox, kv, kext, cos, sin = refs[:7]
    refs = refs[7:]
    results, refs = refs[:n], refs[n:]
    hd, refs = refs[0], refs[1:]
    here = Here(grid)
    jobs, refs = reduce_jobs(here, terms, results, refs, z_majors, pieces)
    don, kx, vx, kt, dq, part, sent, got, kv_sems = refs
    tokens = dox.shape[2]
    half = tokens // 2
    greet(here.peers())
    ticks = pipelined(jobs, len(jobs))
    for tick in ticks[: len(jobs)]:
        tick()
    ticks = ticks[len(jobs) :]

    def gather_queries(h, carry):
        dq[h] = jnp.zeros((HEAD, tokens), f32)
        don[h] = dox[h].astype(f32).T.astype(bf16)
        return carry

    lax.fori_loop(0, QUERY_HEADS, gather_queries, 0)

    def prepare(slot):
        ext = kext[pl.ds(pl.multiple_of(slot * tokens, 16), tokens)]

        def body(g, carry):
            block = kv[slot, g]
            low = lanes_below(block.shape, HEAD)
            kx[g] = jnp.where(low, block, ext)
            ones = jnp.where(lanes_below(block.shape, 3), 1.0, 0.0).astype(bf16)
            vx[g] = jnp.where(low, ones, block)
            kt[g] = block.astype(f32).T[:HEAD].astype(bf16)
            return carry

        lax.fori_loop(0, KEY_VALUE_HEADS, body, 0)

    def tile(g, h, count, k, masked):
        keys, cols = pl.ds(0, count), pl.ds(k * half, half)
        s = mm(kx[g, keys], qx[h, :, cols])
        if masked:
            row = lax.broadcasted_iota(jnp.int32, s.shape, 0)
            col = lax.broadcasted_iota(jnp.int32, s.shape, 1) + k * half
            s = jnp.where(row <= col, s, HIDE)
        p = jnp.exp(s)
        ds = (p * mm(vx[g, keys], dox[h, :, cols])).astype(bf16)
        dq[h, :, cols] += mm(kt[g, :, keys], ds)
        dk = mm(ds, qn[h, cols])
        dv = mm(p.astype(bf16), don[h, cols])
        return jnp.where(lanes_below(dk.shape, HEAD), dk, dv)

    def whole(slot, g):
        total = None
        for i in range(GROUP):
            for k in range(2):
                new = tile(g, g * GROUP + i, tokens, k, False)
                total = new if total is None else total + new
        part[slot, g] = total

    def diagonal(g):
        total = None
        for i in range(GROUP):
            new = tile(g, g * GROUP + i, tokens, 1, True)
            total = new if total is None else total + new
        part[here.z, g] = total
        total = part[here.z, g, pl.ds(0, half)]
        for i in range(GROUP):
            total += tile(g, g * GROUP + i, half, 0, True)
        part[here.z, g, pl.ds(0, half)] = total

    chain = GradChain(here, part, sent, got, kv_sems)
    micros = grid.nz * KEY_VALUE_HEADS
    top = here.z == grid.nz - 1

    def micro(t, carry):
        slot = t // KEY_VALUE_HEADS
        g = lax.rem(t, KEY_VALUE_HEADS)

        @pl.when(slot <= here.z)
        def _():
            pl.when(g == 0)(lambda: prepare(slot))

            @pl.when(slot < here.z)
            def _():
                whole(slot, g)
                pl.when(top)(lambda: chain.relay(slot, g))

            pl.when(slot == here.z)(lambda: diagonal(g))

        @pl.when(jnp.logical_and(jnp.logical_not(top), jnp.logical_and(slot >= 1, slot <= here.z)))
        def _():
            chain.relay(slot - 1, g)

        for k, tick in enumerate(ticks):
            pl.when(t == k * micros // len(ticks))(tick)
        return carry

    lax.fori_loop(0, micros, micro, 0)

    def turn_back(a, b):
        c, s = cos[...], sin[...]
        return a * c + b * s, b * c - a * s

    def queries(h, carry):
        scale = HEAD**-0.5
        a, b = turn_back(dq[h, pl.ds(0, 32)] * scale, dq[h, pl.ds(32, 32)] * scale)
        hd[pl.ds(pl.multiple_of(h * HEAD, 16), 32)] = a.astype(bf16)
        hd[pl.ds(pl.multiple_of(h * HEAD + 32, 16), 32)] = b.astype(bf16)
        return carry

    lax.fori_loop(0, QUERY_HEADS, queries, 0)

    def write(g, value):
        turned = value.T
        a, b = turn_back(turned[:32], turned[32:64])
        base = (QUERY_HEADS + g) * HEAD
        hd[pl.ds(pl.multiple_of(base, 16), 32)] = a.astype(bf16)
        hd[pl.ds(pl.multiple_of(base + 32, 16), 32)] = b.astype(bf16)
        base = (QUERY_HEADS + KEY_VALUE_HEADS + g) * HEAD
        hd[pl.ds(pl.multiple_of(base, 16), HEAD)] = turned[64:].astype(bf16)

    def close(g, carry):
        chain.summed(here.z, g, write)
        return carry

    lax.fori_loop(0, KEY_VALUE_HEADS, close, 0)
    chain.drain()
    for job in jobs:
        job.drain()


def back(grid, terms, z_majors, leads, qx, qn, dox, kv, kext, cos, sin, collective_id):
    tokens = dox.shape[2]
    n = len(terms)
    pieces = chunk_list(terms, leads)
    shapes = []
    for term, chosen in zip(terms, leads):
        lead = (term.shape[0],) if chosen else ()
        shapes.append(jax.ShapeDtypeStruct(lead + term.shape[-2:], f32))
    scratch = reduce_scratch(grid, terms, z_majors, pieces)
    shapes.append(jax.ShapeDtypeStruct((QKV, tokens), bf16))
    blocks = (grid.nz, KEY_VALUE_HEADS, tokens, 128)
    scratch += [
        pltpu.VMEM((QUERY_HEADS, tokens, 128), bf16),
        pltpu.VMEM((KEY_VALUE_HEADS, tokens, 128), bf16),
        pltpu.VMEM((KEY_VALUE_HEADS, tokens, 128), bf16),
        pltpu.VMEM((KEY_VALUE_HEADS, HEAD, tokens), bf16),
        pltpu.VMEM((QUERY_HEADS, HEAD, tokens), f32),
        pltpu.VMEM(blocks, f32),
        pltpu.VMEM((grid.nz - 1,) + blocks[1:], bf16),
        pltpu.VMEM(blocks, bf16),
        pltpu.SemaphoreType.DMA((2, grid.nz, KEY_VALUE_HEADS)),
    ]
    return pl.pallas_call(
        functools.partial(back_kernel, grid, tuple(z_majors), pieces),
        out_shape=shapes,
        in_specs=[ANY] * n + [VMEM] * 7,
        out_specs=[VMEM] * (n + 1),
        scratch_shapes=scratch,
        compiler_params=pltpu.CompilerParams(
            collective_id=collective_id, has_side_effects=True, vmem_limit_bytes=63 << 20
        ),
        name="back",
    )(*split_terms(grid, terms, z_majors), qx, qn, dox, kv, kext, cos, sin)


def adamw(weight, grad, first, second, rate, decay):
    first_new = beta_one * first + (1.0 - beta_one) * grad
    second_new = beta_two * second + (1.0 - beta_two) * grad * grad
    first_hat = first_new / (1.0 - beta_one**ADAM_STEP)
    second_hat = second_new / (1.0 - beta_two**ADAM_STEP)
    weight_new = weight - rate * (
        first_hat / (jnp.sqrt(second_hat) + adam_epsilon) + decay * weight
    )
    return (weight_new, first_new, second_new)


def finish_kernel(grid, pieces, *refs):
    hd, heads, x, gain, rg, gain_two, ig, gheads, ggains, h1, og, flat, wide, terms, value = refs[:15]
    here = Here(grid)
    greet(here.peers())
    jobs, refs = reduce_jobs(here, [terms], [gheads], refs[15:], (True,), pieces)
    share = Share(here, value, ggains, refs[:4], refs[4])
    tokens = x.shape[1]
    inverse = inverse_rms(x)
    for k in range(DEPTH):
        rows = pl.ds(k * SLICE, SLICE)
        h1[rows] = (x[rows].astype(f32) * inverse * gain[rows]).astype(bf16)
    rows = terms.shape[-2]
    for k in range(DEPTH):
        flat[...] = mm_nt(hd[...], h1[pl.ds(k * SLICE, SLICE)])
        for d in range(grid.nd):
            place = (k, d // (2 * grid.nx), d // 2 % grid.nx, d % 2)
            terms[place] = flat[pl.ds(d * rows, rows)].astype(bf16)
    ticks = pipelined(jobs, len(jobs))
    for tick in ticks[: len(jobs)]:
        tick()
    ticks = ticks[len(jobs) :]

    def turn(count=1):
        for _ in range(count):
            if ticks:
                ticks.pop(0)()

    for k in range(DEPTH):
        og[pl.ds(k * SLICE, SLICE)] = mm_tn(heads[k], hd[...])
        if k == 1:
            turn()
    turn()
    total = jnp.zeros((1, tokens), f32)
    for k in range(DEPTH):
        rows = pl.ds(k * SLICE, SLICE)
        normed = x[rows].astype(f32) * inverse
        column = jnp.sum(og[rows] * normed, axis=1, keepdims=True)
        place = lax.broadcasted_iota(jnp.int32, (SLICE, 128), 1)
        wide[rows] = jnp.where(place == 0, column, jnp.where(place == 1, gain_two[rows], 0.0))
        total += jnp.sum(og[rows] * gain[rows] * normed, axis=0, keepdims=True)
    value[...] = wide[...].T[:8]
    share.start(0)
    turn()
    mean = total * (1.0 / D)
    for k in range(DEPTH):
        rows = pl.ds(k * SLICE, SLICE)
        normed = x[rows].astype(f32) * inverse
        ig[rows] = rg[rows] + inverse * (og[rows] * gain[rows] - normed * mean)
    turn()
    for k in range(4):
        share.end(k)
        if k < 3:
            share.start(k + 1)
        turn(2)
    turn(len(ticks))
    share.drain()
    for job in jobs:
        job.drain()


def finish(grid, hd, heads, x, gain, rg, gain_two, collective_id):
    tokens = x.shape[1]
    rows = QKV // grid.nd
    term = jax.ShapeDtypeStruct((rows, SLICE), bf16)
    pieces = chunk_list([term])
    scratch = [
        pltpu.VMEM((D, tokens), bf16),
        pltpu.VMEM((D, tokens), f32),
        pltpu.VMEM((QKV, SLICE), f32),
        pltpu.VMEM((D, 128), f32),
        pltpu.VMEM((grid.nz, grid.ny, grid.nx, 2, rows, SLICE), bf16),
        pltpu.VMEM((8, D), f32),
    ]
    scratch += reduce_scratch(grid, [term], (True,), pieces)
    scratch += Share.scratch(grid, (8, D))
    scratch.append(pltpu.SemaphoreType.DMA((SHARE_SEMS,)))
    return pl.pallas_call(
        functools.partial(finish_kernel, grid, pieces),
        out_shape=[
            jax.ShapeDtypeStruct((D, tokens), f32),
            jax.ShapeDtypeStruct((rows, SLICE), f32),
            jax.ShapeDtypeStruct((8, D), f32),
        ],
        in_specs=[VMEM] * 6,
        out_specs=[VMEM] * 3,
        scratch_shapes=scratch,
        compiler_params=pltpu.CompilerParams(
            collective_id=collective_id, has_side_effects=True, vmem_limit_bytes=62 << 20
        ),
        name="finish",
    )(hd, heads, x, gain, rg, gain_two)


READY = 3
SUMMED = 1


def local(
    grid,
    hidden_in,
    out_grad,
    seg_ids,
    doc_start,
    norm_gains,
    heads_weight,
    output_weight,
    expand_weight,
    down_weight,
    gains_first,
    gains_second,
    heads_first,
    heads_second,
    output_first,
    output_second,
    expand_first,
    expand_second,
    down_first,
    down_second,
):
    tokens = hidden_in.shape[0]
    first_row = lax.axis_index("shard") * tokens
    positions = first_row + jnp.arange(tokens, dtype=jnp.int32)
    freq = jnp.power(10000.0, -jnp.arange(HEAD // 2).astype(f32) / (HEAD // 2))
    angle = (positions - doc_start).astype(f32)[None, :] * freq[:, None]
    cos, sin = jnp.cos(angle), jnp.sin(angle)
    seg_row = seg_ids[0]
    seg_query = lax.dynamic_slice_in_dim(seg_row, first_row, tokens)
    doc = jnp.arange(HEAD, dtype=jnp.int32)
    qext = jnp.where((doc[:, None] < DOCS) & (seg_query[None, :] == doc[:, None]), HIDE, 0.0).astype(bf16)
    lane = jnp.arange(128, dtype=jnp.int32) - HEAD
    other_doc = (lane[None, :] >= 0) & (lane[None, :] < DOCS) & (seg_row[:, None] != lane[None, :])
    kext = jnp.where(other_doc | ((lane >= DOCS) & (lane < DOCS + 3))[None, :], 1.0, 0.0).astype(bf16)
    x, ogt = hidden_in.T, out_grad.T
    gain_one, gain_two = norm_gains[0][:, None], norm_gains[1][:, None]

    (heads_stack,) = gather_weights(grid, [heads_weight.astype(bf16).T], (True,), 1)
    heads = heads_stack.reshape(DEPTH, QKV, SLICE)
    expand_half = expand_weight.astype(bf16)
    stepped = expand_half.shape[1] == STEPS * WIDTH
    if stepped:
        shard = expand_half.reshape(SLICE, STEPS, WIDTH).transpose(1, 0, 2)
        leads = [None, None, list(range(READY))]
    else:
        shard, leads = expand_half, [None, None, None]
    shards = [output_weight.astype(bf16).T, down_weight.astype(bf16).T, shard]
    output_stack, down_stack, expand_stack, qx, qn, kv, att = front(
        grid, shards, (True, True, False), leads, heads, x, gain_one, cos, sin, qext, kext, 2
    )
    wo = output_stack.reshape(DEPTH, D, SLICE)
    down = down_stack.reshape(DEPTH, D, FF // DEPTH)
    blocks = (8, DEPTH, SLICE)
    if stepped:
        late = middle(grid, att, wo, x, ogt, gain_two, expand_stack, down, shard, SUMMED, 5)
        out, rg, gain_two_term, dwo, dox, dexpand, ddn, _, early_exp = late
    else:
        expand = expand_stack.transpose(1, 2, 0, 3).reshape(DEPTH, SLICE, 8, STEPS, WIDTH)
        expand = expand.transpose(3, 2, 0, 1, 4)
        out, rg, gain_two_term, dwo, dox, dexpand, ddn = middle(
            grid, att, wo, x, ogt, gain_two, expand, down, None, 0, 5
        )
        early_exp = None
        dexpand = dexpand.transpose(2, 3, 1, 0, 4).reshape(DEPTH, SLICE, grid.nd, -1).transpose(2, 0, 1, 3)
    if stepped:
        dexpand = dexpand.reshape((STEPS, grid.nd, grid.nz, SLICE, WIDTH))
    terms = [ddn.reshape(down_stack.shape), dexpand, dwo.reshape(output_stack.shape)]
    leads = [None, list(range(SUMMED, STEPS)) if stepped else None, None]
    down_grad, late_exp, output_grad, hd = back(
        grid, terms, (True, False, True), leads, qx, qn, dox, kv, kext, cos, sin, 3
    )
    ig, heads_grad, gains_grad = finish(grid, hd, heads, x, gain_one, rg, gain_two_term, 4)
    if stepped:
        steps = [(early_exp if k < SUMMED else late_exp)[k] for k in range(STEPS)]
        expand_grad = jnp.concatenate(steps, axis=1)
    else:
        expand_grad = late_exp
    heads_grad, output_grad, down_grad, gains_grad = heads_grad.T, output_grad.T, down_grad.T, gains_grad[:2]
    hidden_out, input_grad = out.T, ig.T
    gains_new, gains_first_new, gains_second_new = adamw(
        norm_gains, gains_grad, gains_first, gains_second, gain_rate, 0.0
    )
    heads_new, heads_first_new, heads_second_new = adamw(
        heads_weight, heads_grad, heads_first, heads_second, matrix_rate, decay_rate
    )
    output_new, output_first_new, output_second_new = adamw(
        output_weight, output_grad, output_first, output_second, output_rate, decay_rate
    )
    expand_new, expand_first_new, expand_second_new = adamw(
        expand_weight, expand_grad, expand_first, expand_second, matrix_rate, decay_rate
    )
    down_new, down_first_new, down_second_new = adamw(
        down_weight, down_grad, down_first, down_second, matrix_rate, decay_rate
    )
    return (
        hidden_out,
        input_grad,
        gains_grad,
        heads_grad,
        output_grad,
        expand_grad,
        down_grad,
        gains_new,
        heads_new,
        output_new,
        expand_new,
        down_new,
        gains_first_new,
        gains_second_new,
        heads_first_new,
        heads_second_new,
        output_first_new,
        output_second_new,
        expand_first_new,
        expand_second_new,
        down_first_new,
        down_second_new,
    )


def solution(mesh):
    return jax.shard_map(
        functools.partial(local, Grid(mesh)),
        mesh=mesh,
        in_specs=(
            P(("dp", "shard"), None),
            P(("dp", "shard"), None),
            P("dp", None),
            P(("dp", "shard")),
            P(),
            P("shard", "dp"),
            P("shard", "dp"),
            P("shard", "dp"),
            P("shard", "dp"),
            P(),
            P(),
            P("shard", "dp"),
            P("shard", "dp"),
            P("shard", "dp"),
            P("shard", "dp"),
            P("shard", "dp"),
            P("shard", "dp"),
            P("shard", "dp"),
            P("shard", "dp"),
        ),
        out_specs=(
            P(("dp", "shard"), None),
            P(("dp", "shard"), None),
            P(),
            P("shard", "dp"),
            P("shard", "dp"),
            P("shard", "dp"),
            P("shard", "dp"),
            P(),
            P("shard", "dp"),
            P("shard", "dp"),
            P("shard", "dp"),
            P("shard", "dp"),
            P(),
            P(),
            P("shard", "dp"),
            P("shard", "dp"),
            P("shard", "dp"),
            P("shard", "dp"),
            P("shard", "dp"),
            P("shard", "dp"),
            P("shard", "dp"),
            P("shard", "dp"),
        ),
        check_vma=False,
    )
```

time: 458 us -> 383 us (0.84)
  Pallas kernels: 429 us -> 344 us
  local copies, waits for them, and re-layouts: 11.1 us -> 20.1 us
    pallas_call x6 -> x5, Pallas kernels: 429 us -> 344 us  [the longest x1 107 us: back(): pl.pallas_call(functools.partial(back_kernel, grid, tuple(z_majors), piec...]
    unnamed x47 -> x55, local copies, waits for them, and re-layouts: 6.17 us -> 14.6 us
where the time goes in v3:
time: 383 us; the launch traced here: 382 us
  Pallas kernels  344 us (90%)
  local copies, waits for them, and re-layouts  20.1 us (5%)
  other arithmetic  16.7 us (4%)
    pallas_call x1, Pallas kernels, back(): pl.pallas_call(functools.partial(back_kernel, grid, tuple(z_majors), piec...  107 us
    pallas_call x1, Pallas kernels, front(): pl.pallas_call(functools.partial(front_kernel, grid, tuple(z_majors), pie...  95.9 us
    pallas_call x1, Pallas kernels, middle(): pl.pallas_call(functools.partial(middle_kernel, grid, ready, summed), out...  73.6 us
    pallas_call x1, Pallas kernels, finish(): pl.pallas_call(functools.partial(finish_kernel, grid, pieces), out_shape=...  37.2 us
    pallas_call x1, Pallas kernels, gather_weights(): pl.pallas_call(functools.partial(gather_kernel, grid, tuple(z_majors), pi...  30.3 us
    unnamed x55, local copies, waits for them, and re-layouts  14.6 us
    sub x5, other arithmetic, adamw(): weight - rate * (first_hat / (jnp.sqrt(second_hat) + adam_epsilon) + deca...  9.45 us

profile of v3, /device:TPU:0, one launch (start us, length us, event | category | flops | bytes accessed | tf_op | source)
XLA Modules:
  0.0 382.0 jit_solution(5920129548450262562)
XLA Ops:
  0.7 0.7 constant_dynamic-slice_fusion
  1.4 0.7 select_convert_fusion.1.refs_8_
  2.1 0.7 subtract_convert_fusion
  2.8 1.0 multiply_sine_fusion
  3.7 1.8 select_convert_fusion.refs_9_.refs_7_
  5.6 0.8 slice_bitcast_fusion
  6.4 1.0 copy.53.refs_5_.refs_3_
  7.4 1.6 convert_bitcast_fusion.1.refs_0_
  9.0 30.3 %gather_weights.1 = bf16[4,8,200,240]{3,2,1,0:T(8,128)(2,1)} custom-call(bf16[200,240]{1,0:T(8,128)(2,1)} %convert_bitcast_fusion.1.refs_0_), custom_call_target="tpu_custom_call" | custom-call | tf_op jit(solution)/shard_map/gather_weights/pallas_call | solution.py:237
  39.3 0.0 copy-start.2
  39.4 0.2 copy.51
  39.6 0.9 copy.52
  40.5 0.1 copy.50
  40.6 0.0 copy-start.4
  40.6 0.7 convert_bitcast_fusion.2.refs_0_
  41.2 0.7 convert_bitcast_fusion.refs_1_
  41.9 95.9 %front.1 = (bf16[4,8,120,240]{3,2,1,0:T(8,128)(2,1)}, bf16[4,8,120,640]{3,2,1,0:T(8,128)(2,1)}, bf16[3,8,4,240,128]{4,3,2,1,0:T(8,128)(2,1)}, bf16[15,128,512]{2...) custom-call(bf16[120,240]{1,0:T(8,128)(2,1)} %convert_bitcast_fusion.2, ...), custom_call_target="tpu_custom_call" | custom-call | tf_op jit(solution)/shard_map/front/pallas_call | solution.py:758
  137.8 1.0 copy.54.refs_4_
  138.8 73.6 %middle.1 = (bf16[960,512]{1,0:T(8,128)(2,1)}, f32[960,512]{1,0:T(8,128)}, f32[960,1]{1,0:T(8,128)}, bf16[4,960,240]{2,1,0:T(8,128)(2,1)}, bf16[15,128,512]{2,1,...) custom-call(bf16[960,512]{1,0:T(8,128)(2,1)} %get-tuple-element.44.r, ...), custom_call_target="tpu_custom_call" | custom-call | tf_op jit(solution)/shard_map/middle/pallas_call | solution.py:1036
  212.4 107.4 %back.1 = (f32[120,640]{1,0:T(8,128)}, f32[5,240,128]{2,1,0:T(8,128)}, f32[120,240]{1,0:T(8,128)}, bf16[1600,512]{1,0:T(8,128)(2,1)}) custom-call(bf16[4,2,2,2,120,640]{5,4,3,2,1,0:T(8,128)(2,1)} %bitcast.47, bf16[5,2,2,2,4,240,128]{6,5,4,3,2,1,0:T(8,128)(2,1)} %get-tuple-element.50.refs_1_, bf16[4,2,2,2,120,240]{5,4,3,2,1,0:T(8,128)(2,1)} %bitcast.52, ...), custom_call_target="tpu_custom_call" | custom-call | tf_op jit(solution)/shard_map/back/pallas_call | solution.py:1240
  319.8 0.9 bitcast_dynamic-update-slice_fusion.4
  320.7 0.9 bitcast_dynamic-update-slice_fusion.3
  321.6 0.9 bitcast_dynamic-update-slice_fusion.2
  322.6 0.9 bitcast_dynamic-update-slice_fusion.1
  323.5 0.9 bitcast_dynamic-update-slice_fusion
  324.4 0.0 copy-start.7
  324.4 3.0 multiply_subtract_fusion
  327.4 0.0 copy-start.17
  327.4 0.0 copy-start.18
  327.5 0.0 copy-start.19
  327.5 0.0 copy-start.11
  327.5 37.2 %finish.1 = (f32[960,512]{1,0:T(8,128)}, f32[200,240]{1,0:T(8,128)}, f32[8,960]{1,0:T(8,128)}) custom-call(bf16[1600,512]{1,0:T(8,128)(2,1)} %get-tuple-element.56.refs_0_, bf16[4,1600,240]{2,1,0:T(8,128)(2,1)} %bitcast.43, bf16[960,512]{1,0:T(8,128)(2,1)} %bitcast.46, f32[960,1]{1,0:T(8,128)} %copy.53.refs_5_.refs_3_, ...), custom_call_target="tpu_custom_call" | custom-call | tf_op jit(solution)/shard_map/finish/pallas_call | solution.py:1340
  364.7 0.0 copy-start.16
  364.7 0.0 copy-start.5
  364.7 2.0 multiply_subtract_fusion.2
  366.8 1.4 multiply_subtract_fusion.4
  368.2 1.1 multiply_subtract_fusion.1
  369.3 0.7 copy.56
  370.0 0.7 copy.57
  370.8 1.9 multiply_subtract_fusion.3
  372.7 1.6 copy.61
  374.3 1.6 copy.62
  376.0 1.6 copy.63
  377.6 0.7 copy.60
  378.4 0.9 copy.72
  379.4 1.3 copy.73
  380.6 0.7 copy.74
  381.3 0.7 copy.75
  (36 shorter events, 0.1 us)
Async XLA Ops:
  7.4 32.0 %copy-start = (f32[240,640]{1,0:T(8,128)S(1)}, f32[240,640]{1,0:T(8,128)}, u32[]{:S(2)}) copy-start(f32[240,640]{1,0:T(8,128)} %param.26) | copy-start | bytes 1843204
  9.0 31.4 %copy-start.14 = (f32[240,120]{1,0:T(8,128)S(1)}, f32[240,120]{1,0:T(8,128)}, u32[]{:S(2)}) copy-start(f32[240,120]{1,0:T(8,128)} %param.25) | copy-start | bytes 345604
  39.3 1.9 copy-start.2
  40.6 97.3 %copy-start.4 = (f32[240,120]{0,1:T(8,128)}, f32[240,120]{0,1:T(8,128)S(1)}, u32[]{:S(2)}) copy-start(f32[240,120]{0,1:T(8,128)S(1)} %copy.50) | copy-start | bytes 345604
  324.4 3.0 copy-start.7
  327.4 37.3 %copy-start.8 = (f32[240,200]{0,1:T(8,128)S(1)}, f32[240,200]{0,1:T(8,128)}, u32[]{:S(2)}) copy-start(f32[240,200]{0,1:T(8,128)} %param.24) | copy-start | bytes 576004
  327.4 37.3 %copy-start.13 = (f32[240,200]{0,1:T(8,128)S(1)}, f32[240,200]{0,1:T(8,128)}, u32[]{:S(2)}) copy-start(f32[240,200]{0,1:T(8,128)} %param.30) | copy-start | bytes 576004
  327.4 39.3 %copy-start.17 = (f32[2,960]{1,0:T(2,128)S(1)}, f32[2,960]{1,0:T(2,128)}, u32[]{:S(2)}) copy-start(f32[2,960]{1,0:T(2,128)} %param.23) | copy-start | bytes 23044
  327.4 39.3 %copy-start.18 = (f32[2,960]{1,0:T(2,128)S(1)}, f32[2,960]{1,0:T(2,128)}, u32[]{:S(2)}) copy-start(f32[2,960]{1,0:T(2,128)} %param.28) | copy-start | bytes 23044
  327.5 39.3 %copy-start.19 = (f32[2,960]{1,0:T(2,128)S(1)}, f32[2,960]{1,0:T(2,128)}, u32[]{:S(2)}) copy-start(f32[2,960]{1,0:T(2,128)} %param.29) | copy-start | bytes 23044
  327.5 40.7 %copy-start.3 = (f32[120,640]{1,0:T(8,128)S(1)}, f32[120,640]{1,0:T(8,128)}, u32[]{:S(2)}) copy-start(f32[120,640]{1,0:T(8,128)} %get-tuple-element.65) | copy-start | bytes 921604
  327.5 40.7 %copy-start.11 = (f32[640,120]{0,1:T(8,128)S(1)}, f32[640,120]{0,1:T(8,128)}, u32[]{:S(2)}) copy-start(f32[640,120]{0,1:T(8,128)} %param.36) | copy-start | bytes 921604
  327.5 40.7 %copy-start.12 = (f32[640,120]{0,1:T(8,128)S(1)}, f32[640,120]{0,1:T(8,128)}, u32[]{:S(2)}) copy-start(f32[640,120]{0,1:T(8,128)} %param.37) | copy-start | bytes 921604
  364.7 4.6 %copy-start.15 = (f32[240,120]{1,0:T(8,128)S(1)}, f32[240,120]{1,0:T(8,128)}, u32[]{:S(2)}) copy-start(f32[240,120]{1,0:T(8,128)} %param.32) | copy-start | bytes 345604
  364.7 5.3 %copy-start.16 = (f32[240,120]{1,0:T(8,128)S(1)}, f32[240,120]{1,0:T(8,128)}, u32[]{:S(2)}) copy-start(f32[240,120]{1,0:T(8,128)} %param.33) | copy-start | bytes 345604
  364.7 6.0 %copy-start.5 = (f32[240,120]{0,1:T(8,128)S(1)}, f32[240,120]{0,1:T(8,128)}, u32[]{:S(2)}) copy-start(f32[240,120]{0,1:T(8,128)} %copy-done.4) | copy-start | bytes 345604
  369.2 8.4 %copy-start.10 = (f32[120,240]{1,0:T(8,128)S(1)}, f32[120,240]{1,0:T(8,128)}, u32[]{:S(2)}) copy-start(f32[120,240]{1,0:T(8,128)} %get-tuple-element.62) | copy-start | bytes 345604
  369.3 9.1 %copy-start.6 = (bf16[960,512]{1,0:T(8,128)(2,1)S(1)}, bf16[960,512]{1,0:T(8,128)(2,1)}, u32[]{:S(2)}) copy-start(bf16[960,512]{1,0:T(8,128)(2,1)} %get-tuple-element.48) | copy-start | bytes 2949124
  370.8 8.6 %copy-start.1 = (f32[960,512]{1,0:T(8,128)S(1)}, f32[960,512]{1,0:T(8,128)}, u32[]{:S(2)}) copy-start(f32[960,512]{1,0:T(8,128)} %get-tuple-element.59) | copy-start | bytes 5898244
  379.3 1.3 copy-start.9

commit v4 on v3

--- a/solution.py
+++ b/solution.py
@@ -126,9 +126,15 @@
             send(self.shard.at[self.span()], self.block(h.d, h.z), s.at[0], s.at[1], h.on_z(z))
         self.own().start()
 
+    def await_z(self):
+        wait_bytes(self.blocks(len(self.h.zs)), self.sems.at[1])
+
+    def drain_z(self):
+        wait_bytes(self.blocks(len(self.h.zs)), self.sems.at[0])
+
     def stage_one(self):
         h, s = self.h, self.sems
-        wait_bytes(self.blocks(len(h.zs)), s.at[1])
+        self.await_z()
         self.own().wait()
         for x in h.xs:
             send(self.column(h.d, 0), self.column(h.d, 0), s.at[2], s.at[3], h.on_x(x))
@@ -172,7 +178,7 @@
 
     def drain(self):
         h, s, g = self.h, self.sems, self.h.grid
-        wait_bytes(self.blocks(len(h.zs)), s.at[0])
+        self.drain_z()
         wait_bytes(self.columns(len(h.xs)), s.at[2])
         wait_bytes(self.columns(g.nx * len(h.ys)), s.at[4])
         wait_bytes(self.columns(g.nd // 2), s.at[6])
@@ -180,13 +186,47 @@
     stages = ("stage_z", "stage_one", "stage_two", "stage_three")
 
 
+class ColumnGather(Gather):
+    def own(self):
+        return pltpu.make_async_copy(self.shard.at[:, self.span()], self.column(self.h.d), self.sems.at[8])
+
+    def stage_z(self):
+        self.own().start()
+
+    def await_z(self):
+        pass
+
+    def drain_z(self):
+        pass
+
+
+class Spread:
+    def __init__(self, here, shard, out, sems):
+        self.h, self.shard, self.out, self.sems = here, shard, out, sems
+
+    def own(self):
+        return pltpu.make_async_copy(self.shard, self.out.at[self.h.z], self.sems.at[2])
+
+    def begin(self):
+        h, s = self.h, self.sems
+        for z in h.zs:
+            send(self.shard, self.out.at[h.z], s.at[0], s.at[1], h.on_z(z))
+        self.own().start()
+
+    def end(self):
+        some = self.out.at[pl.ds(0, len(self.h.zs))]
+        wait_bytes(some, self.sems.at[1])
+        wait_bytes(some, self.sems.at[0])
+        self.own().wait()
+
+
 def pipelined(jobs, ahead=0):
     ticks = [getattr(job, job.stages[0]) for job in jobs[:ahead]]
-    depth = len(jobs[0].stages) if jobs else 0
+    depth = max((len(job.stages) for job in jobs), default=0)
     for step in range(len(jobs) + depth - 1):
         for k in range(depth):
             i = step - k
-            if 0 <= i < len(jobs) and not (k == 0 and i < ahead):
+            if 0 <= i < len(jobs) and k < len(jobs[i].stages) and not (k == 0 and i < ahead):
                 ticks.append(getattr(jobs[i], jobs[i].stages[k]))
     return ticks
 
@@ -206,43 +246,62 @@
 
 
 def gather_jobs(here, shards, outs, sems, z_majors, pieces):
-    return [
-        Gather(here, piece_of(shards[i], lead), piece_of(outs[i], lead), sems.at[k], z_majors[i], rows)
-        for k, (i, lead, rows) in enumerate(pieces)
-    ]
+    jobs = []
+    for k, (i, lead, rows) in enumerate(pieces):
+        kind = ColumnGather if lead is None and len(shards[i].shape) == 3 else Gather
+        job = kind(here, piece_of(shards[i], lead), piece_of(outs[i], lead), sems.at[k], z_majors[i], rows)
+        jobs.append(job)
+    return jobs
 
 
 GATHER_SEMS = 9
 
 
-def gather_kernel(grid, z_majors, pieces, *refs):
+def gather_kernel(grid, z_majors, pieces, spreads, *refs):
     n = len(z_majors)
-    shards, outs, sems = refs[:n], refs[n : 2 * n], refs[2 * n]
+    shards, refs = refs[:n], refs[n:]
+    singles, refs = refs[:spreads], refs[spreads:]
+    outs, refs = refs[:n], refs[n:]
+    columns, refs = refs[:spreads], refs[spreads:]
+    sems, spread_sems = refs
     here = Here(grid)
     greet(here.peers())
     jobs = gather_jobs(here, shards, outs, sems, z_majors, pieces)
-    for tick in pipelined(jobs, len(jobs)):
+    ticks = pipelined(jobs, len(jobs))
+    for tick in ticks[: len(jobs)]:
+        tick()
+    others = [Spread(here, singles[k], columns[k], spread_sems.at[k]) for k in range(spreads)]
+    for other in others:
+        other.begin()
+    for tick in ticks[len(jobs) :]:
         tick()
     for job in jobs:
         job.arrive()
         job.drain()
-
-
-def gather_weights(grid, shards, z_majors, collective_id):
+    for other in others:
+        other.end()
+
+
+def gather_weights(grid, shards, z_majors, singles, collective_id):
     shapes = []
     for shard, z_major in zip(shards, z_majors):
         lead = (grid.nz, grid.nd) if z_major else (grid.nd, grid.nz)
         shapes.append(jax.ShapeDtypeStruct(lead + shard.shape, shard.dtype))
+    for single in singles:
+        shapes.append(jax.ShapeDtypeStruct((grid.nz,) + single.shape, single.dtype))
     pieces = chunk_list(shards)
     return pl.pallas_call(
-        functools.partial(gather_kernel, grid, tuple(z_majors), pieces),
+        functools.partial(gather_kernel, grid, tuple(z_majors), pieces, len(singles)),
         out_shape=shapes,
-        in_specs=[VMEM] * len(shards),
-        out_specs=[ANY] * len(shards),
-        scratch_shapes=[pltpu.SemaphoreType.DMA((len(pieces), GATHER_SEMS))],
+        in_specs=[VMEM] * (len(shards) + len(singles)),
+        out_specs=[ANY] * len(shapes),
+        scratch_shapes=[
+            pltpu.SemaphoreType.DMA((len(pieces), GATHER_SEMS)),
+            pltpu.SemaphoreType.DMA((len(singles), 3)),
+        ],
         compiler_params=pltpu.CompilerParams(collective_id=collective_id, has_side_effects=True),
         name="gather_weights",
-    )(*shards)
+    )(*shards, *singles)
 
 
 class Reduce:
@@ -377,6 +436,9 @@
 
     stages = ("stage_core", "stage_one", "stage_two", "stage_three", "finish")
 
+    def drain_z(self):
+        wait_bytes(self.last.at[pl.ds(0, self.h.grid.nz - 1)], self.sems.at[6])
+
     def drain(self):
         g, s = self.h.grid, self.sems
         wait_bytes(self.other, s.at[0])
@@ -384,7 +446,53 @@
         wait_bytes(self.one_b.at[pl.ds(0, g.nx - 1)], s.at[9])
         wait_bytes(self.two_a.at[pl.ds(0, g.nx - 1)], s.at[4])
         wait_bytes(self.two_b.at[pl.ds(0, g.ny - 1)], s.at[11])
-        wait_bytes(self.last.at[pl.ds(0, g.nz - 1)], s.at[6])
+        self.drain_z()
+
+
+class ColumnReduce(Reduce):
+    stages = ("stage_core", "stage_one", "stage_two", "stage_three")
+
+    def stage_three(self):
+        h, s, g = self.h, self.sems, self.h.grid
+        wait_bytes(self.two_a.at[pl.ds(0, g.nx - 1)], s.at[5])
+        wait_bytes(self.two_b.at[pl.ds(0, g.ny - 1)], s.at[12])
+
+        def body(place):
+            (z,) = place
+            total = self.own[self.at(h.y, h.x, z, 0)].astype(jnp.float32)
+            for x in h.xs:
+                total += self.two_a[x, z].astype(jnp.float32)
+            self.result[z, pl.ds(self.start, self.cut)] = total.astype(jnp.bfloat16)
+            total = self.own[self.at(h.y, h.x, z, 1)].astype(jnp.float32)
+            for y in h.ys:
+                total += self.two_b[y, z].astype(jnp.float32)
+            self.result[z, pl.ds(self.start + self.cut, self.rows - self.cut)] = total.astype(jnp.bfloat16)
+
+        self.add_loop((g.nz,), body)
+
+    def drain_z(self):
+        pass
+
+
+class Collect:
+    def __init__(self, here, column, last, sems):
+        self.h, self.column, self.last, self.sems = here, column, last, sems
+
+    def begin(self):
+        h, s = self.h, self.sems
+        for z in h.zs:
+            send(self.column.at[z], self.last.at[h.z], s.at[0], s.at[1], h.on_z(z))
+
+    def end(self):
+        h = self.h
+        wait_bytes(self.last.at[pl.ds(0, len(h.zs))], self.sems.at[1])
+        total = self.column[h.z].astype(jnp.float32)
+        for z in h.zs:
+            total += self.last[z].astype(jnp.float32)
+        return total
+
+    def drain(self):
+        wait_bytes(self.last.at[pl.ds(0, len(self.h.zs))], self.sems.at[0])
 
 
 REDUCE_SEMS = 13
@@ -467,8 +575,14 @@
     jobs = []
     for k, (i, lead, rows) in enumerate(pieces):
         bufs = refs[k * REDUCE_BUFS : (k + 1) * REDUCE_BUFS]
-        term, result = piece_of(terms[i], lead), piece_of(results[i], lead)
-        jobs.append(Reduce(here, term, result, bufs, sems.at[k], z_majors[i], rows))
+        term, result, kind = piece_of(terms[i], lead), results[i], Reduce
+        deep = len(result.shape) == 3
+        if lead is None:
+            kind = ColumnReduce if deep else Reduce
+        else:
+            width = term.shape[-1]
+            result = result.at[lead] if deep else result.at[:, pl.ds(lead * width, width)]
+        jobs.append(kind(here, term, result, bufs, sems.at[k], z_majors[i], rows))
     return jobs, refs[n * REDUCE_BUFS + 1 :]
 
 
@@ -819,7 +933,7 @@
         sums, refs = reduce_jobs(here, [dexp], [gexp], refs, (False,), pieces)
         for k, job in enumerate(sums):
             for i, stage in enumerate(job.stages):
-                place = min((k + 1) * PARTS + 3 + 4 * i, STEPS * PARTS - 1)
+                place = min((k + 1) * PARTS + 2 + 5 * i, STEPS * PARTS - 1)
                 schedule.setdefault(place, []).append(getattr(job, stage))
 
     def fetch_from(source, index, step, slot, go):
@@ -1082,12 +1196,16 @@
         lax.fori_loop(0, h.z * KEY_VALUE_HEADS, body, 0)
 
 
-def back_kernel(grid, z_majors, pieces, *refs):
+def back_kernel(grid, z_majors, pieces, early, *refs):
     n = len(z_majors)
     terms, refs = refs[:n], refs[n:]
     qx, qn, dox, kv, kext, cos, sin = refs[:7]
     refs = refs[7:]
+    if early:
+        first, refs = refs[0], refs[1:]
     results, refs = refs[:n], refs[n:]
+    for k in range(early):
+        results[1][:, pl.ds(k * WIDTH, WIDTH)] = first[k]
     hd, refs = refs[0], refs[1:]
     here = Here(grid)
     jobs, refs = reduce_jobs(here, terms, results, refs, z_majors, pieces)
@@ -1215,14 +1333,17 @@
         job.drain()
 
 
-def back(grid, terms, z_majors, leads, qx, qn, dox, kv, kext, cos, sin, collective_id):
+def back(grid, terms, z_majors, leads, early, qx, qn, dox, kv, kext, cos, sin, collective_id):
     tokens = dox.shape[2]
     n = len(terms)
     pieces = chunk_list(terms, leads)
     shapes = []
-    for term, chosen in zip(terms, leads):
-        lead = (term.shape[0],) if chosen else ()
-        shapes.append(jax.ShapeDtypeStruct(lead + term.shape[-2:], f32))
+    for k, (term, chosen) in enumerate(zip(terms, leads)):
+        rows, cols = term.shape[-2:]
+        if k == 1:
+            shapes.append(jax.ShapeDtypeStruct((rows, cols * term.shape[0] if chosen else cols), f32))
+        else:
+            shapes.append(jax.ShapeDtypeStruct((grid.nz, rows, cols), bf16))
     scratch = reduce_scratch(grid, terms, z_majors, pieces)
     shapes.append(jax.ShapeDtypeStruct((QKV, tokens), bf16))
     blocks = (grid.nz, KEY_VALUE_HEADS, tokens, 128)
@@ -1238,16 +1359,16 @@
         pltpu.SemaphoreType.DMA((2, grid.nz, KEY_VALUE_HEADS)),
     ]
     return pl.pallas_call(
-        functools.partial(back_kernel, grid, tuple(z_majors), pieces),
+        functools.partial(back_kernel, grid, tuple(z_majors), pieces, 0 if early is None else early.shape[0]),
         out_shape=shapes,
-        in_specs=[ANY] * n + [VMEM] * 7,
+        in_specs=[ANY] * n + [VMEM] * (7 + (early is not None)),
         out_specs=[VMEM] * (n + 1),
         scratch_shapes=scratch,
         compiler_params=pltpu.CompilerParams(
             collective_id=collective_id, has_side_effects=True, vmem_limit_bytes=63 << 20
         ),
         name="back",
-    )(*split_terms(grid, terms, z_majors), qx, qn, dox, kv, kext, cos, sin)
+    )(*split_terms(grid, terms, z_majors), qx, qn, dox, kv, kext, cos, sin, *([] if early is None else [early]))
 
 
 def adamw(weight, grad, first, second, rate, decay):
@@ -1262,10 +1383,14 @@
 
 
 def finish_kernel(grid, pieces, *refs):
-    hd, heads, x, gain, rg, gain_two, ig, gheads, ggains, h1, og, flat, wide, terms, value = refs[:15]
+    hd, heads, x, gain, rg, gain_two, down, output, ig, gheads, ggains, gdown, goutput = refs[:13]
+    h1, og, flat, wide, terms, value, last_down, last_output, last_sems = refs[13:22]
     here = Here(grid)
     greet(here.peers())
-    jobs, refs = reduce_jobs(here, [terms], [gheads], refs[15:], (True,), pieces)
+    columns = [Collect(here, down, last_down, last_sems.at[0]), Collect(here, output, last_output, last_sems.at[1])]
+    for column in columns:
+        column.begin()
+    jobs, refs = reduce_jobs(here, [terms], [gheads], refs[22:], (True,), pieces)
     share = Share(here, value, ggains, refs[:4], refs[4])
     tokens = x.shape[1]
     inverse = inverse_rms(x)
@@ -1297,9 +1422,9 @@
     for k in range(DEPTH):
         rows = pl.ds(k * SLICE, SLICE)
         normed = x[rows].astype(f32) * inverse
-        column = jnp.sum(og[rows] * normed, axis=1, keepdims=True)
+        sums = jnp.sum(og[rows] * normed, axis=1, keepdims=True)
         place = lax.broadcasted_iota(jnp.int32, (SLICE, 128), 1)
-        wide[rows] = jnp.where(place == 0, column, jnp.where(place == 1, gain_two[rows], 0.0))
+        wide[rows] = jnp.where(place == 0, sums, jnp.where(place == 1, gain_two[rows], 0.0))
         total += jnp.sum(og[rows] * gain[rows] * normed, axis=0, keepdims=True)
     value[...] = wide[...].T[:8]
     share.start(0)
@@ -1310,6 +1435,8 @@
         normed = x[rows].astype(f32) * inverse
         ig[rows] = rg[rows] + inverse * (og[rows] * gain[rows] - normed * mean)
     turn()
+    gdown[...] = columns[0].end()
+    goutput[...] = columns[1].end().T
     for k in range(4):
         share.end(k)
         if k < 3:
@@ -1317,11 +1444,11 @@
         turn(2)
     turn(len(ticks))
     share.drain()
-    for job in jobs:
+    for job in jobs + columns:
         job.drain()
 
 
-def finish(grid, hd, heads, x, gain, rg, gain_two, collective_id):
+def finish(grid, hd, heads, x, gain, rg, gain_two, down, output, collective_id):
     tokens = x.shape[1]
     rows = QKV // grid.nd
     term = jax.ShapeDtypeStruct((rows, SLICE), bf16)
@@ -1333,6 +1460,9 @@
         pltpu.VMEM((D, 128), f32),
         pltpu.VMEM((grid.nz, grid.ny, grid.nx, 2, rows, SLICE), bf16),
         pltpu.VMEM((8, D), f32),
+        pltpu.VMEM(down.shape, bf16),
+        pltpu.VMEM(output.shape, bf16),
+        pltpu.SemaphoreType.DMA((2, 2)),
     ]
     scratch += reduce_scratch(grid, [term], (True,), pieces)
     scratch += Share.scratch(grid, (8, D))
@@ -1343,18 +1473,20 @@
             jax.ShapeDtypeStruct((D, tokens), f32),
             jax.ShapeDtypeStruct((rows, SLICE), f32),
             jax.ShapeDtypeStruct((8, D), f32),
+            jax.ShapeDtypeStruct(down.shape[1:], f32),
+            jax.ShapeDtypeStruct(output.shape[:0:-1], f32),
         ],
-        in_specs=[VMEM] * 6,
-        out_specs=[VMEM] * 3,
+        in_specs=[VMEM] * 8,
+        out_specs=[VMEM] * 5,
         scratch_shapes=scratch,
         compiler_params=pltpu.CompilerParams(
             collective_id=collective_id, has_side_effects=True, vmem_limit_bytes=62 << 20
         ),
         name="finish",
-    )(hd, heads, x, gain, rg, gain_two)
-
-
-READY = 3
+    )(hd, heads, x, gain, rg, gain_two, down, output)
+
+
+READY = 4
 SUMMED = 1
 
 
@@ -1396,7 +1528,8 @@
     x, ogt = hidden_in.T, out_grad.T
     gain_one, gain_two = norm_gains[0][:, None], norm_gains[1][:, None]
 
-    (heads_stack,) = gather_weights(grid, [heads_weight.astype(bf16).T], (True,), 1)
+    singles = [output_weight.astype(bf16).T, down_weight.astype(bf16).T]
+    heads_stack, *columns = gather_weights(grid, [heads_weight.astype(bf16).T], (True,), singles, 1)
     heads = heads_stack.reshape(DEPTH, QKV, SLICE)
     expand_half = expand_weight.astype(bf16)
     stepped = expand_half.shape[1] == STEPS * WIDTH
@@ -1405,7 +1538,7 @@
         leads = [None, None, list(range(READY))]
     else:
         shard, leads = expand_half, [None, None, None]
-    shards = [output_weight.astype(bf16).T, down_weight.astype(bf16).T, shard]
+    shards = [*columns, shard]
     output_stack, down_stack, expand_stack, qx, qn, kv, att = front(
         grid, shards, (True, True, False), leads, heads, x, gain_one, cos, sin, qext, kext, 2
     )
@@ -1427,16 +1560,13 @@
         dexpand = dexpand.reshape((STEPS, grid.nd, grid.nz, SLICE, WIDTH))
     terms = [ddn.reshape(down_stack.shape), dexpand, dwo.reshape(output_stack.shape)]
     leads = [None, list(range(SUMMED, STEPS)) if stepped else None, None]
-    down_grad, late_exp, output_grad, hd = back(
-        grid, terms, (True, False, True), leads, qx, qn, dox, kv, kext, cos, sin, 3
+    down_column, expand_grad, output_column, hd = back(
+        grid, terms, (True, False, True), leads, early_exp, qx, qn, dox, kv, kext, cos, sin, 3
     )
-    ig, heads_grad, gains_grad = finish(grid, hd, heads, x, gain_one, rg, gain_two_term, 4)
-    if stepped:
-        steps = [(early_exp if k < SUMMED else late_exp)[k] for k in range(STEPS)]
-        expand_grad = jnp.concatenate(steps, axis=1)
-    else:
-        expand_grad = late_exp
-    heads_grad, output_grad, down_grad, gains_grad = heads_grad.T, output_grad.T, down_grad.T, gains_grad[:2]
+    ig, heads_grad, gains_grad, down_grad, output_grad = finish(
+        grid, hd, heads, x, gain_one, rg, gain_two_term, down_column, output_column, 4
+    )
+    heads_grad, down_grad, gains_grad = heads_grad.T, down_grad.T, gains_grad[:2]
     hidden_out, input_grad = out.T, ig.T
     gains_new, gains_first_new, gains_second_new = adamw(
         norm_gains, gains_grad, gains_first, gains_second, gain_rate, 0.0

time: 383 us -> 355 us (0.927)
  Pallas kernels: 344 us -> 326 us
  local copies, waits for them, and re-layouts: 20.1 us -> 12.3 us
    pallas_call x1, Pallas kernels: 107 us -> 93.8 us  [back(): pl.pallas_call(functools.partial(back_kernel, grid, tuple(z_majors), piec...]
    pallas_call x1, Pallas kernels: 95.9 us -> 86.4 us  [front(): pl.pallas_call(functools.partial(front_kernel, grid, tuple(z_majors), pie...]
    unnamed x55 -> x51, local copies, waits for them, and re-layouts: 14.6 us -> 7.77 us
    pallas_call x1, Pallas kernels: 30.3 us -> 35.5 us  [gather_weights(): pl.pallas_call(functools.partial(gather_kernel, grid, tuple(z_majors), pi...]
    pallas_call x1, Pallas kernels: 73.6 us -> 69.7 us  [middle(): pl.pallas_call(functools.partial(middle_kernel, grid, ready, summed), out...]
where the time goes in v4:
time: 355 us; the launch traced here: 354 us
  Pallas kernels  326 us (92%)
  other arithmetic  15.7 us (4%)
  local copies, waits for them, and re-layouts  12.3 us (3%)
    pallas_call x1, Pallas kernels, back(): pl.pallas_call(functools.partial(back_kernel, grid, tuple(z_majors), piec...  93.8 us
    pallas_call x1, Pallas kernels, front(): pl.pallas_call(functools.partial(front_kernel, grid, tuple(z_majors), pie...  86.4 us
    pallas_call x1, Pallas kernels, middle(): pl.pallas_call(functools.partial(middle_kernel, grid, ready, summed), out...  69.7 us
    pallas_call x1, Pallas kernels, finish(): pl.pallas_call(functools.partial(finish_kernel, grid, pieces), out_shape=...  40.1 us
    pallas_call x1, Pallas kernels, gather_weights(): pl.pallas_call(functools.partial(gather_kernel, grid, tuple(z_majors), pi...  35.5 us
    sub x5, other arithmetic, adamw(): weight - rate * (first_hat / (jnp.sqrt(second_hat) + adam_epsilon) + deca...  7.79 us
    unnamed x51, local copies, waits for them, and re-layouts  7.77 us

profile of v4, /device:TPU:0, one launch (start us, length us, event | category | flops | bytes accessed | tf_op | source)
XLA Modules:
  0.0 354.4 jit_solution(11773920099446066921)
XLA Ops:
  0.7 0.7 subtract_convert_fusion
  1.4 0.7 constant_dynamic-slice_fusion
  2.1 0.8 slice_bitcast_fusion
  2.9 1.6 copy.42
  4.5 0.7 select_convert_fusion.1.refs_8_
  5.2 1.6 convert_bitcast_fusion.1.refs_0_
  6.8 1.0 multiply_sine_fusion
  7.8 1.6 convert_bitcast_fusion.refs_2_
  9.4 1.1 convert_element_type.31
  10.5 0.2 copy.43
  10.7 0.9 copy.44
  11.6 1.0 copy.46.refs_4_
  12.6 1.0 copy.45.refs_5_.refs_3_
  13.6 1.1 select_convert_fusion.refs_9_.refs_7_
  14.7 35.5 %gather_weights.1 = (bf16[4,8,200,240]{3,2,1,0:T(8,128)(2,1)}, bf16[4,120,240]{2,1,0:T(8,128)(2,1)}, bf16[4,120,640]{2,1,0:T(8,128)(2,1)}) custom-call(bf16[200,240]{1,0:T(8,128)(2,1)} %convert_bitcast_fusion.1.refs_0_, bf16[120,240]{1,0:T(8,128)(2,1)} %bitcast.45, bf16[120,640]{1,0:T(8,128)(2,1)} %convert_bitcast_fusion.refs_2_), custom_call_target="tpu_custom_call" | custom-call | tf_op jit(solution)/shard_map/gather_weights/pallas_call | solution.py:293
  50.2 86.4 %front.1 = (bf16[4,8,120,240]{3,2,1,0:T(8,128)(2,1)}, bf16[4,8,120,640]{3,2,1,0:T(8,128)(2,1)}, bf16[4,8,4,240,128]{4,3,2,1,0:T(8,128)(2,1)}, bf16[15,128,512]{2...) custom-call(bf16[4,120,240]{2,1,0:T(8,128)(2,1)} %get-tuple-element.49, ...), custom_call_target="tpu_custom_call" | custom-call | tf_op jit(solution)/shard_map/front/pallas_call | solution.py:872
  136.7 69.7 %middle.1 = (bf16[960,512]{1,0:T(8,128)(2,1)}, f32[960,512]{1,0:T(8,128)}, f32[960,1]{1,0:T(8,128)}, bf16[4,960,240]{2,1,0:T(8,128)(2,1)}, bf16[15,128,512]{2,1,...) custom-call(bf16[960,512]{1,0:T(8,128)(2,1)} %get-tuple-element.52.r, ...), custom_call_target="tpu_custom_call" | custom-call | tf_op jit(solution)/shard_map/middle/pallas_call | solution.py:1150
  206.4 93.8 %back.1 = (bf16[4,120,640]{2,1,0:T(8,128)(2,1)}, f32[240,640]{1,0:T(8,128)}, bf16[4,120,240]{2,1,0:T(8,128)(2,1)}, bf16[1600,512]{1,0:T(8,128)(2,1)}) custom-call(bf16[4,2,2,2,120,640]{5,4,3,2,1,0:T(8,128)(2,1)} %bitcast.33, bf16[5,2,2,2,4,240,128]{6,5,4,3,2,1,0:T(8,128)(2,1)} %get-tuple-element.58.refs_1_, bf16[4,2,2,2,120,240]{5,4,3,2,1,0:T(8,128)(2,1)} %bitcast.39, ...), custom_call_target="tpu_custom_call" | custom-call | tf_op jit(solution)/shard_map/back/pallas_call | solution.py:1361
  300.2 0.0 copy-start.18
  300.2 0.0 copy-start.20
  300.2 0.0 copy-start.21
  300.2 0.0 copy-start.10
  300.3 0.0 copy-start.16
  300.3 0.0 copy-start.17
  300.3 0.0 copy-start.6
  300.3 0.0 copy-start.14
  300.3 0.0 copy-start.15
  300.3 40.1 %finish.1 = (f32[960,512]{1,0:T(8,128)}, f32[200,240]{1,0:T(8,128)}, f32[8,960]{1,0:T(8,128)}, f32[120,640]{1,0:T(8,128)}, f32[240,120]{1,0:T(8,128)}) custom-call(bf16[1600,512]{1,0:T(8,128)(2,1)} %get-tuple-element.65.refs_0_, bf16[4,1600,240]{2,1,0:T(8,128)(2,1)} %bitcast.29, bf16[960,512]{1,0:T(8,128)(2,1)} %bitcast.32, f32[960,1]{1,0:T(8,128)} %copy.45.refs_5_.refs_3_, ...), custom_call_target="tpu_custom_call" | custom-call | tf_op jit(solution)/shard_map/finish/pallas_call | solution.py:1470
  340.4 0.0 copy-start.3
  340.4 0.0 copy-start.12
  340.4 0.0 copy-start.13
  340.4 0.0 copy-done.18
  340.4 0.0 copy-done.20
  340.5 0.0 copy-done.21
  340.5 1.5 multiply_subtract_fusion.4
  342.0 0.0 copy-done.17
  342.0 1.7 multiply_subtract_fusion.3
  343.7 2.0 multiply_subtract_fusion.2
  345.7 0.0 copy-done.12
  345.7 1.1 multiply_subtract_fusion.1
  346.8 1.5 multiply_subtract_fusion
  348.4 0.9 copy.54
  349.3 1.0 copy-done.2
  350.3 1.3 copy.55
  351.5 0.7 copy.56
  352.2 0.6 copy.57
  352.9 0.8 copy.58
  353.7 0.7 copy.59
  (30 shorter events, 0.1 us)
Async XLA Ops:
  6.8 6.8 %copy-start.19 = (s32[1,2048]{1,0:T(1,128)S(1)}, s32[1,2048]{1,0:T(1,128)}, u32[]{:S(2)}) copy-start(s32[1,2048]{1,0:T(1,128)} %param.21) | copy-start | bytes 24580
  300.2 40.2 %copy-start.18 = (f32[2,960]{1,0:T(2,128)S(1)}, f32[2,960]{1,0:T(2,128)}, u32[]{:S(2)}) copy-start(f32[2,960]{1,0:T(2,128)} %param.23) | copy-start | bytes 23044
  300.2 40.2 %copy-start.20 = (f32[2,960]{1,0:T(2,128)S(1)}, f32[2,960]{1,0:T(2,128)}, u32[]{:S(2)}) copy-start(f32[2,960]{1,0:T(2,128)} %param.28) | copy-start | bytes 23044
  300.2 40.2 %copy-start.21 = (f32[2,960]{1,0:T(2,128)S(1)}, f32[2,960]{1,0:T(2,128)}, u32[]{:S(2)}) copy-start(f32[2,960]{1,0:T(2,128)} %param.29) | copy-start | bytes 23044
  300.2 41.7 %copy-start.10 = (f32[240,120]{1,0:T(8,128)S(1)}, f32[240,120]{1,0:T(8,128)}, u32[]{:S(2)}) copy-start(f32[240,120]{1,0:T(8,128)} %param.25) | copy-start | bytes 345604
  300.3 41.7 %copy-start.16 = (f32[240,120]{1,0:T(8,128)S(1)}, f32[240,120]{1,0:T(8,128)}, u32[]{:S(2)}) copy-start(f32[240,120]{1,0:T(8,128)} %param.32) | copy-start | bytes 345604
  300.3 41.7 %copy-start.17 = (f32[240,120]{1,0:T(8,128)S(1)}, f32[240,120]{1,0:T(8,128)}, u32[]{:S(2)}) copy-start(f32[240,120]{1,0:T(8,128)} %param.33) | copy-start | bytes 345604
  300.3 43.4 %copy-start.6 = (f32[240,200]{0,1:T(8,128)S(1)}, f32[240,200]{0,1:T(8,128)}, u32[]{:S(2)}) copy-start(f32[240,200]{0,1:T(8,128)} %param.24) | copy-start | bytes 576004
  300.3 43.4 %copy-start.14 = (f32[240,200]{0,1:T(8,128)S(1)}, f32[240,200]{0,1:T(8,128)}, u32[]{:S(2)}) copy-start(f32[240,200]{0,1:T(8,128)} %param.30) | copy-start | bytes 576004
  300.3 43.4 %copy-start.15 = (f32[240,200]{0,1:T(8,128)S(1)}, f32[240,200]{0,1:T(8,128)}, u32[]{:S(2)}) copy-start(f32[240,200]{0,1:T(8,128)} %param.31) | copy-start | bytes 576004
  340.4 5.3 %copy-start.3 = (f32[640,120]{0,1:T(8,128)S(1)}, f32[640,120]{0,1:T(8,128)}, u32[]{:S(2)}) copy-start(f32[640,120]{0,1:T(8,128)} %param.27) | copy-start | bytes 921604
  340.4 5.3 %copy-start.4 = (f32[120,640]{1,0:T(8,128)S(1)}, f32[120,640]{1,0:T(8,128)}, u32[]{:S(2)}) copy-start(f32[120,640]{1,0:T(8,128)} %get-tuple-element.75) | copy-start | bytes 921604
  340.4 5.3 %copy-start.12 = (f32[640,120]{0,1:T(8,128)S(1)}, f32[640,120]{0,1:T(8,128)}, u32[]{:S(2)}) copy-start(f32[640,120]{0,1:T(8,128)} %param.36) | copy-start | bytes 921604
  340.4 5.3 %copy-start.13 = (f32[640,120]{0,1:T(8,128)S(1)}, f32[640,120]{0,1:T(8,128)}, u32[]{:S(2)}) copy-start(f32[640,120]{0,1:T(8,128)} %param.37) | copy-start | bytes 921604
  343.7 3.1 copy-start
  343.7 3.1 copy-start.1
  343.7 3.1 copy-start.8
  343.7 3.2 copy-start.9
  346.8 1.5 copy-start.5
  348.4 1.9 copy-start.2
  350.3 1.3 copy-start.7
  350.3 2.0 copy-start.11

commit v5 on v4

--- a/solution.py
+++ b/solution.py
@@ -257,13 +257,15 @@
 GATHER_SEMS = 9
 
 
-def gather_kernel(grid, z_majors, pieces, spreads, *refs):
-    n = len(z_majors)
-    shards, refs = refs[:n], refs[n:]
-    singles, refs = refs[:spreads], refs[spreads:]
+def gather_kernel(grid, z_majors, pieces, turns, *refs):
+    n, spreads = len(z_majors), len(turns) - len(z_majors)
+    given, refs = refs[: n + spreads], refs[n + spreads :]
     outs, refs = refs[:n], refs[n:]
     columns, refs = refs[:spreads], refs[spreads:]
-    sems, spread_sems = refs
+    rounded, (sems, spread_sems) = refs[: n + spreads], refs[n + spreads :]
+    for source, half, turn in zip(given, rounded, turns):
+        half[...] = (source[...].T if turn else source[...]).astype(jnp.bfloat16)
+    shards, singles = rounded[:n], rounded[n:]
     here = Here(grid)
     greet(here.peers())
     jobs = gather_jobs(here, shards, outs, sems, z_majors, pieces)
@@ -282,20 +284,25 @@
         other.end()
 
 
-def gather_weights(grid, shards, z_majors, singles, collective_id):
+def gather_weights(grid, shards, z_majors, singles, turns, collective_id):
+    blocks = []
+    for value, turn in zip([*shards, *singles], turns):
+        blocks.append(jax.ShapeDtypeStruct(value.shape[::-1] if turn else value.shape, jnp.bfloat16))
+    n = len(shards)
     shapes = []
-    for shard, z_major in zip(shards, z_majors):
+    for block, z_major in zip(blocks, z_majors):
         lead = (grid.nz, grid.nd) if z_major else (grid.nd, grid.nz)
-        shapes.append(jax.ShapeDtypeStruct(lead + shard.shape, shard.dtype))
-    for single in singles:
-        shapes.append(jax.ShapeDtypeStruct((grid.nz,) + single.shape, single.dtype))
-    pieces = chunk_list(shards)
+        shapes.append(jax.ShapeDtypeStruct(lead + block.shape, block.dtype))
+    for block in blocks[n:]:
+        shapes.append(jax.ShapeDtypeStruct((grid.nz,) + block.shape, block.dtype))
+    pieces = chunk_list(blocks[:n])
     return pl.pallas_call(
-        functools.partial(gather_kernel, grid, tuple(z_majors), pieces, len(singles)),
+        functools.partial(gather_kernel, grid, tuple(z_majors), pieces, tuple(turns)),
         out_shape=shapes,
-        in_specs=[VMEM] * (len(shards) + len(singles)),
+        in_specs=[VMEM] * len(blocks),
         out_specs=[ANY] * len(shapes),
-        scratch_shapes=[
+        scratch_shapes=[pltpu.VMEM(block.shape, block.dtype) for block in blocks]
+        + [
             pltpu.SemaphoreType.DMA((len(pieces), GATHER_SEMS)),
             pltpu.SemaphoreType.DMA((len(singles), 3)),
         ],
@@ -710,6 +717,14 @@
                 wait_bytes(self.kv.at[h.z - s], self.sems.at[0, h.z - s])
 
 
+def round_steps(source, rounded, start):
+    if len(rounded.shape) == 2:
+        rounded[...] = source[...].astype(bf16)
+    else:
+        for k in range(rounded.shape[0]):
+            rounded[k] = source[:, pl.ds((start + k) * WIDTH, WIDTH)].astype(bf16)
+
+
 def front_kernel(grid, z_majors, pieces, *refs):
     n = len(z_majors)
     shards, refs = refs[:n], refs[n:]
@@ -717,12 +732,13 @@
     refs = refs[7:]
     outs, refs = refs[:n], refs[n:]
     qx, qn, kv, att = refs[:4]
-    h1, proj, kx, vt, acc, sems, kv_sems = refs[4:]
+    h1, proj, kx, vt, acc, rounded, sems, kv_sems = refs[4:]
     here = Here(grid)
     tokens = x.shape[1]
     half = tokens // 2
+    round_steps(shards[-1], rounded, 0)
     greet(here.peers())
-    jobs = gather_jobs(here, shards, outs, sems, z_majors, pieces)
+    jobs = gather_jobs(here, [*shards[:-1], rounded], outs, sems, z_majors, pieces)
     ticks = pipelined(jobs, 3)
     for tick in ticks[:3]:
         tick()
@@ -730,7 +746,7 @@
     inverse = inverse_rms(x)
     for k in range(DEPTH):
         rows = pl.ds(k * SLICE, SLICE)
-        h1[rows] = (x[rows].astype(f32) * inverse * gain[rows]).astype(bf16)
+        h1[rows] = (x[rows].astype(f32) * inverse * gain[rows, 0:1]).astype(bf16)
 
     part = QKV // 5
 
@@ -742,7 +758,7 @@
         proj[rows] = total
         return carry
 
-    lax.fori_loop(0, 5, project, 0)
+    lax.fori_loop(3, 5, project, 0)
 
     def turned(h):
         base = h * HEAD
@@ -761,6 +777,7 @@
     lax.fori_loop(0, KEY_VALUE_HEADS, keys, 0)
     chain = KeyChain(here, kv, kv_sems)
     chain.up(here.z)
+    lax.fori_loop(0, 3, project, 0)
 
     def queries(h, carry):
         a, b = turned(h)
@@ -834,7 +851,7 @@
                 whole(g)
 
         for k, tick in enumerate(ticks):
-            pl.when(t == k * micros // len(ticks))(tick)
+            pl.when(t == k * (micros - KEY_VALUE_HEADS) // len(ticks))(tick)
         return carry
 
     micros = grid.nz * KEY_VALUE_HEADS
@@ -857,12 +874,16 @@
 def front(grid, shards, z_majors, leads, heads, x, gain, cos, sin, qext, kext, collective_id):
     tokens = x.shape[1]
     shapes = []
-    for shard, z_major, chosen in zip(shards, z_majors, leads):
+    chosen = leads[-1]
+    expand = shards[-1]
+    rounded = (len(chosen), SLICE, WIDTH) if chosen else expand.shape
+    blocks = [*shards[:-1], jax.ShapeDtypeStruct(rounded, bf16)]
+    for block, z_major, chosen in zip(blocks, z_majors, leads):
         lead = (grid.nz, grid.nd) if z_major else (grid.nd, grid.nz)
         lead = (len(chosen),) + lead if chosen else lead
-        shapes.append(jax.ShapeDtypeStruct(lead + shard.shape[-2:], shard.dtype))
+        shapes.append(jax.ShapeDtypeStruct(lead + block.shape[-2:], bf16))
     n = len(shards)
-    pieces = chunk_list(shards, leads)
+    pieces = chunk_list(blocks, leads)
     shapes += [
         jax.ShapeDtypeStruct((QUERY_HEADS, 128, tokens), bf16),
         jax.ShapeDtypeStruct((QUERY_HEADS, tokens, 128), bf16),
@@ -880,6 +901,7 @@
             pltpu.VMEM((KEY_VALUE_HEADS, tokens, 128), bf16),
             pltpu.VMEM((KEY_VALUE_HEADS, 80, tokens), bf16),
             pltpu.VMEM((QUERY_HEADS, 80, tokens), f32),
+            pltpu.VMEM(rounded, bf16),
             pltpu.SemaphoreType.DMA((max(len(pieces), 1), GATHER_SEMS)),
             pltpu.SemaphoreType.DMA((2, grid.nz)),
         ],
@@ -913,20 +935,22 @@
     half = 2 * WIDTH
     schedule = {}
     gathers, sums = [], []
+    if late:
+        round_steps(shard, refs[0], ready)
     if late or summed:
         here = Here(grid)
         greet(here.peers())
     if late:
         pieces = [(0, k, (0, SLICE)) for k in range(late)]
-        g_sems, refs = refs[0], refs[1:]
+        rounded, g_sems, refs = refs[0], refs[1], refs[2:]
         gathers = [
-            Gather(here, shard.at[ready + k], exp_late.at[k], g_sems.at[k], False, (0, SLICE)) for k in range(late)
+            Gather(here, rounded.at[k], exp_late.at[k], g_sems.at[k], False, (0, SLICE)) for k in range(late)
         ]
         for job in gathers:
             job.stage_z()
         for k, job in enumerate(gathers):
             for i, stage in enumerate(job.stages[1:]):
-                schedule.setdefault(5 * i + 2 * k, []).append(getattr(job, stage))
+                schedule.setdefault((k, 4 + 2 * k, 9 + 4 * k)[i], []).append(getattr(job, stage))
             schedule.setdefault((ready + k - 1) * PARTS + 1, []).append(job.arrive)
     if summed:
         pieces = [(0, k, (0, SLICE)) for k in range(summed)]
@@ -987,7 +1011,7 @@
     inv[...] = inverse
     for m in range(DEPTH):
         rows = pl.ds(m * SLICE, SLICE)
-        h2t[rows] = (res[rows] * inverse * gain[rows]).astype(bf16)
+        h2t[rows] = (res[rows] * inverse * gain[rows, 1:2]).astype(bf16)
     h2[...] = h2t[...].astype(f32).T.astype(bf16)
     og[...] = ogt[...].astype(f32).T.astype(bf16)
     acc_o[...] = jnp.zeros_like(acc_o)
@@ -1067,12 +1091,12 @@
         normed = res[rows] * inverse
         up = acc_h[rows]
         gsum[rows] = jnp.sum(up * normed, axis=1, keepdims=True)
-        total += jnp.sum(up * gain[rows] * normed, axis=0, keepdims=True)
+        total += jnp.sum(up * gain[rows, 1:2] * normed, axis=0, keepdims=True)
     mean = total * (1.0 / D)
     for m in range(DEPTH):
         rows = pl.ds(m * SLICE, SLICE)
         normed = res[rows] * inverse
-        r = ogt[rows].astype(f32) + inverse * (acc_h[rows] * gain[rows] - normed * mean)
+        r = ogt[rows].astype(f32) + inverse * (acc_h[rows] * gain[rows, 1:2] - normed * mean)
         rg[rows] = r
         h2t[rows] = r.astype(bf16)
     for k in range(DEPTH):
@@ -1139,6 +1163,7 @@
         in_specs.append(VMEM)
         shapes.append(jax.ShapeDtypeStruct((late,) + blocks, bf16))
         out_specs.append(ANY)
+        scratch.append(pltpu.VMEM((late, SLICE, WIDTH), bf16))
         scratch.append(pltpu.SemaphoreType.DMA((late, GATHER_SEMS)))
     if summed:
         shapes.append(jax.ShapeDtypeStruct((summed,) + blocks[2:], f32))
@@ -1396,7 +1421,7 @@
     inverse = inverse_rms(x)
     for k in range(DEPTH):
         rows = pl.ds(k * SLICE, SLICE)
-        h1[rows] = (x[rows].astype(f32) * inverse * gain[rows]).astype(bf16)
+        h1[rows] = (x[rows].astype(f32) * inverse * gain[rows, 0:1]).astype(bf16)
     rows = terms.shape[-2]
     for k in range(DEPTH):
         flat[...] = mm_nt(hd[...], h1[pl.ds(k * SLICE, SLICE)])
@@ -1425,7 +1450,7 @@
         sums = jnp.sum(og[rows] * normed, axis=1, keepdims=True)
         place = lax.broadcasted_iota(jnp.int32, (SLICE, 128), 1)
         wide[rows] = jnp.where(place == 0, sums, jnp.where(place == 1, gain_two[rows], 0.0))
-        total += jnp.sum(og[rows] * gain[rows] * normed, axis=0, keepdims=True)
+        total += jnp.sum(og[rows] * gain[rows, 0:1] * normed, axis=0, keepdims=True)
     value[...] = wide[...].T[:8]
     share.start(0)
     turn()
@@ -1433,7 +1458,7 @@
     for k in range(DEPTH):
         rows = pl.ds(k * SLICE, SLICE)
         normed = x[rows].astype(f32) * inverse
-        ig[rows] = rg[rows] + inverse * (og[rows] * gain[rows] - normed * mean)
+        ig[rows] = rg[rows] + inverse * (og[rows] * gain[rows, 0:1] - normed * mean)
     turn()
     gdown[...] = columns[0].end()
     goutput[...] = columns[1].end().T
@@ -1486,7 +1511,7 @@
     )(hd, heads, x, gain, rg, gain_two, down, output)
 
 
-READY = 4
+READY = 3
 SUMMED = 1
 
 
@@ -1526,33 +1551,30 @@
     other_doc = (lane[None, :] >= 0) & (lane[None, :] < DOCS) & (seg_row[:, None] != lane[None, :])
     kext = jnp.where(other_doc | ((lane >= DOCS) & (lane < DOCS + 3))[None, :], 1.0, 0.0).astype(bf16)
     x, ogt = hidden_in.T, out_grad.T
-    gain_one, gain_two = norm_gains[0][:, None], norm_gains[1][:, None]
-
-    singles = [output_weight.astype(bf16).T, down_weight.astype(bf16).T]
-    heads_stack, *columns = gather_weights(grid, [heads_weight.astype(bf16).T], (True,), singles, 1)
+    gain = norm_gains.T
+
+    heads_stack, *columns = gather_weights(
+        grid, [heads_weight.T], (True,), [output_weight, down_weight.T], (False, True, False), 1
+    )
     heads = heads_stack.reshape(DEPTH, QKV, SLICE)
-    expand_half = expand_weight.astype(bf16)
-    stepped = expand_half.shape[1] == STEPS * WIDTH
-    if stepped:
-        shard = expand_half.reshape(SLICE, STEPS, WIDTH).transpose(1, 0, 2)
-        leads = [None, None, list(range(READY))]
-    else:
-        shard, leads = expand_half, [None, None, None]
-    shards = [*columns, shard]
+    stepped = expand_weight.shape[1] == STEPS * WIDTH
+    leads = [None, None, list(range(READY)) if stepped else None]
+    shards = [*columns, expand_weight]
     output_stack, down_stack, expand_stack, qx, qn, kv, att = front(
-        grid, shards, (True, True, False), leads, heads, x, gain_one, cos, sin, qext, kext, 2
+        grid, shards, (True, True, False), leads, heads, x, gain, cos, sin, qext, kext, 2
     )
     wo = output_stack.reshape(DEPTH, D, SLICE)
     down = down_stack.reshape(DEPTH, D, FF // DEPTH)
     blocks = (8, DEPTH, SLICE)
     if stepped:
-        late = middle(grid, att, wo, x, ogt, gain_two, expand_stack, down, shard, SUMMED, 5)
-        out, rg, gain_two_term, dwo, dox, dexpand, ddn, _, early_exp = late
+        late = middle(grid, att, wo, x, ogt, gain, expand_stack, down, expand_weight, SUMMED, 5)
+        out, rg, gain_two_term, dwo, dox, dexpand, ddn, *late = late
+        early_exp = late[-1] if SUMMED else None
     else:
         expand = expand_stack.transpose(1, 2, 0, 3).reshape(DEPTH, SLICE, 8, STEPS, WIDTH)
         expand = expand.transpose(3, 2, 0, 1, 4)
         out, rg, gain_two_term, dwo, dox, dexpand, ddn = middle(
-            grid, att, wo, x, ogt, gain_two, expand, down, None, 0, 5
+            grid, att, wo, x, ogt, gain, expand, down, None, 0, 5
         )
         early_exp = None
         dexpand = dexpand.transpose(2, 3, 1, 0, 4).reshape(DEPTH, SLICE, grid.nd, -1).transpose(2, 0, 1, 3)
@@ -1564,7 +1586,7 @@
         grid, terms, (True, False, True), leads, early_exp, qx, qn, dox, kv, kext, cos, sin, 3
     )
     ig, heads_grad, gains_grad, down_grad, output_grad = finish(
-        grid, hd, heads, x, gain_one, rg, gain_two_term, down_column, output_column, 4
+        grid, hd, heads, x, gain, rg, gain_two_term, down_column, output_column, 4
     )
     heads_grad, down_grad, gains_grad = heads_grad.T, down_grad.T, gains_grad[:2]
     hidden_out, input_grad = out.T, ig.T

time: 355 us -> 337 us (0.949)
  Pallas kernels: 326 us -> 316 us
  local copies, waits for them, and re-layouts: 12.3 us -> 8.52 us
  other arithmetic: 15.7 us -> 12 us
    pallas_call x1, Pallas kernels: 86.4 us -> 74.1 us  [front(): pl.pallas_call(functools.partial(front_kernel, grid, tuple(z_majors), pie...]
    pallas_call x1, Pallas kernels: 69.7 us -> 73.3 us  [middle(): pl.pallas_call(functools.partial(middle_kernel, grid, ready, summed), out...]
    unnamed x51 -> x49, local copies, waits for them, and re-layouts: 7.77 us -> 7.83 us
where the time goes in v5:
time: 337 us
  Pallas kernels  316 us (94%)
  other arithmetic  12 us (4%)
  local copies, waits for them, and re-layouts  8.52 us (3%)
    pallas_call x1, Pallas kernels, back(): pl.pallas_call(functools.partial(back_kernel, grid, tuple(z_majors), piec...  92.9 us
    pallas_call x1, Pallas kernels, front(): pl.pallas_call(functools.partial(front_kernel, grid, tuple(z_majors), pie...  74.1 us
    pallas_call x1, Pallas kernels, middle(): pl.pallas_call(functools.partial(middle_kernel, grid, ready, summed), out...  73.3 us
    pallas_call x1, Pallas kernels, finish(): pl.pallas_call(functools.partial(finish_kernel, grid, pieces), out_shape=...  39.6 us
    pallas_call x1, Pallas kernels, gather_weights(): pl.pallas_call(functools.partial(gather_kernel, grid, tuple(z_majors), pi...  35.8 us
    unnamed x49, local copies, waits for them, and re-layouts  7.83 us
    sub x5, other arithmetic, adamw(): weight - rate * (first_hat / (jnp.sqrt(second_hat) + adam_epsilon) + deca...  7.79 us

profile of v5, /device:TPU:0, one launch (start us, length us, event | category | flops | bytes accessed | tf_op | source)
XLA Modules:
  0.0 337.0 jit_solution(18413329426105488074)
XLA Ops:
  0.7 0.7 subtract_convert_fusion
  1.4 0.7 constant_dynamic-slice_fusion
  2.1 0.7 select_convert_fusion.1.refs_8_
  2.8 1.0 multiply_sine_fusion
  3.8 1.7 copy.41
  5.5 1.8 select_convert_fusion.refs_9_.refs_7_
  7.3 35.8 %gather_weights.1 = (bf16[4,8,200,240]{3,2,1,0:T(8,128)(2,1)}, bf16[4,120,240]{2,1,0:T(8,128)(2,1)}, bf16[4,120,640]{2,1,0:T(8,128)(2,1)}) custom-call(f32[200,240]{1,0:T(8,128)} %bitcast.35, f32[240,120]{1,0:T(8,128)} %refs_1_.1, f32[120,640]{1,0:T(8,128)} %bitcast.31), custom_call_target="tpu_custom_call" | custom-call | tf_op jit(solution)/shard_map/gather_weights/pallas_call | solution.py:299
  43.0 74.1 %front.1 = (bf16[4,8,120,240]{3,2,1,0:T(8,128)(2,1)}, bf16[4,8,120,640]{3,2,1,0:T(8,128)(2,1)}, bf16[3,8,4,240,128]{4,3,2,1,0:T(8,128)(2,1)}, bf16[15,128,512]{2...) custom-call(bf16[4,120,240]{2,1,0:T(8,128)(2,1)} %get-tuple-element.49, ...), custom_call_target="tpu_custom_call" | custom-call | tf_op jit(solution)/shard_map/front/pallas_call | solution.py:893
  117.1 73.3 %middle.1 = (bf16[960,512]{1,0:T(8,128)(2,1)}, f32[960,512]{1,0:T(8,128)}, f32[960,1]{1,0:T(8,128)}, bf16[4,960,240]{2,1,0:T(8,128)(2,1)}, bf16[15,128,512]{2,1,...) custom-call(bf16[960,512]{1,0:T(8,128)(2,1)} %get-tuple-element.52.r, ...), custom_call_target="tpu_custom_call" | custom-call | tf_op jit(solution)/shard_map/middle/pallas_call | solution.py:1175
  190.4 92.9 %back.1 = (bf16[4,120,640]{2,1,0:T(8,128)(2,1)}, f32[240,640]{1,0:T(8,128)}, bf16[4,120,240]{2,1,0:T(8,128)(2,1)}, bf16[1600,512]{1,0:T(8,128)(2,1)}) custom-call(bf16[4,2,2,2,120,640]{5,4,3,2,1,0:T(8,128)(2,1)} %bitcast.26, bf16[5,2,2,2,4,240,128]{6,5,4,3,2,1,0:T(8,128)(2,1)} %get-tuple-element.58.refs_1_, bf16[4,2,2,2,120,240]{5,4,3,2,1,0:T(8,128)(2,1)} %bitcast.30, ...), custom_call_target="tpu_custom_call" | custom-call | tf_op jit(solution)/shard_map/back/pallas_call | solution.py:1386
  283.3 0.0 copy-start.18
  283.3 0.0 copy-start.19
  283.3 0.0 copy-start.20
  283.3 0.0 copy-start.10
  283.3 0.0 copy-start.16
  283.3 0.0 copy-start.17
  283.4 0.0 copy-start.6
  283.4 0.0 copy-start.14
  283.4 0.0 copy-start.15
  283.4 39.6 %finish.1 = (f32[960,512]{1,0:T(8,128)}, f32[200,240]{1,0:T(8,128)}, f32[8,960]{1,0:T(8,128)}, f32[120,640]{1,0:T(8,128)}, f32[240,120]{1,0:T(8,128)}) custom-call(bf16[1600,512]{1,0:T(8,128)(2,1)} %get-tuple-element.65.refs_0_, bf16[4,1600,240]{2,1,0:T(8,128)(2,1)} %bitcast.19, bf16[960,512]{1,0:T(8,128)(2,1)} %bitcast.22, f32[960,2]{1,0:T(8,128)} %bitcast.25, ...), custom_call_target="tpu_custom_call" | custom-call | tf_op jit(solution)/shard_map/finish/pallas_call | solution.py:1495
  323.0 0.0 copy-start.3
  323.0 0.0 copy-start.4
  323.0 0.0 copy-start.12
  323.0 0.0 copy-start.13
  323.1 0.0 copy-done.18
  323.1 0.0 copy-done.19
  323.1 0.0 copy-done.20
  323.1 1.5 multiply_subtract_fusion.4
  324.6 0.0 copy-done.10
  324.6 0.0 copy-done.16
  324.6 0.0 copy-done.17
  324.6 1.7 multiply_subtract_fusion.3
  326.3 0.0 copy-done.6
  326.3 0.0 copy-done.14
  326.3 0.0 copy-done.15
  326.3 2.0 multiply_subtract_fusion.2
  328.3 0.0 copy-done.3
  328.3 0.0 copy-done.4
  328.3 1.1 multiply_subtract_fusion.1
  329.4 0.0 copy-done.1
  329.5 1.5 multiply_subtract_fusion
  331.0 0.9 copy.48
  331.9 1.0 copy-done.2
  332.9 1.3 copy.49
  334.2 0.7 copy.50
  334.8 0.6 copy.51
  335.5 0.8 copy.52
  336.3 0.7 copy.53
  (20 shorter events, 0.1 us)
Async XLA Ops:
  283.3 39.8 %copy-start.18 = (f32[2,960]{1,0:T(2,128)S(1)}, f32[2,960]{1,0:T(2,128)}, u32[]{:S(2)}) copy-start(f32[2,960]{1,0:T(2,128)} %param.23) | copy-start | bytes 23044
  283.3 39.8 %copy-start.19 = (f32[2,960]{1,0:T(2,128)S(1)}, f32[2,960]{1,0:T(2,128)}, u32[]{:S(2)}) copy-start(f32[2,960]{1,0:T(2,128)} %param.28) | copy-start | bytes 23044
  283.3 39.8 %copy-start.20 = (f32[2,960]{1,0:T(2,128)S(1)}, f32[2,960]{1,0:T(2,128)}, u32[]{:S(2)}) copy-start(f32[2,960]{1,0:T(2,128)} %param.29) | copy-start | bytes 23044
  283.3 41.3 %copy-start.10 = (f32[240,120]{1,0:T(8,128)S(1)}, f32[240,120]{1,0:T(8,128)}, u32[]{:S(2)}) copy-start(f32[240,120]{1,0:T(8,128)} %refs_1_.1) | copy-start | bytes 345604
  283.3 41.2 %copy-start.16 = (f32[240,120]{1,0:T(8,128)S(1)}, f32[240,120]{1,0:T(8,128)}, u32[]{:S(2)}) copy-start(f32[240,120]{1,0:T(8,128)} %param.32) | copy-start | bytes 345604
  283.3 41.2 %copy-start.17 = (f32[240,120]{1,0:T(8,128)S(1)}, f32[240,120]{1,0:T(8,128)}, u32[]{:S(2)}) copy-start(f32[240,120]{1,0:T(8,128)} %param.33) | copy-start | bytes 345604
  283.4 42.9 %copy-start.6 = (f32[240,200]{0,1:T(8,128)S(1)}, f32[240,200]{0,1:T(8,128)}, u32[]{:S(2)}) copy-start(f32[240,200]{0,1:T(8,128)} %param.24) | copy-start | bytes 576004
  283.4 42.9 %copy-start.14 = (f32[240,200]{0,1:T(8,128)S(1)}, f32[240,200]{0,1:T(8,128)}, u32[]{:S(2)}) copy-start(f32[240,200]{0,1:T(8,128)} %param.30) | copy-start | bytes 576004
  283.4 42.9 %copy-start.15 = (f32[240,200]{0,1:T(8,128)S(1)}, f32[240,200]{0,1:T(8,128)}, u32[]{:S(2)}) copy-start(f32[240,200]{0,1:T(8,128)} %param.31) | copy-start | bytes 576004
  323.0 5.3 %copy-start.3 = (f32[640,120]{0,1:T(8,128)S(1)}, f32[640,120]{0,1:T(8,128)}, u32[]{:S(2)}) copy-start(f32[640,120]{0,1:T(8,128)} %param.27) | copy-start | bytes 921604
  323.0 5.3 %copy-start.4 = (f32[120,640]{1,0:T(8,128)S(1)}, f32[120,640]{1,0:T(8,128)}, u32[]{:S(2)}) copy-start(f32[120,640]{1,0:T(8,128)} %get-tuple-element.75) | copy-start | bytes 921604
  323.0 5.3 %copy-start.12 = (f32[640,120]{0,1:T(8,128)S(1)}, f32[640,120]{0,1:T(8,128)}, u32[]{:S(2)}) copy-start(f32[640,120]{0,1:T(8,128)} %param.36) | copy-start | bytes 921604
  323.0 5.3 %copy-start.13 = (f32[640,120]{0,1:T(8,128)S(1)}, f32[640,120]{0,1:T(8,128)}, u32[]{:S(2)}) copy-start(f32[640,120]{0,1:T(8,128)} %param.37) | copy-start | bytes 921604
  326.3 3.1 copy-start
  326.3 3.1 copy-start.1
  326.3 3.1 copy-start.8
  326.3 3.2 copy-start.9
  329.4 1.5 copy-start.5
  331.0 1.9 copy-start.2
  332.9 1.3 copy-start.7
  332.9 2.0 copy-start.11

commit v6 on v5

--- a/solution.py
+++ b/solution.py
@@ -725,18 +725,26 @@
             rounded[k] = source[:, pl.ds((start + k) * WIDTH, WIDTH)].astype(bf16)
 
 
-def front_kernel(grid, z_majors, pieces, *refs):
+def front_kernel(grid, z_majors, pieces, late, *refs):
     n = len(z_majors)
     shards, refs = refs[:n], refs[n:]
     heads, x, gain, cos, sin, qext, kext = refs[:7]
     refs = refs[7:]
     outs, refs = refs[:n], refs[n:]
     qx, qn, kv, att = refs[:4]
-    h1, proj, kx, vt, acc, rounded, sems, kv_sems = refs[4:]
+    refs = refs[4:]
+    if late:
+        columns, refs = refs[0], refs[1:]
+    h1, proj, kx, vt, acc, rounded, sems, kv_sems = refs[:8]
     here = Here(grid)
     tokens = x.shape[1]
     half = tokens // 2
     round_steps(shards[-1], rounded, 0)
+    spreads = []
+    if late:
+        late_rounded, late_sems = refs[8:]
+        round_steps(shards[-1], late_rounded, STEPS - late)
+        spreads = [Spread(here, late_rounded.at[k], columns.at[k], late_sems.at[k]) for k in range(late)]
     greet(here.peers())
     jobs = gather_jobs(here, [*shards[:-1], rounded], outs, sems, z_majors, pieces)
     ticks = pipelined(jobs, 3)
@@ -852,6 +860,8 @@
 
         for k, tick in enumerate(ticks):
             pl.when(t == k * (micros - KEY_VALUE_HEADS) // len(ticks))(tick)
+        for spread in spreads:
+            pl.when(t == micros - 2 * KEY_VALUE_HEADS + 1)(spread.begin)
         return carry
 
     micros = grid.nz * KEY_VALUE_HEADS
@@ -868,6 +878,8 @@
     for job in jobs:
         job.arrive()
         job.drain()
+    for spread in spreads:
+        spread.end()
     chain.drain()
 
 
@@ -890,11 +902,16 @@
         jax.ShapeDtypeStruct((grid.nz, KEY_VALUE_HEADS, tokens, 128), bf16),
         jax.ShapeDtypeStruct((D, tokens), bf16),
     ]
+    late = STEPS - len(leads[-1]) if leads[-1] else 0
+    last = []
+    if late:
+        shapes.append(jax.ShapeDtypeStruct((late, grid.nz, SLICE, WIDTH), bf16))
+        last = [pltpu.VMEM((late, SLICE, WIDTH), bf16), pltpu.SemaphoreType.DMA((late, 3))]
     return pl.pallas_call(
-        functools.partial(front_kernel, grid, tuple(z_majors), pieces),
+        functools.partial(front_kernel, grid, tuple(z_majors), pieces, late),
         out_shape=shapes,
         in_specs=[VMEM] * (n + 7),
-        out_specs=[ANY] * n + [VMEM] * 4,
+        out_specs=[ANY] * n + [VMEM] * 4 + [ANY] * (late > 0),
         scratch_shapes=[
             pltpu.VMEM((D, tokens), bf16),
             pltpu.VMEM((QKV, tokens), f32),
@@ -904,6 +921,7 @@
             pltpu.VMEM(rounded, bf16),
             pltpu.SemaphoreType.DMA((max(len(pieces), 1), GATHER_SEMS)),
             pltpu.SemaphoreType.DMA((2, grid.nz)),
+            *last,
         ],
         compiler_params=pltpu.CompilerParams(
             collective_id=collective_id, has_side_effects=True, vmem_limit_bytes=60 << 20
@@ -935,22 +953,22 @@
     half = 2 * WIDTH
     schedule = {}
     gathers, sums = [], []
-    if late:
-        round_steps(shard, refs[0], ready)
     if late or summed:
         here = Here(grid)
         greet(here.peers())
     if late:
         pieces = [(0, k, (0, SLICE)) for k in range(late)]
-        rounded, g_sems, refs = refs[0], refs[1], refs[2:]
+        g_sems, refs = refs[0], refs[1:]
         gathers = [
-            Gather(here, rounded.at[k], exp_late.at[k], g_sems.at[k], False, (0, SLICE)) for k in range(late)
+            ColumnGather(here, shard.at[k], exp_late.at[k], g_sems.at[k], False, (0, SLICE)) for k in range(late)
         ]
         for job in gathers:
             job.stage_z()
+        for job in gathers:
+            job.stage_one()
         for k, job in enumerate(gathers):
-            for i, stage in enumerate(job.stages[1:]):
-                schedule.setdefault((k, 4 + 2 * k, 9 + 4 * k)[i], []).append(getattr(job, stage))
+            for i, stage in enumerate(job.stages[2:]):
+                schedule.setdefault((2 * k, 6 + 4 * k)[i], []).append(getattr(job, stage))
             schedule.setdefault((ready + k - 1) * PARTS + 1, []).append(job.arrive)
     if summed:
         pieces = [(0, k, (0, SLICE)) for k in range(summed)]
@@ -1163,7 +1181,6 @@
         in_specs.append(VMEM)
         shapes.append(jax.ShapeDtypeStruct((late,) + blocks, bf16))
         out_specs.append(ANY)
-        scratch.append(pltpu.VMEM((late, SLICE, WIDTH), bf16))
         scratch.append(pltpu.SemaphoreType.DMA((late, GATHER_SEMS)))
     if summed:
         shapes.append(jax.ShapeDtypeStruct((summed,) + blocks[2:], f32))
@@ -1560,14 +1577,14 @@
     stepped = expand_weight.shape[1] == STEPS * WIDTH
     leads = [None, None, list(range(READY)) if stepped else None]
     shards = [*columns, expand_weight]
-    output_stack, down_stack, expand_stack, qx, qn, kv, att = front(
+    output_stack, down_stack, expand_stack, qx, qn, kv, att, *late_columns = front(
         grid, shards, (True, True, False), leads, heads, x, gain, cos, sin, qext, kext, 2
     )
     wo = output_stack.reshape(DEPTH, D, SLICE)
     down = down_stack.reshape(DEPTH, D, FF // DEPTH)
     blocks = (8, DEPTH, SLICE)
     if stepped:
-        late = middle(grid, att, wo, x, ogt, gain, expand_stack, down, expand_weight, SUMMED, 5)
+        late = middle(grid, att, wo, x, ogt, gain, expand_stack, down, late_columns[0], SUMMED, 5)
         out, rg, gain_two_term, dwo, dox, dexpand, ddn, *late = late
         early_exp = late[-1] if SUMMED else None
     else:

time: 337 us -> 339 us (level)
  no operation moved by 1% of the time
where the time goes in v6:
time: 339 us; the launch traced here: 338 us
  Pallas kernels  317 us (94%)
  other arithmetic  12 us (4%)
  local copies, waits for them, and re-layouts  8.52 us (3%)
    pallas_call x1, Pallas kernels, back(): pl.pallas_call(functools.partial(back_kernel, grid, tuple(z_majors), piec...  92.4 us
    pallas_call x1, Pallas kernels, front(): pl.pallas_call(functools.partial(front_kernel, grid, tuple(z_majors), pie...  74.1 us
    pallas_call x1, Pallas kernels, middle(): pl.pallas_call(functools.partial(middle_kernel, grid, ready, summed), out...  72.1 us
    pallas_call x1, Pallas kernels, finish(): pl.pallas_call(functools.partial(finish_kernel, grid, pieces), out_shape=...  42.3 us
    pallas_call x1, Pallas kernels, gather_weights(): pl.pallas_call(functools.partial(gather_kernel, grid, tuple(z_majors), pi...  35.8 us
    unnamed x49, local copies, waits for them, and re-layouts  7.83 us
    sub x5, other arithmetic, adamw(): weight - rate * (first_hat / (jnp.sqrt(second_hat) + adam_epsilon) + deca...  7.8 us

profile of v6, /device:TPU:0, one launch (start us, length us, event | category | flops | bytes accessed | tf_op | source)
XLA Modules:
  0.0 338.2 jit_solution(14279678084083612979)
XLA Ops:
  0.7 0.7 subtract_convert_fusion
  1.4 0.7 constant_dynamic-slice_fusion
  2.1 0.7 select_convert_fusion.1.refs_8_
  2.8 1.0 multiply_sine_fusion
  3.8 1.7 copy.41
  5.5 1.8 select_convert_fusion.refs_9_.refs_7_
  7.3 35.8 %gather_weights.1 = (bf16[4,8,200,240]{3,2,1,0:T(8,128)(2,1)}, bf16[4,120,240]{2,1,0:T(8,128)(2,1)}, bf16[4,120,640]{2,1,0:T(8,128)(2,1)}) custom-call(f32[200,240]{1,0:T(8,128)} %bitcast.35, f32[240,120]{1,0:T(8,128)} %refs_1_.1, f32[120,640]{1,0:T(8,128)} %bitcast.31), custom_call_target="tpu_custom_call" | custom-call | tf_op jit(solution)/shard_map/gather_weights/pallas_call | solution.py:299
  43.0 74.1 %front.1 = (bf16[4,8,120,240]{3,2,1,0:T(8,128)(2,1)}, bf16[4,8,120,640]{3,2,1,0:T(8,128)(2,1)}, bf16[3,8,4,240,128]{4,3,2,1,0:T(8,128)(2,1)}, bf16[15,128,512]{2...) custom-call(bf16[4,120,240]{2,1,0:T(8,128)(2,1)} %get-tuple-element., ...), custom_call_target="tpu_custom_call" | custom-call | tf_op jit(solution)/shard_map/front/pallas_call | solution.py:910
  117.2 72.1 %middle.1 = (bf16[960,512]{1,0:T(8,128)(2,1)}, f32[960,512]{1,0:T(8,128)}, f32[960,1]{1,0:T(8,128)}, bf16[4,960,240]{2,1,0:T(8,128)(2,1)}, bf16[15,128,512]{2,1,...) custom-call(bf16[960,512]{1,0:T(8,128)(2,1)} %get-tuple-element.53.r, ...), custom_call_target="tpu_custom_call" | custom-call | tf_op jit(solution)/shard_map/middle/pallas_call | solution.py:1192
  189.3 92.4 %back.1 = (bf16[4,120,640]{2,1,0:T(8,128)(2,1)}, f32[240,640]{1,0:T(8,128)}, bf16[4,120,240]{2,1,0:T(8,128)(2,1)}, bf16[1600,512]{1,0:T(8,128)(2,1)}) custom-call(bf16[4,2,2,2,120,640]{5,4,3,2,1,0:T(8,128)(2,1)} %bitcast.26, bf16[5,2,2,2,4,240,128]{6,5,4,3,2,1,0:T(8,128)(2,1)} %get-tuple-element.60.refs_1_, bf16[4,2,2,2,120,240]{5,4,3,2,1,0:T(8,128)(2,1)} %bitcast.29, ...), custom_call_target="tpu_custom_call" | custom-call | tf_op jit(solution)/shard_map/back/pallas_call | solution.py:1403
  281.7 0.0 copy-start.18
  281.7 0.0 copy-start.19
  281.7 0.0 copy-start.20
  281.7 0.0 copy-start.10
  281.7 0.0 copy-start.16
  281.8 0.0 copy-start.17
  281.8 0.0 copy-start.6
  281.8 0.0 copy-start.14
  281.8 0.0 copy-start.15
  281.8 42.3 %finish.1 = (f32[960,512]{1,0:T(8,128)}, f32[200,240]{1,0:T(8,128)}, f32[8,960]{1,0:T(8,128)}, f32[120,640]{1,0:T(8,128)}, f32[240,120]{1,0:T(8,128)}) custom-call(bf16[1600,512]{1,0:T(8,128)(2,1)} %get-tuple-element.67.refs_0_, bf16[4,1600,240]{2,1,0:T(8,128)(2,1)} %bitcast.19, bf16[960,512]{1,0:T(8,128)(2,1)} %bitcast.22, f32[960,2]{1,0:T(8,128)} %bitcast.25, ...), custom_call_target="tpu_custom_call" | custom-call | tf_op jit(solution)/shard_map/finish/pallas_call | solution.py:1512
  324.1 0.0 copy-start.3
  324.1 0.0 copy-start.4
  324.2 0.0 copy-start.12
  324.2 0.0 copy-start.13
  324.2 0.0 copy-done.18
  324.2 0.0 copy-done.19
  324.2 0.0 copy-done.20
  324.2 1.5 multiply_subtract_fusion.4
  325.7 0.0 copy-done.10
  325.7 0.0 copy-done.16
  325.7 0.0 copy-done.17
  325.7 1.7 multiply_subtract_fusion.3
  327.4 0.0 copy-done.6
  327.4 0.0 copy-done.14
  327.4 0.0 copy-done.15
  327.4 2.0 multiply_subtract_fusion.2
  329.5 0.0 copy-done.3
  329.5 0.0 copy-done.4
  329.5 1.1 multiply_subtract_fusion.1
  330.6 0.0 copy-done.1
  330.6 1.5 multiply_subtract_fusion
  332.1 0.9 copy.48
  333.1 1.0 copy-done.2
  334.0 1.3 copy.49
  335.3 0.7 copy.50
  336.0 0.6 copy.51
  336.6 0.8 copy.52
  337.5 0.7 copy.53
  (20 shorter events, 0.1 us)
Async XLA Ops:
  281.7 42.5 %copy-start.18 = (f32[2,960]{1,0:T(2,128)S(1)}, f32[2,960]{1,0:T(2,128)}, u32[]{:S(2)}) copy-start(f32[2,960]{1,0:T(2,128)} %param.23) | copy-start | bytes 23044
  281.7 42.5 %copy-start.19 = (f32[2,960]{1,0:T(2,128)S(1)}, f32[2,960]{1,0:T(2,128)}, u32[]{:S(2)}) copy-start(f32[2,960]{1,0:T(2,128)} %param.28) | copy-start | bytes 23044
  281.7 42.5 %copy-start.20 = (f32[2,960]{1,0:T(2,128)S(1)}, f32[2,960]{1,0:T(2,128)}, u32[]{:S(2)}) copy-start(f32[2,960]{1,0:T(2,128)} %param.29) | copy-start | bytes 23044
  281.7 44.0 %copy-start.10 = (f32[240,120]{1,0:T(8,128)S(1)}, f32[240,120]{1,0:T(8,128)}, u32[]{:S(2)}) copy-start(f32[240,120]{1,0:T(8,128)} %refs_1_.1) | copy-start | bytes 345604
  281.7 44.0 %copy-start.16 = (f32[240,120]{1,0:T(8,128)S(1)}, f32[240,120]{1,0:T(8,128)}, u32[]{:S(2)}) copy-start(f32[240,120]{1,0:T(8,128)} %param.32) | copy-start | bytes 345604
  281.8 43.9 %copy-start.17 = (f32[240,120]{1,0:T(8,128)S(1)}, f32[240,120]{1,0:T(8,128)}, u32[]{:S(2)}) copy-start(f32[240,120]{1,0:T(8,128)} %param.33) | copy-start | bytes 345604
  281.8 45.6 %copy-start.6 = (f32[240,200]{0,1:T(8,128)S(1)}, f32[240,200]{0,1:T(8,128)}, u32[]{:S(2)}) copy-start(f32[240,200]{0,1:T(8,128)} %param.24) | copy-start | bytes 576004
  281.8 45.6 %copy-start.14 = (f32[240,200]{0,1:T(8,128)S(1)}, f32[240,200]{0,1:T(8,128)}, u32[]{:S(2)}) copy-start(f32[240,200]{0,1:T(8,128)} %param.30) | copy-start | bytes 576004
  281.8 45.6 %copy-start.15 = (f32[240,200]{0,1:T(8,128)S(1)}, f32[240,200]{0,1:T(8,128)}, u32[]{:S(2)}) copy-start(f32[240,200]{0,1:T(8,128)} %param.31) | copy-start | bytes 576004
  324.1 5.3 %copy-start.3 = (f32[640,120]{0,1:T(8,128)S(1)}, f32[640,120]{0,1:T(8,128)}, u32[]{:S(2)}) copy-start(f32[640,120]{0,1:T(8,128)} %param.27) | copy-start | bytes 921604
  324.1 5.3 %copy-start.4 = (f32[120,640]{1,0:T(8,128)S(1)}, f32[120,640]{1,0:T(8,128)}, u32[]{:S(2)}) copy-start(f32[120,640]{1,0:T(8,128)} %get-tuple-element.77) | copy-start | bytes 921604
  324.2 5.3 %copy-start.12 = (f32[640,120]{0,1:T(8,128)S(1)}, f32[640,120]{0,1:T(8,128)}, u32[]{:S(2)}) copy-start(f32[640,120]{0,1:T(8,128)} %param.36) | copy-start | bytes 921604
  324.2 5.3 %copy-start.13 = (f32[640,120]{0,1:T(8,128)S(1)}, f32[640,120]{0,1:T(8,128)}, u32[]{:S(2)}) copy-start(f32[640,120]{0,1:T(8,128)} %param.37) | copy-start | bytes 921604
  327.4 3.2 copy-start
  327.4 3.2 copy-start.1
  327.4 3.2 copy-start.8
  327.4 3.2 copy-start.9
  330.6 1.6 copy-start.5
  332.1 1.9 copy-start.2
  334.0 1.3 copy-start.7
  334.0 2.0 copy-start.11

commit v7 on v6

--- a/solution.py
+++ b/solution.py
@@ -1528,7 +1528,7 @@
     )(hd, heads, x, gain, rg, gain_two, down, output)
 
 
-READY = 3
+READY = 2
 SUMMED = 1
 
 

time: 339 us -> 348 us (1.027)
  Pallas kernels: 317 us -> 326 us
    pallas_call x1, Pallas kernels: 74.1 us -> 79.5 us  [front(): pl.pallas_call(functools.partial(front_kernel, grid, tuple(z_majors), pie...]
    pallas_call x1, Pallas kernels: 72.1 us -> 75.8 us  [middle(): pl.pallas_call(functools.partial(middle_kernel, grid, ready, summed), out...]
where the time goes in v7:
time: 348 us; the launch traced here: 347 us
  Pallas kernels  326 us (94%)
  other arithmetic  12 us (3%)
  local copies, waits for them, and re-layouts  8.52 us (2%)
    pallas_call x1, Pallas kernels, back(): pl.pallas_call(functools.partial(back_kernel, grid, tuple(z_majors), piec...  94.1 us
    pallas_call x1, Pallas kernels, front(): pl.pallas_call(functools.partial(front_kernel, grid, tuple(z_majors), pie...  79.5 us
    pallas_call x1, Pallas kernels, middle(): pl.pallas_call(functools.partial(middle_kernel, grid, ready, summed), out...  75.8 us
    pallas_call x1, Pallas kernels, finish(): pl.pallas_call(functools.partial(finish_kernel, grid, pieces), out_shape=...  40.4 us
    pallas_call x1, Pallas kernels, gather_weights(): pl.pallas_call(functools.partial(gather_kernel, grid, tuple(z_majors), pi...  35.8 us
    unnamed x49, local copies, waits for them, and re-layouts  7.83 us
    sub x5, other arithmetic, adamw(): weight - rate * (first_hat / (jnp.sqrt(second_hat) + adam_epsilon) + deca...  7.8 us

profile of v7, /device:TPU:0, one launch (start us, length us, event | category | flops | bytes accessed | tf_op | source)
XLA Modules:
  0.0 347.1 jit_solution(2472509684309584667)
XLA Ops:
  0.7 0.7 subtract_convert_fusion
  1.4 0.7 constant_dynamic-slice_fusion
  2.1 0.7 select_convert_fusion.1.refs_8_
  2.8 1.0 multiply_sine_fusion
  3.8 1.7 copy.41
  5.5 1.8 select_convert_fusion.refs_9_.refs_7_
  7.3 35.8 %gather_weights.1 = (bf16[4,8,200,240]{3,2,1,0:T(8,128)(2,1)}, bf16[4,120,240]{2,1,0:T(8,128)(2,1)}, bf16[4,120,640]{2,1,0:T(8,128)(2,1)}) custom-call(f32[200,240]{1,0:T(8,128)} %bitcast.35, f32[240,120]{1,0:T(8,128)} %refs_1_.1, f32[120,640]{1,0:T(8,128)} %bitcast.31), custom_call_target="tpu_custom_call" | custom-call | tf_op jit(solution)/shard_map/gather_weights/pallas_call | solution.py:299
  43.0 79.5 %front.1 = (bf16[4,8,120,240]{3,2,1,0:T(8,128)(2,1)}, bf16[4,8,120,640]{3,2,1,0:T(8,128)(2,1)}, bf16[2,8,4,240,128]{4,3,2,1,0:T(8,128)(2,1)}, bf16[15,128,512]{2...) custom-call(bf16[4,120,240]{2,1,0:T(8,128)(2,1)} %get-tuple-element., ...), custom_call_target="tpu_custom_call" | custom-call | tf_op jit(solution)/shard_map/front/pallas_call | solution.py:910
  122.6 75.8 %middle.1 = (bf16[960,512]{1,0:T(8,128)(2,1)}, f32[960,512]{1,0:T(8,128)}, f32[960,1]{1,0:T(8,128)}, bf16[4,960,240]{2,1,0:T(8,128)(2,1)}, bf16[15,128,512]{2,1,...) custom-call(bf16[960,512]{1,0:T(8,128)(2,1)} %get-tuple-element.53.r, ...), custom_call_target="tpu_custom_call" | custom-call | tf_op jit(solution)/shard_map/middle/pallas_call | solution.py:1192
  198.4 94.1 %back.1 = (bf16[4,120,640]{2,1,0:T(8,128)(2,1)}, f32[240,640]{1,0:T(8,128)}, bf16[4,120,240]{2,1,0:T(8,128)(2,1)}, bf16[1600,512]{1,0:T(8,128)(2,1)}) custom-call(bf16[4,2,2,2,120,640]{5,4,3,2,1,0:T(8,128)(2,1)} %bitcast.26, bf16[5,2,2,2,4,240,128]{6,5,4,3,2,1,0:T(8,128)(2,1)} %get-tuple-element.60.refs_1_, bf16[4,2,2,2,120,240]{5,4,3,2,1,0:T(8,128)(2,1)} %bitcast.30, ...), custom_call_target="tpu_custom_call" | custom-call | tf_op jit(solution)/shard_map/back/pallas_call | solution.py:1403
  292.6 0.0 copy-start.18
  292.6 0.0 copy-start.19
  292.6 0.0 copy-start.20
  292.6 0.0 copy-start.10
  292.6 0.0 copy-start.16
  292.6 0.0 copy-start.17
  292.6 0.0 copy-start.6
  292.6 0.0 copy-start.14
  292.7 0.0 copy-start.15
  292.7 40.4 %finish.1 = (f32[960,512]{1,0:T(8,128)}, f32[200,240]{1,0:T(8,128)}, f32[8,960]{1,0:T(8,128)}, f32[120,640]{1,0:T(8,128)}, f32[240,120]{1,0:T(8,128)}) custom-call(bf16[1600,512]{1,0:T(8,128)(2,1)} %get-tuple-element.67.refs_0_, bf16[4,1600,240]{2,1,0:T(8,128)(2,1)} %bitcast.19, bf16[960,512]{1,0:T(8,128)(2,1)} %bitcast.22, f32[960,2]{1,0:T(8,128)} %bitcast.25, ...), custom_call_target="tpu_custom_call" | custom-call | tf_op jit(solution)/shard_map/finish/pallas_call | solution.py:1512
  333.1 0.0 copy-start.3
  333.1 0.0 copy-start.4
  333.1 0.0 copy-start.12
  333.1 0.0 copy-start.13
  333.1 0.0 copy-done.18
  333.2 0.0 copy-done.19
  333.2 0.0 copy-done.20
  333.2 1.5 multiply_subtract_fusion.4
  334.7 0.0 copy-done.10
  334.7 0.0 copy-done.16
  334.7 0.0 copy-done.17
  334.7 1.7 multiply_subtract_fusion.3
  336.4 0.0 copy-done.6
  336.4 0.0 copy-done.14
  336.4 0.0 copy-done.15
  336.4 2.0 multiply_subtract_fusion.2
  338.4 0.0 copy-done.3
  338.4 0.0 copy-done.4
  338.4 0.0 copy-done.12
  338.4 1.1 multiply_subtract_fusion.1
  339.5 1.5 multiply_subtract_fusion
  341.1 0.9 copy.48
  342.0 1.0 copy-done.2
  343.0 1.3 copy.49
  344.3 0.7 copy.50
  344.9 0.6 copy.51
  345.6 0.8 copy.52
  346.4 0.7 copy.53
  (20 shorter events, 0.1 us)
Async XLA Ops:
  292.6 40.6 %copy-start.18 = (f32[2,960]{1,0:T(2,128)S(1)}, f32[2,960]{1,0:T(2,128)}, u32[]{:S(2)}) copy-start(f32[2,960]{1,0:T(2,128)} %param.23) | copy-start | bytes 23044
  292.6 40.6 %copy-start.19 = (f32[2,960]{1,0:T(2,128)S(1)}, f32[2,960]{1,0:T(2,128)}, u32[]{:S(2)}) copy-start(f32[2,960]{1,0:T(2,128)} %param.28) | copy-start | bytes 23044
  292.6 40.6 %copy-start.20 = (f32[2,960]{1,0:T(2,128)S(1)}, f32[2,960]{1,0:T(2,128)}, u32[]{:S(2)}) copy-start(f32[2,960]{1,0:T(2,128)} %param.29) | copy-start | bytes 23044
  292.6 42.1 %copy-start.10 = (f32[240,120]{1,0:T(8,128)S(1)}, f32[240,120]{1,0:T(8,128)}, u32[]{:S(2)}) copy-start(f32[240,120]{1,0:T(8,128)} %refs_1_.1) | copy-start | bytes 345604
  292.6 42.1 %copy-start.16 = (f32[240,120]{1,0:T(8,128)S(1)}, f32[240,120]{1,0:T(8,128)}, u32[]{:S(2)}) copy-start(f32[240,120]{1,0:T(8,128)} %param.32) | copy-start | bytes 345604
  292.6 42.0 %copy-start.17 = (f32[240,120]{1,0:T(8,128)S(1)}, f32[240,120]{1,0:T(8,128)}, u32[]{:S(2)}) copy-start(f32[240,120]{1,0:T(8,128)} %param.33) | copy-start | bytes 345604
  292.6 43.7 %copy-start.6 = (f32[240,200]{0,1:T(8,128)S(1)}, f32[240,200]{0,1:T(8,128)}, u32[]{:S(2)}) copy-start(f32[240,200]{0,1:T(8,128)} %param.24) | copy-start | bytes 576004
  292.6 43.7 %copy-start.14 = (f32[240,200]{0,1:T(8,128)S(1)}, f32[240,200]{0,1:T(8,128)}, u32[]{:S(2)}) copy-start(f32[240,200]{0,1:T(8,128)} %param.30) | copy-start | bytes 576004
  292.7 43.7 %copy-start.15 = (f32[240,200]{0,1:T(8,128)S(1)}, f32[240,200]{0,1:T(8,128)}, u32[]{:S(2)}) copy-start(f32[240,200]{0,1:T(8,128)} %param.31) | copy-start | bytes 576004
  333.1 5.3 %copy-start.3 = (f32[640,120]{0,1:T(8,128)S(1)}, f32[640,120]{0,1:T(8,128)}, u32[]{:S(2)}) copy-start(f32[640,120]{0,1:T(8,128)} %param.27) | copy-start | bytes 921604
  333.1 5.3 %copy-start.4 = (f32[120,640]{1,0:T(8,128)S(1)}, f32[120,640]{1,0:T(8,128)}, u32[]{:S(2)}) copy-start(f32[120,640]{1,0:T(8,128)} %get-tuple-element.77) | copy-start | bytes 921604
  333.1 5.3 %copy-start.12 = (f32[640,120]{0,1:T(8,128)S(1)}, f32[640,120]{0,1:T(8,128)}, u32[]{:S(2)}) copy-start(f32[640,120]{0,1:T(8,128)} %param.36) | copy-start | bytes 921604
  333.1 5.3 %copy-start.13 = (f32[640,120]{0,1:T(8,128)S(1)}, f32[640,120]{0,1:T(8,128)}, u32[]{:S(2)}) copy-start(f32[640,120]{0,1:T(8,128)} %param.37) | copy-start | bytes 921604
  336.4 3.2 copy-start
  336.4 3.2 copy-start.1
  336.4 3.2 copy-start.8
  336.4 3.2 copy-start.9
  339.5 1.6 copy-start.5
  341.1 1.9 copy-start.2
  343.0 1.3 copy-start.7
  343.0 2.0 copy-start.11

commit v8 on v5

--- a/solution.py
+++ b/solution.py
@@ -1321,7 +1321,7 @@
             chain.relay(slot - 1, g)
 
         for k, tick in enumerate(ticks):
-            pl.when(t == k * micros // len(ticks))(tick)
+            pl.when(t == k * (micros - 3) // len(ticks))(tick)
         return carry
 
     lax.fori_loop(0, micros, micro, 0)

time: 337 us -> 340 us (level)
  no operation moved by 1% of the time
where the time goes in v8:
time: 340 us
  Pallas kernels  319 us (94%)
  other arithmetic  12 us (4%)
  local copies, waits for them, and re-layouts  8.52 us (3%)
    pallas_call x1, Pallas kernels, back(): pl.pallas_call(functools.partial(back_kernel, grid, tuple(z_majors), piec...  94.9 us
    pallas_call x1, Pallas kernels, front(): pl.pallas_call(functools.partial(front_kernel, grid, tuple(z_majors), pie...  74.1 us
    pallas_call x1, Pallas kernels, middle(): pl.pallas_call(functools.partial(middle_kernel, grid, ready, summed), out...  73.3 us
    pallas_call x1, Pallas kernels, finish(): pl.pallas_call(functools.partial(finish_kernel, grid, pieces), out_shape=...  40.6 us
    pallas_call x1, Pallas kernels, gather_weights(): pl.pallas_call(functools.partial(gather_kernel, grid, tuple(z_majors), pi...  35.8 us
    unnamed x49, local copies, waits for them, and re-layouts  7.83 us
    sub x5, other arithmetic, adamw(): weight - rate * (first_hat / (jnp.sqrt(second_hat) + adam_epsilon) + deca...  7.79 us

profile of v8, /device:TPU:0, one launch (start us, length us, event | category | flops | bytes accessed | tf_op | source)
XLA Modules:
  0.0 340.1 jit_solution(324373957001766044)
XLA Ops:
  0.7 0.7 subtract_convert_fusion
  1.4 0.7 constant_dynamic-slice_fusion
  2.1 0.7 select_convert_fusion.1.refs_8_
  2.8 1.0 multiply_sine_fusion
  3.8 1.7 copy.41
  5.5 1.8 select_convert_fusion.refs_9_.refs_7_
  7.3 35.8 %gather_weights.1 = (bf16[4,8,200,240]{3,2,1,0:T(8,128)(2,1)}, bf16[4,120,240]{2,1,0:T(8,128)(2,1)}, bf16[4,120,640]{2,1,0:T(8,128)(2,1)}) custom-call(f32[200,240]{1,0:T(8,128)} %bitcast.35, f32[240,120]{1,0:T(8,128)} %refs_1_.1, f32[120,640]{1,0:T(8,128)} %bitcast.31), custom_call_target="tpu_custom_call" | custom-call | tf_op jit(solution)/shard_map/gather_weights/pallas_call | solution.py:299
  43.0 74.1 %front.1 = (bf16[4,8,120,240]{3,2,1,0:T(8,128)(2,1)}, bf16[4,8,120,640]{3,2,1,0:T(8,128)(2,1)}, bf16[3,8,4,240,128]{4,3,2,1,0:T(8,128)(2,1)}, bf16[15,128,512]{2...) custom-call(bf16[4,120,240]{2,1,0:T(8,128)(2,1)} %get-tuple-element.49, ...), custom_call_target="tpu_custom_call" | custom-call | tf_op jit(solution)/shard_map/front/pallas_call | solution.py:893
  117.1 73.3 %middle.1 = (bf16[960,512]{1,0:T(8,128)(2,1)}, f32[960,512]{1,0:T(8,128)}, f32[960,1]{1,0:T(8,128)}, bf16[4,960,240]{2,1,0:T(8,128)(2,1)}, bf16[15,128,512]{2,1,...) custom-call(bf16[960,512]{1,0:T(8,128)(2,1)} %get-tuple-element.52.r, ...), custom_call_target="tpu_custom_call" | custom-call | tf_op jit(solution)/shard_map/middle/pallas_call | solution.py:1175
  190.4 94.9 %back.1 = (bf16[4,120,640]{2,1,0:T(8,128)(2,1)}, f32[240,640]{1,0:T(8,128)}, bf16[4,120,240]{2,1,0:T(8,128)(2,1)}, bf16[1600,512]{1,0:T(8,128)(2,1)}) custom-call(bf16[4,2,2,2,120,640]{5,4,3,2,1,0:T(8,128)(2,1)} %bitcast.26, bf16[5,2,2,2,4,240,128]{6,5,4,3,2,1,0:T(8,128)(2,1)} %get-tuple-element.58.refs_1_, bf16[4,2,2,2,120,240]{5,4,3,2,1,0:T(8,128)(2,1)} %bitcast.30, ...), custom_call_target="tpu_custom_call" | custom-call | tf_op jit(solution)/shard_map/back/pallas_call | solution.py:1386
  285.4 0.0 copy-start.18
  285.4 0.0 copy-start.19
  285.4 0.0 copy-start.20
  285.4 0.0 copy-start.10
  285.4 0.0 copy-start.16
  285.4 0.0 copy-start.17
  285.4 0.0 copy-start.6
  285.5 0.0 copy-start.14
  285.5 0.0 copy-start.15
  285.5 40.6 %finish.1 = (f32[960,512]{1,0:T(8,128)}, f32[200,240]{1,0:T(8,128)}, f32[8,960]{1,0:T(8,128)}, f32[120,640]{1,0:T(8,128)}, f32[240,120]{1,0:T(8,128)}) custom-call(bf16[1600,512]{1,0:T(8,128)(2,1)} %get-tuple-element.65.refs_0_, bf16[4,1600,240]{2,1,0:T(8,128)(2,1)} %bitcast.19, bf16[960,512]{1,0:T(8,128)(2,1)} %bitcast.22, f32[960,2]{1,0:T(8,128)} %bitcast.25, ...), custom_call_target="tpu_custom_call" | custom-call | tf_op jit(solution)/shard_map/finish/pallas_call | solution.py:1495
  326.1 0.0 copy-start.3
  326.1 0.0 copy-start.4
  326.1 0.0 copy-start.12
  326.1 0.0 copy-start.13
  326.1 0.0 copy-done.18
  326.1 0.0 copy-done.19
  326.1 0.0 copy-done.20
  326.1 1.5 multiply_subtract_fusion.4
  327.6 0.0 copy-done.10
  327.6 0.0 copy-done.16
  327.6 0.0 copy-done.17
  327.6 1.7 multiply_subtract_fusion.3
  329.3 0.0 copy-done.6
  329.3 0.0 copy-done.14
  329.4 0.0 copy-done.15
  329.4 2.0 multiply_subtract_fusion.2
  331.4 1.1 multiply_subtract_fusion.1
  332.5 0.0 copy-done.9
  332.5 0.0 copy-start.5
  332.5 1.5 multiply_subtract_fusion
  334.0 0.9 copy.48
  335.0 1.0 copy-done.2
  335.9 1.3 copy.49
  337.2 0.0 copy-done.7
  337.2 0.7 copy.50
  337.9 0.6 copy.51
  338.5 0.8 copy.52
  339.4 0.7 copy.53
  (20 shorter events, 0.1 us)
Async XLA Ops:
  285.4 40.7 %copy-start.18 = (f32[2,960]{1,0:T(2,128)S(1)}, f32[2,960]{1,0:T(2,128)}, u32[]{:S(2)}) copy-start(f32[2,960]{1,0:T(2,128)} %param.23) | copy-start | bytes 23044
  285.4 40.7 %copy-start.19 = (f32[2,960]{1,0:T(2,128)S(1)}, f32[2,960]{1,0:T(2,128)}, u32[]{:S(2)}) copy-start(f32[2,960]{1,0:T(2,128)} %param.28) | copy-start | bytes 23044
  285.4 40.7 %copy-start.20 = (f32[2,960]{1,0:T(2,128)S(1)}, f32[2,960]{1,0:T(2,128)}, u32[]{:S(2)}) copy-start(f32[2,960]{1,0:T(2,128)} %param.29) | copy-start | bytes 23044
  285.4 42.2 %copy-start.10 = (f32[240,120]{1,0:T(8,128)S(1)}, f32[240,120]{1,0:T(8,128)}, u32[]{:S(2)}) copy-start(f32[240,120]{1,0:T(8,128)} %refs_1_.1) | copy-start | bytes 345604
  285.4 42.2 %copy-start.16 = (f32[240,120]{1,0:T(8,128)S(1)}, f32[240,120]{1,0:T(8,128)}, u32[]{:S(2)}) copy-start(f32[240,120]{1,0:T(8,128)} %param.32) | copy-start | bytes 345604
  285.4 42.2 %copy-start.17 = (f32[240,120]{1,0:T(8,128)S(1)}, f32[240,120]{1,0:T(8,128)}, u32[]{:S(2)}) copy-start(f32[240,120]{1,0:T(8,128)} %param.33) | copy-start | bytes 345604
  285.4 43.9 %copy-start.6 = (f32[240,200]{0,1:T(8,128)S(1)}, f32[240,200]{0,1:T(8,128)}, u32[]{:S(2)}) copy-start(f32[240,200]{0,1:T(8,128)} %param.24) | copy-start | bytes 576004
  285.5 43.9 %copy-start.14 = (f32[240,200]{0,1:T(8,128)S(1)}, f32[240,200]{0,1:T(8,128)}, u32[]{:S(2)}) copy-start(f32[240,200]{0,1:T(8,128)} %param.30) | copy-start | bytes 576004
  285.5 43.9 %copy-start.15 = (f32[240,200]{0,1:T(8,128)S(1)}, f32[240,200]{0,1:T(8,128)}, u32[]{:S(2)}) copy-start(f32[240,200]{0,1:T(8,128)} %param.31) | copy-start | bytes 576004
  326.1 5.3 %copy-start.3 = (f32[640,120]{0,1:T(8,128)S(1)}, f32[640,120]{0,1:T(8,128)}, u32[]{:S(2)}) copy-start(f32[640,120]{0,1:T(8,128)} %param.27) | copy-start | bytes 921604
  326.1 5.3 %copy-start.4 = (f32[120,640]{1,0:T(8,128)S(1)}, f32[120,640]{1,0:T(8,128)}, u32[]{:S(2)}) copy-start(f32[120,640]{1,0:T(8,128)} %get-tuple-element.75) | copy-start | bytes 921604
  326.1 5.3 %copy-start.12 = (f32[640,120]{0,1:T(8,128)S(1)}, f32[640,120]{0,1:T(8,128)}, u32[]{:S(2)}) copy-start(f32[640,120]{0,1:T(8,128)} %param.36) | copy-start | bytes 921604
  326.1 5.3 %copy-start.13 = (f32[640,120]{0,1:T(8,128)S(1)}, f32[640,120]{0,1:T(8,128)}, u32[]{:S(2)}) copy-start(f32[640,120]{0,1:T(8,128)} %param.37) | copy-start | bytes 921604
  329.3 3.1 copy-start
  329.3 3.1 copy-start.1
  329.3 3.1 copy-start.8
  329.3 3.2 copy-start.9
  332.5 1.5 copy-start.5
  334.0 1.9 copy-start.2
  335.9 1.3 copy-start.7
  335.9 2.0 copy-start.11
